TPU v7x, 32 devices: a whole 2x2x4 slice. The times are simulated.
32 devices in a mesh: fsdp: 4 (over y, x), dp: 8 (over z, core).
Axes of the slice: x: 2, y: 2, z: 4, core: 2. Of those that a mesh axis runs over, the one named last changes fastest.
Arguments:
- hidden_in: bfloat16 [8192, 1536], P(('fsdp', 'dp')), may hold values from -6 to 6
- lengths: int32 [32, 4], P(('fsdp', 'dp')), may hold values from 0 to 256, as said below
- norm_gain: bfloat16 [1536], P(('fsdp', 'dp')), may hold values from 0.5 to 1.5
- in_proj: bfloat16 [1536, 6448], P(('fsdp', 'dp')), may hold values from -0.15625 to 0.15625
- conv_weight: bfloat16 [3328, 4], P(('fsdp', 'dp')), may hold values from -3 to 3
- conv_bias: bfloat16 [3328], P(('fsdp', 'dp')), may hold values from -3 to 3
- gate_gain: bfloat16 [3072], P(('fsdp', 'dp')), may hold values from 0.5 to 1.5
- out_proj: bfloat16 [3072, 1536], P(('fsdp', 'dp')), may hold values from -0.109375 to 0.109375
- decay_log: float32 [48], replicated, may hold values from -3 to 1.5
- step_bias: float32 [48], replicated, may hold values from -5 to -2
- skip_gain: float32 [48], replicated, may hold values from 0.5 to 1.5
- grad_out: bfloat16 [8192, 1536], P(('fsdp', 'dp')), may hold values from -6 to 6
Outputs:
- hidden_out: bfloat16 [8192, 1536], P(('fsdp', 'dp'))
- grad_in: float32 [8192, 1536], P(('fsdp', 'dp'))
- grad_norm_gain: float32 [1536], P(('fsdp', 'dp'))
- grad_in_proj: float32 [1536, 6448], P(('fsdp', 'dp'))
- grad_conv_weight: float32 [3328, 4], P(('fsdp', 'dp'))
- grad_conv_bias: float32 [3328], P(('fsdp', 'dp'))
- grad_gate_gain: float32 [3072], P(('fsdp', 'dp'))
- grad_out_proj: float32 [3072, 1536], P(('fsdp', 'dp'))
- grad_decay_log: float32 [48], replicated
- grad_step_bias: float32 [48], replicated
- grad_skip_gain: float32 [48], replicated
Inputs may be any that keep to these rules, and one draw needn't show every extreme that they name: lengths[b] lists the sequences packed from the first row of block b on, in order; a length may be 0 (an empty slot); each block's lengths sum to at most 256 and the rows after that sum are padding; in every draw one block holds a single sequence of exactly 256 rows.
All inputs are finite; a program needn't handle non-finite values.
Results may differ from a plain program's by a relative error of at most 0.0063.
Values may be sent and summed in bfloat16 or wider, within the bound.
A program may use at most 192 MiB of HBM per device.

v0:
```python
import jax
import jax.numpy as jnp
from jax import lax
from jax.sharding import PartitionSpec as P

SPAN = 256


EPS = 1e-05
full_precision = lax.Precision.HIGHEST


def segment_ids(lens_row, row_count):
    ends = jnp.cumsum(lens_row)
    places = jnp.arange(row_count, dtype=jnp.int32)
    seg_ids = jnp.sum((places[:, None] >= ends[None, :]).astype(jnp.int32), axis=1)
    valid = (seg_ids < lens_row.shape[0]).astype(jnp.float32)
    return (seg_ids, valid)


def pre_norm(values, weight):
    return (
        values * lax.rsqrt(jnp.mean(values * values, axis=1, keepdims=True) + EPS) * weight[None, :]
    )


def convolve(inputs, weight, bias_row, seg_ids):
    kernel_len = weight.shape[1]
    summed = bias_row[None, :] + inputs * weight[:, kernel_len - 1][None, :]
    for offset in range(1, kernel_len):
        shifted = jnp.pad(inputs, ((offset, 0), (0, 0)))[:-offset]
        earlier = jnp.pad(seg_ids, (offset, 0), constant_values=-1)[:-offset]
        keep_mask = (earlier == seg_ids).astype(jnp.float32)
        summed = summed + shifted * keep_mask[:, None] * weight[:, kernel_len - 1 - offset][None, :]
    return summed


def state_scan(x_act, steps_dt, decay_rate, b_mat, c_mat, skips, seg_ids):
    row_count = x_act.shape[0]
    head_count = steps_dt.shape[1]
    head_dim = x_act.shape[1] // head_count
    state_dim = b_mat.shape[1]
    blocks = row_count // SPAN
    x_blocks = x_act.reshape(blocks, SPAN, head_count, head_dim)
    dt_blocks = steps_dt.reshape(blocks, SPAN, head_count)
    b_blocks = b_mat.reshape(blocks, SPAN, state_dim)
    c_blocks = c_mat.reshape(blocks, SPAN, state_dim)
    seg_blocks = seg_ids.reshape(blocks, SPAN)
    lower_tri = jnp.arange(SPAN)[:, None] >= jnp.arange(SPAN)[None, :]

    def block_step(scan_carry, block_in):
        old_state, prev_seg = scan_carry
        x_blk, dt_blk, b_blk, c_blk, seg_blk = block_in
        log_decay = jnp.cumsum(dt_blk * decay_rate[None, :], axis=0)
        same_seq = (seg_blk[:, None] == seg_blk[None, :]) & lower_tri
        spread = log_decay.T[:, :, None] - log_decay.T[:, None, :]
        decays = jnp.exp(jnp.where(same_seq[None], spread, -jnp.inf))
        inner_cb = jnp.dot(c_blk, b_blk.T, precision=full_precision)
        mixing = decays * inner_cb[None] * dt_blk.T[:, None, :]
        result = jnp.einsum("hts,shp->thp", mixing, x_blk, precision=full_precision)
        enters = (seg_blk == prev_seg).astype(jnp.float32)
        carried = jnp.einsum("tn,hpn->thp", c_blk, old_state, precision=full_precision)
        result = result + jnp.exp(log_decay)[:, :, None] * enters[:, None, None] * carried
        result = result + skips[None, :, None] * x_blk
        last_seg = seg_blk[-1]
        tail_wts = (
            jnp.exp(log_decay[-1][None, :] - log_decay)
            * (seg_blk == last_seg).astype(jnp.float32)[:, None]
            * dt_blk
        )
        new_state = jnp.einsum("sh,shp,sn->hpn", tail_wts, x_blk, b_blk, precision=full_precision)
        keep_old = jnp.exp(log_decay[-1]) * (prev_seg == last_seg).astype(jnp.float32)
        new_state = new_state + keep_old[:, None, None] * old_state
        return ((new_state, last_seg), result)

    start_state = (
        jnp.zeros((head_count, head_dim, state_dim), jnp.float32),
        jnp.array(-1, jnp.int32),
    )
    _, outputs = lax.scan(
        jax.checkpoint(block_step),
        start_state,
        (x_blocks, dt_blocks, b_blocks, c_blocks, seg_blocks),
    )
    return outputs.reshape(row_count, head_count * head_dim)


def mixer_branch(projected, kernel, shift_bias, gate, rates, biases, skips, seg_ids, valid):
    inner_dim = gate.shape[0]
    conv_dim = shift_bias.shape[0]
    state_dim = (conv_dim - inner_dim) // 2
    gate_in = projected[:, :inner_dim]
    conv_in = projected[:, inner_dim : inner_dim + conv_dim]
    dt_raw = projected[:, inner_dim + conv_dim :]
    activ = jax.nn.silu(convolve(conv_in, kernel, shift_bias, seg_ids))
    x_act = activ[:, :inner_dim]
    b_mat = activ[:, inner_dim : inner_dim + state_dim]
    c_mat = activ[:, inner_dim + state_dim :]
    steps_dt = jax.nn.softplus(dt_raw + biases[None, :])
    decay_rate = -jnp.exp(rates)
    scanned = state_scan(x_act, steps_dt, decay_rate, b_mat, c_mat, skips, seg_ids)
    gated = scanned * jax.nn.silu(gate_in)
    scale = lax.rsqrt(jnp.mean(gated * gated, axis=1, keepdims=True) + EPS)
    return gated * scale * gate[None, :] * valid[:, None]


def right_product(left, right):
    return lax.dot_general(
        left, right, (((1,), (1,)), ((), ())), preferred_element_type=jnp.float32
    )


def left_product(left, right):
    return lax.dot_general(
        left, right, (((0,), (0,)), ((), ())), preferred_element_type=jnp.float32
    )


def local(
    hidden_in,
    lengths,
    norm_gain,
    in_proj,
    conv_weight,
    conv_bias,
    gate_gain,
    out_proj,
    decay_log,
    step_bias,
    skip_gain,
    grad_out,
):
    row_count = hidden_in.shape[0]
    gain_all, kernel_all, shift_all, gate_all, out_all = (
        lax.all_gather(norm_gain, ("fsdp", "dp"), axis=0, tiled=True),
        lax.all_gather(conv_weight, ("fsdp", "dp"), axis=0, tiled=True),
        lax.all_gather(conv_bias, ("fsdp", "dp"), axis=0, tiled=True),
        lax.all_gather(gate_gain, ("fsdp", "dp"), axis=0, tiled=True),
        lax.all_gather(out_proj, ("fsdp", "dp"), axis=0, tiled=True),
    )
    seg_ids, valid = segment_ids(lengths[0], row_count)
    x_float = hidden_in.astype(jnp.float32)
    normed32, norm_back = jax.vjp(pre_norm, x_float, gain_all.astype(jnp.float32))
    normed = normed32.astype(jnp.bfloat16)
    columns = normed
    projected = jnp.dot(
        columns,
        lax.all_gather(in_proj, ("fsdp", "dp"), axis=0, tiled=True),
        preferred_element_type=jnp.float32,
    )

    def branch(proj_in, kernel, shift_bias, gate, rates, biases, skips):
        return mixer_branch(proj_in, kernel, shift_bias, gate, rates, biases, skips, seg_ids, valid)

    mixed32, branch_back = jax.vjp(
        branch,
        projected,
        kernel_all.astype(jnp.float32),
        shift_all.astype(jnp.float32),
        gate_all.astype(jnp.float32),
        decay_log,
        step_bias,
        skip_gain,
    )
    mixed = mixed32.astype(jnp.bfloat16)
    hidden_out = (x_float + jnp.dot(mixed, out_all, preferred_element_type=jnp.float32)).astype(
        jnp.bfloat16
    )
    columns = mixed
    grad_out_proj = lax.psum_scatter(
        left_product(columns, grad_out), ("fsdp", "dp"), scatter_dimension=0, tiled=True
    )
    grad_mixed = right_product(
        grad_out, lax.all_gather(out_proj, ("fsdp", "dp"), axis=0, tiled=True)
    )
    grad_proj, grad_kernel, grad_shift, grad_gate, grad_rates, grad_biases, grad_skips = (
        branch_back(grad_mixed)
    )
    proj_low = grad_proj.astype(jnp.bfloat16)
    columns = normed
    grad_in_proj = lax.psum_scatter(
        left_product(columns, proj_low), ("fsdp", "dp"), scatter_dimension=0, tiled=True
    )
    grad_normed = right_product(
        proj_low, lax.all_gather(in_proj, ("fsdp", "dp"), axis=0, tiled=True)
    )
    grad_x, grad_gain = norm_back(grad_normed)
    grad_in = grad_out.astype(jnp.float32) + grad_x
    small_sums = (
        lax.psum_scatter(grad_gain, ("fsdp", "dp"), scatter_dimension=0, tiled=True),
        lax.psum_scatter(grad_kernel, ("fsdp", "dp"), scatter_dimension=0, tiled=True),
        lax.psum_scatter(grad_shift, ("fsdp", "dp"), scatter_dimension=0, tiled=True),
        lax.psum_scatter(grad_gate, ("fsdp", "dp"), scatter_dimension=0, tiled=True),
    )
    head_sums = lax.psum((grad_rates, grad_biases, grad_skips), ("fsdp", "dp"))
    return (
        hidden_out,
        grad_in,
        small_sums[0],
        grad_in_proj,
        small_sums[1],
        small_sums[2],
        small_sums[3],
        grad_out_proj,
        head_sums[0],
        head_sums[1],
        head_sums[2],
    )


def solution(mesh):
    in_specs = (
        P(("fsdp", "dp"), None),
        P(("fsdp", "dp"), None),
        P(("fsdp", "dp")),
        P(("fsdp", "dp"), None),
        P(("fsdp", "dp"), None),
        P(("fsdp", "dp")),
        P(("fsdp", "dp")),
        P(("fsdp", "dp"), None),
        P(),
        P(),
        P(),
        P(("fsdp", "dp"), None),
    )
    out_specs = (
        P(("fsdp", "dp"), None),
        P(("fsdp", "dp"), None),
        P(("fsdp", "dp")),
        P(("fsdp", "dp"), None),
        P(("fsdp", "dp"), None),
        P(("fsdp", "dp")),
        P(("fsdp", "dp")),
        P(("fsdp", "dp"), None),
        P(),
        P(),
        P(),
    )
    return jax.shard_map(local, mesh=mesh, in_specs=in_specs, out_specs=out_specs, check_vma=False)
```

profile of v0, /device:TPU:0, one launch (start us, length us, event | category | flops | bytes accessed | tf_op | source)
XLA Modules:
  0.0 1067.1 jit_solution(12854662397712302054)
XLA Ops:
  8.7 0.9 dynamic-update-slice.1
  9.6 0.8 dynamic-update-slice.2
  10.4 0.8 dynamic-update-slice
  11.3 44.1 %all-reduce.29 = (bf16[1536]{0:T(1024)(128)(2,1)S(1)}, bf16[3328]{0:T(1024)(128)(2,1)S(1)}, bf16[3072]{0:T(1024)(128)(2,1)S(1)}) all-reduce(bf16[1536]{0:T(1024)(128)(2,1)S(1)} %dynamic-update-slice.1, bf16[3328]{0:T(1024)(128)(2,1)S(1)} %dynamic-update-slice, ...), channel_id=1, replica_groups=mesh['fsdp'=4,'dp'=8] {'fsdp','dp'}, use_global_device_ids=true, to_apply=%add.22 | all-reduce | flops 7936 | bytes 31744
  56.6 41.5 %all-gather = bf16[32,104,4]{1,2,0:T(4,128)(2,1)S(1)} all-gather(bf16[1,104,4]{1,2,0:T(4,128)(2,1)} %bitcast.141), channel_id=1, replica_groups=mesh['fsdp'=4,'dp'=8] {'fsdp','dp'}, dimensions={0}, use_global_device_ids=true | all-gather | bytes 27456 | tf_op jit(solution)/shard_map/all_gather | solution.py:136
  98.2 0.8 reduce-window.29
  99.8 0.7 slice_reduce_fusion.6
  100.5 1.4 fusion.56
  101.9 1.2 exponential_negate_fusion
  104.4 40.5 %all-gather.4.cloned.1.call-done = bf16[1536,6448]{1,0:T(8,128)(2,1)} async-done(((bf16[48,6448]{1,0:T(8,128)(2,1)}), bf16[1536,6448]{1,0:T(8,128)(2,1)}) %all-gather.4.cloned.1.call-update) | async-done | bytes 19808272 | tf_op jit(solution)/shard_map/all_gather | solution.py:148
  144.9 10.4 fusion.72
  155.6 2.5 copy-done.10
  158.1 0.9 broadcast_multiply_fusion.1
  159.0 1.8 copy.140
  160.8 1.9 reduce-window.30
  162.7 1.5 slice_reduce_fusion.2
  164.2 1.3 reduce-window.31
  165.5 1.2 slice.97
  167.4 4.8 fusion.32
  172.3 1.7 copy-done.11
  174.0 2.0 slice.112
  176.0 2.4 copy.138
  178.6 1.7 fusion.89
  180.3 3.5 fusion.67
  183.9 15.5 %fusion.38 = f32[256,48,64]{0,2,1:T(8,128)} fusion(f32[256,48,64]{0,2,1:T(8,128)S(1)} %bitcast.127, f32[256,48,64]{0,2,1:T(8,128)S(1)} %fusion.67, f32[48,256]{1,0:T(8,128)S(1)} %copy-done.30, f32[256,256]{1,0:T(8,128)S(1)} %fusion.89, f32[48,256]{1,0:T(8,128)S(1)} %copy_bitcast_fusion, pred[256,256]{1,0:T(8,128)(4,1)S(1)} %copy-done.23, ...), kind=kOutput, calls=%fused_computation.63 | convolution fusion | flops 2431647744 | bytes 9912512 | tf_op jit(solution)/shard_map/jvp()/while/body/eval_jaxpr/hts,shp->thp/dot_general | solution.py:60
  199.4 4.1 copy.144
  203.4 3.9 multiply_reduce_fusion.11
  207.8 0.9 fusion.84
  208.8 1.0 fusion.100
  209.8 18.0 %all-gather.6.cloned.1.call-done = bf16[3072,1536]{1,0:T(8,128)(2,1)} async-done(((bf16[96,1536]{1,0:T(8,128)(2,1)}), bf16[3072,1536]{1,0:T(8,128)(2,1)}) %all-gather.6.cloned.1.call-update) | async-done | bytes 9437200 | tf_op jit(solution)/shard_map/all_gather | solution.py:139
  227.8 6.6 multiply_reduce_fusion.8
  234.4 5.1 fusion.60
  239.5 3.5 copy.145
  245.8 1.2 copy-done
  247.1 2.7 multiply_reduce_fusion.9
  251.5 6.8 multiply_reduce_fusion.7
  258.3 18.8 %fusion.11 = (f32[48,256]{1,0:T(8,128)S(1)}, f32[48,256]{1,0:T(8,128)S(1)}, f32[48,256]{1,0:T(8,128)S(1)}, f32[256,256]{1,0:T(8,128)S(1)}) fusion(f32[48,256]{1,0:T(8,128)S(1)} %copy.152, f32[256,256]{1,0:T(8,128)S(1)} %fusion.101, f32[48,256]{1,0:T(8,128)S(1)} %copy.148, pred[256,256]{1,0:T(8,128)(4,1)S(1)} %compare_and_fusion, ...), kind=kOutput, calls=%fused_computation.14 | convolution fusion | flops 2456711168 | bytes 7127040 | tf_op jit(solution)/shard_map/transpose(jvp())/while/body/eval_jaxpr/checkpoint/hts,shp->thp/dot_general | solution.py:60
  277.4 0.8 copy.150
  278.6 2.5 reduce-window.43
  282.1 7.1 fusion.64
  289.2 13.4 %bitcast_add_fusion = f32[256,48,64]{0,2,1:T(8,128)} fusion(f32[256,48,64]{0,2,1:T(8,128)S(1)} %bitcast.126, f32[256,48,64]{0,2,1:T(8,128)} %get-tuple-element.199, f32[48,256]{1,0:T(8,128)S(1)} %copy.152, f32[256,256]{1,0:T(8,128)S(1)} %fusion.101, f32[48,256]{1,0:T(8,128)S(1)} %copy-done.29, pred[256,256]{1,0:T(8,128)(4,1)S(1)} %compare_and_fusion, ...), kind=kOutput, calls=%fused_computation.58 | convolution fusion | flops 2431647744 | bytes 9912512 | tf_op jit(solution)/shard_map/transpose(jvp())/while/body/eval_jaxpr/checkpoint/hts,shp->thp/dot_general | solution.py:60
  302.6 3.8 copy.159
  306.5 7.1 fusion.61
  314.6 7.1 fusion.95
  324.1 1.6 copy.156
  325.7 2.5 fusion.96
  328.1 1.2 negate_multiply_fusion
  329.3 1.9 multiply_multiply_fusion
  331.2 2.9 fusion.29
  334.8 13.6 %fusion.54 = (f32[1536]{0:T(1024)}, f32[256]{0:T(256)S(1)}, f32[256,1536]{1,0:T(8,128)}) fusion(bf16[256,1536]{1,0:T(8,128)(2,1)} %param.12, f32[256]{0:T(256)S(1)} %fusion.83, f32[1536]{0:T(1024)S(1)} %convert_element_type.81, bf16[1536,6448]{1,0:T(8,128)(2,1)} %all-gather.4.cloned.1.call-done, f32[256,3072]{1,0:T(8,128)} %get-tuple-element.179, ...), kind=kOutput, calls=%fused_computation.87 | convolution fusion | flops 5078616064 | bytes 28784640 | tf_op jit(solution)/shard_map/dot_general | solution.py:108
  348.5 9.1 fusion.94
  357.7 18.9 %fusion.70 = f32[1536,6448]{1,0:T(8,128)} fusion(bf16[256,1536]{1,0:T(8,128)(2,1)} %param.12, f32[1536]{0:T(1024)S(1)} %convert_element_type.81, f32[256]{0:T(256)S(1)} %fusion.83, f32[256,3072]{1,0:T(8,128)} %get-tuple-element.179, f32[256,3328]{1,0:T(8,128)} %fusion.29, f32[256,48]{1,0:T(8,128)S(1)} %copy-done.18), kind=kOutput, calls=%fused_computation.108 | convolution fusion | flops 5077438464 | bytes 47012864 | tf_op jit(solution)/shard_map/dot_general | solution.py:114
  377.3 3.5 fusion.55
  380.8 7.2 fusion.44
  388.0 84.8 %all-reduce.32.cloned.1.call-done = (f32[1536]{0:T(1024)}, f32[3328,4]{0,1:T(4,128)}, f32[3328]{0:T(1024)}, f32[3072]{0:T(1024)}, f32[48]{0:T(128)}, /*index=5*/f32[48]{0:T(128)}, f32[48]{0:T(128)}) async-done(((f32[1536]{0:T(1024)}, f32[3328,4]{0,1:T(4,128)}, f32[3328]{0:T(1024)}, f32[3072]{0:T(1024)}, f32[48]{0:T(128)}, /*index=5*/f32[48]{0:T(128)}, f32[48]{0:T(128)}), (f32[1536]{0:T(1024)}, ...) | async-done | bytes 85584
  472.8 1.3 dynamic-slice.11
  474.0 1.3 dynamic-slice.8
  475.3 1.3 dynamic-slice.10
  476.6 1.3 constant_dynamic-slice_fusion
  477.9 209.4 %reduce-scatter.6.cloned.1.call-done = f32[96,1536]{1,0:T(8,128)} async-done(((f32[3072,1536]{1,0:T(8,128)}), f32[96,1536]{1,0:T(8,128)}) %reduce-scatter.6.cloned.1.call-update) | async-done | bytes 589840 | tf_op jit(solution)/shard_map/reduce_scatter | solution.py:170
  687.3 369.6 %reduce-scatter.4.cloned.1.call-done = f32[48,6448]{1,0:T(8,128)} async-done(((f32[1536,6448]{1,0:T(8,128)}), f32[48,6448]{1,0:T(8,128)}) %reduce-scatter.4.cloned.1.call-update) | async-done | bytes 1238032 | tf_op jit(solution)/shard_map/reduce_scatter | solution.py:181
  1056.9 1.1 copy.184
  1058.0 1.1 copy.185
  1059.1 1.2 copy.186
  (159 shorter events, 16.9 us)
Async XLA Ops:
  7.2 137.7 %all-gather.4.cloned.1.call-start = ((), (), s32[]{:S(2)}) async-start(), calls=%async_computation.2 | async-start | bytes 20680704 | tf_op jit(solution)/shard_map/all_gather | solution.py:148
  7.9 219.8 %all-gather.6.cloned.1.call-start = ((), (), s32[]{:S(2)}) async-start(), calls=%async_computation.3 | async-start | bytes 9732096 | tf_op jit(solution)/shard_map/all_gather | solution.py:139
  8.7 464.1 %all-reduce.32.cloned.1.call-start = ((), (), s32[]{:S(2)}) async-start(), calls=%async_computation.6 | async-start | bytes 183296
  101.9 1.2 copy-start.37
  155.3 2.8 copy-start.10
  155.3 2.8 copy-start.42
  155.3 2.8 copy-start.45
  158.1 14.1 %copy-start.3 = (f32[256,3328]{1,0:T(8,128)}, f32[256,3328]{1,0:T(8,128)S(1)}, u32[]{:S(2)}) copy-start(f32[256,3328]{1,0:T(8,128)S(1)} %slice.107) | copy-start | bytes 10223620
  172.3 1.7 copy-start.11
  176.0 2.4 copy-start.17
  176.0 2.4 copy-start.35
  176.0 2.5 copy-start.44
  178.4 21.0 %copy-start.8 = (f32[256,3072]{0,1:T(8,128)}, f32[256,3072]{0,1:T(8,128)S(1)}, u32[]{:S(2)}) copy-start(f32[256,3072]{0,1:T(8,128)S(1)} %copy.138) | copy-start | bytes 9437188
  178.4 5.5 copy-start.23
  178.4 5.5 copy-start.30
  178.4 5.5 copy-start.46
  207.3 0.6 copy-start.39
  207.3 27.1 %copy-start.5 = (f32[256,3072]{1,0:T(8,128)}, f32[256,3072]{1,0:T(8,128)S(1)}, u32[]{:S(2)}) copy-start(f32[256,3072]{1,0:T(8,128)S(1)} %get-tuple-element.173) | copy-start | bytes 9437188
  209.8 41.3 %copy-start.15 = (f32[256,128]{1,0:T(8,128)}, f32[256,128]{1,0:T(8,128)S(1)}, u32[]{:S(2)}) copy-start(f32[256,128]{1,0:T(8,128)S(1)} %get-tuple-element.113) | copy-start | bytes 393220
  227.7 6.6 copy-start.40
  227.7 6.6 copy-start.7
  227.7 6.6 copy-start.20
  227.8 6.7 copy-start.31
  239.5 5.4 copy-start.19
  244.9 33.4 %copy-start.34 = (f32[256]{0:T(256)}, f32[256]{0:T(256)S(1)}, u32[]{:S(2)}) copy-start(f32[256]{0:T(256)S(1)} %get-tuple-element.192) | copy-start | bytes 3076
  245.2 1.9 copy-start
  245.4 4.5 copy-start.43
  251.0 27.4 %copy-start.13 = (f32[48,2,128]{0,2,1:T(8,128)}, f32[48,2,128]{0,2,1:T(8,128)S(1)}, u32[]{:S(2)}) copy-start(f32[48,2,128]{0,2,1:T(8,128)S(1)} %copy.147) | copy-start | bytes 147460
  251.1 7.2 copy-start.28
  251.5 6.8 copy-start.1
  251.5 6.8 copy-start.9
  278.2 11.0 %copy-start.14 = (f32[256,48]{1,0:T(8,128)}, f32[256,48]{1,0:T(8,128)S(1)}, u32[]{:S(2)}) copy-start(f32[256,48]{1,0:T(8,128)S(1)} %copy.166) | copy-start | bytes 147460
  278.3 10.9 %copy-start.41 = (f32[48]{0:T(128)}, f32[48]{0:T(128)S(1)}, u32[]{:S(2)}) copy-start(f32[48]{0:T(128)S(1)} %get-tuple-element.190) | copy-start | bytes 580
  278.5 10.7 copy-start.29
  278.6 10.7 copy-start.47
  282.1 7.1 copy-start.2
  306.4 7.2 copy-start.16
  306.4 8.2 copy-start.33
  306.5 8.1 copy-start.4
  329.3 1.9 copy-start.22
  331.2 2.9 copy-start.24
  331.2 2.9 copy-start.25
  331.2 2.9 copy-start.26
  331.2 2.9 copy-start.27
  331.2 3.6 copy-start.18
  334.8 13.7 %copy-start.6 = (f32[256,3072]{1,0:T(8,128)S(1)}, f32[256,3072]{1,0:T(8,128)}, u32[]{:S(2)}) copy-start(f32[256,3072]{1,0:T(8,128)} %copy-done.5) | copy-start | bytes 9437188
  334.8 13.7 %copy-start.21 = (f32[3072]{0:T(1024)S(1)}, f32[3072]{0:T(1024)}, u32[]{:S(2)}) copy-start(f32[3072]{0:T(1024)} %convert_element_type.89) | copy-start | bytes 36868
  334.8 13.7 %copy-start.32 = (f32[256]{0:T(256)S(1)}, f32[256]{0:T(256)}, u32[]{:S(2)}) copy-start(f32[256]{0:T(256)} %fusion.84) | copy-start | bytes 3076
  334.8 13.7 %copy-start.36 = (f32[256]{0:T(256)S(1)}, f32[256]{0:T(256)}, u32[]{:S(2)}) copy-start(f32[256]{0:T(256)} %get-tuple-element.193) | copy-start | bytes 3076
  348.4 338.9 %reduce-scatter.6.cloned.1.call-start = ((), (), s32[]{:S(2)}) async-start(), calls=%async_computation.5 | async-start | bytes 19464192 | tf_op jit(solution)/shard_map/reduce_scatter | solution.py:170
  357.7 699.2 %reduce-scatter.4.cloned.1.call-start = ((), (), s32[]{:S(2)}) async-start(), calls=%async_computation.4 | async-start | bytes 41361408 | tf_op jit(solution)/shard_map/reduce_scatter | solution.py:181
  376.6 0.6 copy-start.38
  376.7 4.1 copy-start.12
Sparse Core Ops, SparseCore 0:
  11.0 133.8 all-gather.3
  147.9 79.7 all-gather.5
  348.5 124.1 all-reduce.31
  479.6 207.6 reduce-scatter.5
  694.2 362.6 reduce-scatter.3
where the time goes:
time: 1070 us
  waiting for transfers between devices  724 us (68%)
  matrix products  144 us (13%)
  blocking collectives  85.6 us (8%)
  other arithmetic  50.8 us (5%)
  local copies, waits for them, and re-layouts  47.6 us (4%)
  between operations  15.5 us (1%)
    reduce_scatter x1, waiting for transfers between devices, local(): lax.psum_scatter(left_product(columns, proj_low), ('fsdp', 'dp'), scatter...  370 us
    reduce_scatter x1, waiting for transfers between devices, local(): lax.psum_scatter(left_product(columns, grad_out), ('fsdp', 'dp'), scatter...  209 us
    unnamed x6, waiting for transfers between devices  86.2 us
    dot_general x3, matrix products, block_step(): result = jnp.einsum('hts,shp->thp', mixing, x_blk, precision=full_precision)  47.7 us
    unnamed x1, blocking collectives  44.1 us
    all_gather x1, blocking collectives, local(): lax.all_gather(conv_weight, ('fsdp', 'dp'), axis=0, tiled=True)  41.5 us
    all_gather x1, waiting for transfers between devices, local(): lax.all_gather(in_proj, ('fsdp', 'dp'), axis=0, tiled=True)  40.5 us
    dot_general x2, matrix products, left_product(): lax.dot_general(left, right, (((0,), (0,)), ((), ())), preferred_element_...  28.1 us
  transfers between devices with their start and end apart: 5, of which 5 were waited for; matrix products, arithmetic and copies ran while one was open for 11% of the time, Pallas kernels for 0%

commit v1 on v0

v1 whole, which is shorter than its diff:
```python
import functools
import math

import jax
import jax.numpy as jnp
from jax import lax
from jax.experimental import pallas as pl
from jax.experimental.pallas import tpu as pltpu
from jax.sharding import PartitionSpec as P

EPS = 1e-05
F32 = jnp.float32
BF16 = jnp.bfloat16
EXACT = lax.Precision.HIGHEST
LANES = 128


def nn(a, b):
    return lax.dot_general(a, b, (((1,), (0,)), ((), ())), preferred_element_type=F32)


def nt(a, b):
    return lax.dot_general(a, b, (((1,), (1,)), ((), ())), preferred_element_type=F32)


def tn(a, b):
    return lax.dot_general(a, b, (((0,), (0,)), ((), ())), preferred_element_type=F32)


def iota(shape, dim):
    return lax.broadcasted_iota(jnp.int32, shape, dim)


def segments(pos, ends):
    total = jnp.zeros(pos.shape, jnp.int32)
    for end in ends:
        total = total + (pos >= end).astype(jnp.int32)
    return total


def block_ends(lens_ref, block, count):
    ends, total = [], 0
    for slot in range(count):
        total = total + lens_ref[block, slot]
        ends.append(total)
    return ends


def keep_masks(rows, ends, taps):
    pos = iota((rows, LANES), 0)
    seg = segments(pos, ends)
    keeps = []
    for off in range(1, taps):
        same = (segments(pos - off, ends) == seg) & (pos >= off)
        keeps.append(same.astype(F32))
    valid = (seg < len(ends)).astype(F32)
    return keeps, valid


def conv_tile(u, weights, bias, keeps, taps):
    pre = bias + u * weights[taps - 1 : taps, :]
    for off in range(1, taps):
        pre = pre + pltpu.roll(u, off, 0) * keeps[off - 1] * weights[taps - 1 - off : taps - off, :]
    return pre


def softplus(v):
    return jnp.maximum(v, 0.0) + jnp.log1p(jnp.exp(-jnp.abs(v)))


def split(a):
    hi = a.astype(BF16)
    return hi, (a - hi.astype(F32)).astype(BF16)


def three(product, a, b):
    ah, al = split(a)
    bh, bl = split(b)
    return product(ah, bh) + (product(ah, bl) + product(al, bh))


class Sizes:
    pass


def fwd_kernel(sz, lens_ref, x_ref, go_ref, wzx_ref, wtl_ref, wo_ref, gain_ref, cw_ref, cb_ref, gate_ref, head_ref, rank_ref,
               nrm_ref, pzx_ref, ptl_ref, y_ref, gm_ref, q_ref):
    b = pl.program_id(0)
    rows, cs, st = sz.rows, sz.cs, sz.state
    tiles = cs // LANES
    ends = block_ends(lens_ref, b, sz.seqs)
    xb = x_ref[0].astype(F32)
    mean = jnp.mean(xb * xb, axis=1, keepdims=True)
    nrm = (xb * lax.rsqrt(mean + EPS) * gain_ref[...]).astype(BF16)
    nrm_ref[0] = nrm
    pzx = nn(nrm, wzx_ref[...])
    ptl = nn(nrm, wtl_ref[...])
    gm = nt(go_ref[0], wo_ref[...])
    pzx_ref[0] = pzx
    ptl_ref[0] = ptl
    gm_ref[0] = gm
    keeps, valid = keep_masks(rows, ends, sz.taps)

    def act(u, at):
        w = cw_ref[:, at : at + LANES]
        return jax.nn.silu(conv_tile(u, w, cb_ref[:, at : at + LANES], keeps, sz.taps))

    bm = act(ptl[:, 0:st], cs)
    cm = act(ptl[:, st : 2 * st], cs + st)
    raw = pltpu.roll(ptl[:, 2 * st : 2 * st + LANES], rank_ref[0], 1)
    dt = softplus(raw + head_ref[0:1, :])
    rate = -jnp.exp(head_ref[1:2, :])
    tri = (iota((rows, rows), 0) >= iota((rows, rows), 1))
    log_decay = jnp.dot(tri.astype(F32), dt * rate, precision=EXACT, preferred_element_type=F32)
    log_t = log_decay.T
    same = (segments(iota((rows, rows), 0), ends) == segments(iota((rows, rows), 1), ends)) & tri
    drop = jnp.where(same, 0.0, -jnp.inf)
    inner = three(nt, cm, bm)
    low = iota((rows, LANES), 1) < sz.hd
    q1 = jnp.zeros((rows, LANES), F32)
    q2 = jnp.zeros((rows, LANES), F32)
    for j in range(tiles):
        at = j * LANES
        xa = act(pzx[:, cs + at : cs + at + LANES], at)
        dt2 = jnp.where(low, dt[:, 2 * j : 2 * j + 1], dt[:, 2 * j + 1 : 2 * j + 2])
        xd = xa * dt2
        parts = []
        for e in range(2):
            h = 2 * j + e
            spread = log_decay[:, h : h + 1] - log_t[h : h + 1, :]
            f = (jnp.exp(spread + drop) * inner).astype(BF16)
            mine = low if e == 0 else jnp.logical_not(low)
            parts.append(nn(f, jnp.where(mine, xd, 0.0).astype(BF16)))
        y = parts[0] + parts[1] + xa * gate_ref[1:2, at : at + LANES]
        y_ref[0, :, at : at + LANES] = y
        zt = pzx[:, at : at + LANES]
        gated = y * (zt * jax.nn.sigmoid(zt))
        q1 = q1 + gated * gated
        q2 = q2 + gated * gm[:, at : at + LANES] * gate_ref[0:1, at : at + LANES]
    q2 = q2 * valid
    lane = iota((rows, LANES), 1)
    stats = jnp.where(lane == 0, jnp.sum(q1, axis=1, keepdims=True), jnp.sum(q2, axis=1, keepdims=True)).T
    q_ref[0] = stats[0:8, :]


def bwd_kernel(sz, lens_ref, nrm_ref, x_ref, go_ref, pzx_ref, ptl_ref, y_ref, gm_ref, q_ref, wzx_ref, wtl_ref, wo_ref, cw_ref,
               cb_ref, gate_ref, head_ref, rank_ref, mix_ref, hid_ref, dp_ref, dt_ref, gn_ref, small_ref):
    b = pl.program_id(0)
    rows, cs, st, taps = sz.rows, sz.cs, sz.state, sz.taps
    tiles = cs // LANES
    ends = block_ends(lens_ref, b, sz.seqs)
    keeps, valid = keep_masks(rows, ends, taps)
    at_gate, at_conv, at_head, at_gain = sz.at_gate, sz.at_conv, sz.at_head, sz.at_gain

    @pl.when(b == 0)
    def _():
        small_ref[...] = jnp.zeros(small_ref.shape, F32)

    def colsum(v):
        return jnp.sum(v, axis=0, keepdims=True)

    def conv_pre(u, at):
        return conv_tile(u, cw_ref[:, at : at + LANES], cb_ref[:, at : at + LANES], keeps, taps)

    def silu_pair(v):
        s = jax.nn.sigmoid(v)
        return v * s, s * (1.0 + v * (1.0 - s))

    def conv_back(u, dact, dsilu, at):
        dpre = dact * dsilu
        tile = at // LANES
        row = at_conv + tile * 8 if tile < tiles else sz.at_bc + (tile - tiles) * 8
        back = dpre * cw_ref[taps - 1 : taps, at : at + LANES]
        small_ref[row + taps - 1 : row + taps, :] += colsum(dpre * u)
        small_ref[row + taps : row + taps + 1, :] += colsum(dpre)
        for off in range(1, taps):
            kept = dpre * keeps[off - 1]
            tap = taps - 1 - off
            small_ref[row + tap : row + tap + 1, :] += colsum(kept * pltpu.roll(u, off, 0))
            back = back + pltpu.roll(kept, rows - off, 0) * cw_ref[tap : tap + 1, at : at + LANES]
        return back

    ub, uc = ptl_ref[0, :, 0:st], ptl_ref[0, :, st : 2 * st]
    bm, bslope = silu_pair(conv_pre(ub, cs))
    cm, cslope = silu_pair(conv_pre(uc, cs + st))
    raw = pltpu.roll(ptl_ref[0, :, 2 * st : 2 * st + LANES], rank_ref[0], 1) + head_ref[0:1, :]
    dt = softplus(raw)
    rate = -jnp.exp(head_ref[1:2, :])
    tri = (iota((rows, rows), 0) >= iota((rows, rows), 1))
    log_decay = jnp.dot(tri.astype(F32), dt * rate, precision=EXACT, preferred_element_type=F32)
    log_t = log_decay.T
    upper = (iota((rows, rows), 1) >= iota((rows, rows), 0))
    same = (segments(iota((rows, rows), 0), ends) == segments(iota((rows, rows), 1), ends)) & upper
    drop = jnp.where(same, 0.0, -jnp.inf)
    inner_t = three(nt, bm, cm)
    low = iota((rows, LANES), 1) < sz.hd
    lane = iota((rows, LANES), 1)

    q1 = jnp.broadcast_to(q_ref[0, 0:1, :], (LANES, rows)).T
    q2 = jnp.broadcast_to(q_ref[0, 1:2, :], (LANES, rows)).T
    scale = lax.rsqrt(q1 / sz.di + EPS)
    pull = scale * scale * scale * q2 / sz.di

    dcb = jnp.zeros((rows, rows), F32)
    ddt = jnp.zeros((rows, LANES), F32)
    cols = jnp.zeros((rows, LANES), F32)
    rowsums = jnp.zeros((LANES, rows), F32)
    lane_row = iota((LANES, rows), 0)
    for j in range(tiles):
        at = j * LANES
        tile = slice(at, at + LANES)
        zt = pzx_ref[0, :, tile]
        y = y_ref[0, :, tile]
        gm = gm_ref[0, :, tile] * valid
        gate = gate_ref[0:1, tile]
        sz_, zslope = silu_pair(zt)
        gated = y * sz_
        unit = gated * scale
        mix_ref[0, :, tile] = (unit * gate * valid).astype(BF16)
        small_ref[at_gate + j : at_gate + j + 1, :] += colsum(gm * unit)
        dgated = scale * gm * gate - gated * pull
        dp_ref[0, :, tile] = (dgated * y * zslope).astype(BF16)
        dy = dgated * sz_
        ux = pzx_ref[0, :, cs + at : cs + at + LANES]
        xa, xslope = silu_pair(conv_pre(ux, at))
        small_ref[at_head + 3 + j : at_head + 4 + j, :] += colsum(dy * xa)
        dt2 = jnp.where(low, dt[:, 2 * j : 2 * j + 1], dt[:, 2 * j + 1 : 2 * j + 2])
        xd = xa * dt2
        dxd = []
        for e in range(2):
            h = 2 * j + e
            mine = low if e == 0 else jnp.logical_not(low)
            decay = jnp.exp(log_t[h : h + 1, :] - log_decay[:, h : h + 1] + drop)
            df = three(nt, jnp.where(mine, xd, 0.0), dy) * decay
            dcb = dcb + df
            p = df * inner_t
            cols = jnp.where(lane == h, jnp.sum(p, axis=1, keepdims=True), cols)
            rowsums = jnp.where(lane_row == h, colsum(p), rowsums)
            dxd.append(nn((decay * inner_t).astype(BF16), jnp.where(mine, dy, 0.0).astype(BF16)))
        dxd = dxd[0] + dxd[1]
        both = dxd * xa
        ddt = jnp.where(lane == 2 * j, jnp.sum(jnp.where(low, both, 0.0), axis=1, keepdims=True), ddt)
        ddt = jnp.where(lane == 2 * j + 1, jnp.sum(jnp.where(low, 0.0, both), axis=1, keepdims=True), ddt)
        dx = dxd * dt2 + dy * gate_ref[1:2, tile]
        dp_ref[0, :, cs + at : cs + at + LANES] = conv_back(ux, dx, xslope, at).astype(BF16)

    ga = jnp.dot(upper.astype(F32), rowsums.T - cols, precision=EXACT, preferred_element_type=F32)
    ddt = ddt + ga * rate
    small_ref[at_head : at_head + 1, :] += rate * colsum(ga * dt)
    draw = jnp.where(lane < sz.nh, ddt * jax.nn.sigmoid(raw), 0.0)
    small_ref[at_head + 1 : at_head + 2, :] += colsum(draw)
    dt_ref[0, :, 2 * st : 2 * st + LANES] = pltpu.roll(draw, rank_ref[1], 1).astype(BF16)
    dcb = dcb.astype(BF16)
    db = nn(dcb, cm.astype(BF16))
    dc = tn(dcb, bm.astype(BF16))
    dt_ref[0, :, 0:st] = conv_back(ub, db, bslope, cs).astype(BF16)
    dt_ref[0, :, st : 2 * st] = conv_back(uc, dc, cslope, cs + st).astype(BF16)

    hid_ref[0] = nn(mix_ref[0], wo_ref[...]).astype(BF16)
    gn = nt(dp_ref[0], wzx_ref[...]) + nt(dt_ref[0], wtl_ref[...])
    gn_ref[0] = gn.astype(BF16)
    xb = x_ref[0].astype(F32)
    xhat = xb * lax.rsqrt(jnp.mean(xb * xb, axis=1, keepdims=True) + EPS)
    sums = colsum(gn * xhat)
    for k in range(sz.d // LANES):
        small_ref[at_gain + k : at_gain + k + 1, :] += sums[:, k * LANES : (k + 1) * LANES]


def up8(count):
    return -(-count // 8) * 8


def small_layout(sz):
    tiles = sz.cs // LANES
    sz.at_gain = 0
    sz.at_bc = up8(sz.d // LANES)
    sz.common = sz.at_bc + 2 * sz.state // LANES * 8
    sz.at_conv = sz.common
    sz.at_gate = sz.at_conv + tiles * 8
    sz.at_head = sz.at_gate + up8(tiles)
    sz.small_rows = sz.at_head + up8(3 + tiles)


def run_fwd(sz, lens, ranks, x_all, go_all, wzx, wtl, wo, gain, cw, cb, gate, head):
    t, rows, d, cs, tl = sz.t, sz.rows, sz.d, sz.cs, sz.tl
    whole = lambda a: pl.BlockSpec(a.shape, lambda b, *_: (0,) * a.ndim)
    block = lambda width: pl.BlockSpec((1, rows, width), lambda b, *_: (b, 0, 0))
    smem = pl.BlockSpec(memory_space=pltpu.SMEM)
    kernel = functools.partial(fwd_kernel, sz)
    return pl.pallas_call(
        kernel,
        grid=(t,),
        in_specs=[smem, block(d), block(d), whole(wzx), whole(wtl), whole(wo), whole(gain), whole(cw), whole(cb), whole(gate), whole(head), smem],
        out_specs=[block(d), block(2 * cs), block(tl), block(cs), block(cs), pl.BlockSpec((1, 8, rows), lambda b: (b, 0, 0))],
        out_shape=[
            jax.ShapeDtypeStruct((t, rows, d), BF16),
            jax.ShapeDtypeStruct((t, rows, 2 * cs), F32),
            jax.ShapeDtypeStruct((t, rows, tl), F32),
            jax.ShapeDtypeStruct((t, rows, cs), F32),
            jax.ShapeDtypeStruct((t, rows, cs), F32),
            jax.ShapeDtypeStruct((t, 8, rows), F32),
        ],
        compiler_params=pltpu.CompilerParams(vmem_limit_bytes=60 << 20),
        name="fwd",
    )(lens, x_all, go_all, wzx, wtl, wo, gain, cw, cb, gate, head, ranks)


def run_bwd(sz, lens, ranks, nrm, x_all, go_all, pzx, ptl, y, gm, q, wzx, wtl, wo, cw, cb, gate, head):
    t, rows, d, cs, tl = sz.t, sz.rows, sz.d, sz.cs, sz.tl
    whole = lambda a: pl.BlockSpec(a.shape, lambda b, *_: (0,) * a.ndim)
    block = lambda width: pl.BlockSpec((1, rows, width), lambda b, *_: (b, 0, 0))
    smem = pl.BlockSpec(memory_space=pltpu.SMEM)
    kernel = functools.partial(bwd_kernel, sz)
    return pl.pallas_call(
        kernel,
        grid=(t,),
        in_specs=[smem, block(d), block(d), block(d), block(2 * cs), block(tl), block(cs), block(cs), pl.BlockSpec((1, 8, rows), lambda b: (b, 0, 0)),
                  whole(wzx), whole(wtl), whole(wo), whole(cw), whole(cb), whole(gate), whole(head), smem],
        out_specs=[block(cs), block(d), block(2 * cs), block(tl), block(d), pl.BlockSpec((sz.small_rows, LANES), lambda b: (0, 0))],
        out_shape=[
            jax.ShapeDtypeStruct((t, rows, cs), BF16),
            jax.ShapeDtypeStruct((t, rows, d), BF16),
            jax.ShapeDtypeStruct((t, rows, 2 * cs), BF16),
            jax.ShapeDtypeStruct((t, rows, tl), BF16),
            jax.ShapeDtypeStruct((t, rows, d), BF16),
            jax.ShapeDtypeStruct((sz.small_rows, LANES), F32),
        ],
        compiler_params=pltpu.CompilerParams(vmem_limit_bytes=60 << 20),
        name="bwd",
    )(lens, nrm, x_all, go_all, pzx, ptl, y, gm, q, wzx, wtl, wo, cw, cb, gate, head, ranks)


def device_of(sz, g, t):
    return (lax.div(g, sz.z) * sz.fi + lax.div(t, 2), lax.rem(g, sz.z) * 2 + lax.rem(t, 2))


def index_of(sz, g, t):
    f, p = device_of(sz, g, t)
    return f * sz.p + p


class Place:
    def __init__(self, sz):
        f, p = lax.axis_index("fsdp"), lax.axis_index("dp")
        fi, z = lax.rem(f, sz.fi), lax.div(p, 2)
        self.c = lax.rem(p, 2)
        self.g = lax.div(f, sz.fi) * sz.z + z
        self.t = fi * 2 + self.c
        self.i = f * sz.p + p
        u, v = lax.rem(fi, 2), lax.div(fi, 2)
        across, along = v * 2 + 1 - u, (1 - v) * 2 + u
        self.fi = fi
        self.fa = across * (1 - self.c) + along * self.c
        self.fb = along * (1 - self.c) + across * self.c
        self.fd = sz.fi - 1 - fi
        self.other = 1 - self.c


def remote(sz, src, dst, send, recv, g, t):
    return pltpu.make_async_remote_copy(
        src_ref=src, dst_ref=dst, send_sem=send, recv_sem=recv, device_id=device_of(sz, g, t), device_id_type=pl.DeviceIdType.MESH
    )


def landed(ref, sem):
    pltpu.make_async_copy(ref, ref, sem).wait()


def greet_all(sz, me):
    barrier = pltpu.get_barrier_semaphore()

    @pl.loop(1, sz.n)
    def _(step):
        there = lax.rem(me.i + step, sz.n)
        pl.semaphore_signal(barrier, inc=1, device_id=(lax.div(there, sz.p), lax.rem(there, sz.p)), device_id_type=pl.DeviceIdType.MESH)

    pl.semaphore_wait(barrier, sz.n - 1)


class PlaneGather:
    def __init__(self, sz, me, parts, own, view, send, recv):
        self.sz, self.me, self.parts, self.own, self.view, self.send, self.recv = sz, me, parts, own, view, send, recv
        m = me
        self.a, self.b, self.d = m.fa * 2 + m.c, m.fb * 2 + m.c, m.fd * 2 + m.c
        self.pair = m.fi * 2 + m.other

    def copy(self, kind, slot, part, target, own=False):
        src = self.own(part) if own else self.view(slot, part)
        return remote(self.sz, src, self.view(slot, part), self.send.at[kind, part], self.recv.at[slot, part], self.me.g, target)

    def copies(self, part):
        m = self.me
        yield self.copy(0, m.t, part, self.a, True)
        yield self.copy(1, m.t, part, self.b, True)
        yield self.copy(2, m.t, part, self.pair, True)
        yield self.copy(3, self.a, part, self.b)
        yield self.copy(4, self.a, part, self.pair)
        yield self.copy(5, self.b, part, self.pair)
        yield self.copy(6, self.d, part, self.pair)

    def arrived(self, slot, part):
        landed(self.view(slot, part), self.recv.at[slot, part])

    def start(self):
        for part in range(self.parts):
            for copy in list(self.copies(part))[:3]:
                copy.start()

    def relay(self):
        for part in range(self.parts):
            _, _, _, on, first, second, _ = self.copies(part)
            self.arrived(self.a, part)
            on.start()
            first.start()
            self.arrived(self.b, part)
            second.start()

    def relay_far(self):
        for part in range(self.parts):
            self.arrived(self.d, part)
            list(self.copies(part))[6].start()

    def finish(self):
        for part in range(self.parts):
            for fi in (self.me.fi, self.me.fa, self.me.fb, self.me.fd):
                self.arrived(fi * 2 + self.me.other, part)
            for copy in self.copies(part):
                copy.wait_send()


def gather_kernel(sz, x, go, win, tail, wout, sm, X, GO, WZX, WTL, WO, SM, vx, vg, vw, vt, vo, vs, xsend, xrecv, gsend, grecv, wsend, wrecv,
                  asend, arecv, zsend, zrecv, tsend, trecv, osend, orecv, ssend, srecv, lsem):
    me = Place(sz)
    cs, rows, G, T = sz.cs, sz.rows, sz.g, sz.t
    greet_all(sz, me)

    @pl.loop(1, sz.n)
    def _(step):
        there = lax.rem(me.i + step, sz.n)
        pltpu.make_async_remote_copy(
            src_ref=sm, dst_ref=SM.at[me.i], send_sem=ssend.at[0], recv_sem=srecv.at[0],
            device_id=(lax.div(there, sz.p), lax.rem(there, sz.p)), device_id_type=pl.DeviceIdType.MESH,
        ).start()

    def slices(t):
        return [
            (win.at[:, pl.ds(pl.multiple_of(half * sz.di + t * cs, LANES), cs)], half) for half in range(2)
        ]

    def exchange(step):
        there = lax.rem(me.t + step, T)
        return [
            remote(sz, src, WZX.at[me.i, :, pl.ds(half * cs, cs)], asend.at[step, half], arecv.at[me.t, half], me.g, there)
            for src, half in slices(there)
        ]

    for step in range(1, T):
        for copy in exchange(step):
            copy.start()

    def tail_copy(step):
        there = lax.rem(me.g + step, G)
        return remote(sz, tail, WTL.at[me.i], tsend.at[step], trecv.at[me.g], there, me.t)

    for step in range(1, G):
        tail_copy(step).start()

    owner_t, piece = lax.div(me.i, G), lax.rem(me.i, G)

    def out_copy(g):
        return remote(sz, wout, WO.at[piece], osend.at[g], orecv.at[piece], g, owner_t)

    def is_self(g):
        return (owner_t == me.t) & (me.g == g)

    for g in range(G):
        @pl.when(jnp.logical_not(is_self(g)))
        def _(g=g):
            out_copy(g).start()

    gx = PlaneGather(sz, me, sz.parts, lambda k: x.at[pl.ds(k * sz.part_rows, sz.part_rows)],
                     lambda s, k: X.at[s, pl.ds(k * sz.part_rows, sz.part_rows)], xsend, xrecv)
    gg = PlaneGather(sz, me, sz.parts, lambda k: go.at[pl.ds(k * sz.part_rows, sz.part_rows)],
                     lambda s, k: GO.at[s, pl.ds(k * sz.part_rows, sz.part_rows)], gsend, grecv)
    gt = PlaneGather(sz, me, G, lambda k: WTL.at[index_of(sz, k, me.t)], lambda s, k: WTL.at[index_of(sz, k, s)], wsend, wrecv)
    gx.start()

    mine = slices(me.t)
    ins = [
        pltpu.make_async_copy(mine[0][0], vw.at[:, 0:cs], lsem.at[0]),
        pltpu.make_async_copy(mine[1][0], vw.at[:, cs:], lsem.at[1]),
        pltpu.make_async_copy(tail, vt, lsem.at[2]),
        pltpu.make_async_copy(sm, vs, lsem.at[3]),
        pltpu.make_async_copy(x, vx, lsem.at[4]),
        pltpu.make_async_copy(go, vg, lsem.at[5]),
    ]
    for copy in ins:
        copy.start()
    for copy in ins:
        copy.wait()
    outs = [
        pltpu.make_async_copy(vw, WZX.at[me.i], lsem.at[0]),
        pltpu.make_async_copy(vt, WTL.at[me.i], lsem.at[1]),
        pltpu.make_async_copy(vs, SM.at[me.i], lsem.at[2]),
        pltpu.make_async_copy(vx, X.at[me.t], lsem.at[3]),
        pltpu.make_async_copy(vg, GO.at[me.t], lsem.at[4]),
    ]
    for copy in outs:
        copy.start()
    for copy in outs:
        copy.wait()

    @pl.when(owner_t == me.t)
    def _():
        copy = pltpu.make_async_copy(wout, vo, lsem.at[6])
        copy.start()
        copy.wait()
        copy = pltpu.make_async_copy(vo, WO.at[piece], lsem.at[6])
        copy.start()
        copy.wait()

    for step in range(1, G):
        there = lax.rem(me.g + step, G)
        landed(WTL.at[index_of(sz, there, me.t)], trecv.at[there])
    gt.start()
    for step in range(1, T):
        there = lax.rem(me.t + step, T)
        for half in range(2):
            landed(WZX.at[index_of(sz, me.g, there), :, pl.ds(half * cs, cs)], arecv.at[there, half])

    def line(step, fi, up):
        plane = me.g - step if up else me.g + step
        have = (plane >= 0) if up else (plane < G)
        more = (me.g < G - 1) if up else (me.g > 0)
        plane = jnp.clip(plane, 0, G - 1)
        block = WZX.at[pl.ds(index_of(sz, plane, jnp.int32(2 * fi)), 2)]
        nxt = jnp.clip(me.g + 1 if up else me.g - 1, 0, G - 1)
        copy = remote(sz, block, block, zsend.at[int(up), plane, fi], zrecv.at[plane, fi], nxt, me.t)
        return have, more, block, copy, plane

    def advance(step):
        for fi in range(sz.fi):
            for up in (True, False):
                have, more, block, copy, plane = line(step, fi, up)
                if step > 0:
                    @pl.when(have)
                    def _(block=block, plane=plane, fi=fi):
                        landed(block, zrecv.at[plane, fi])
                if step < G - 1:
                    @pl.when(have & more)
                    def _(copy=copy):
                        copy.start()

    advance(0)
    gx.relay()
    gg.start()
    gt.relay()
    advance(1)
    gx.relay_far()
    gt.relay_far()
    gg.relay()
    for step in range(2, G):
        advance(step)
    gg.relay_far()
    gx.finish()
    gt.finish()
    gg.finish()
    for k in range(G):
        @pl.when(t_differs(sz, me, k))
        def _(k=k):
            landed(WO.at[k], orecv.at[k])
    for g in range(G):
        @pl.when(jnp.logical_not(is_self(g)))
        def _(g=g):
            out_copy(g).wait_send()
    for step in range(1, T):
        for copy in exchange(step):
            copy.wait_send()
    for step in range(1, G):
        tail_copy(step).wait_send()
    for step in range(G - 1):
        for fi in range(sz.fi):
            for up in (True, False):
                have, more, _, copy, _ = line(step, fi, up)

                @pl.when(have & more)
                def _(copy=copy):
                    copy.wait_send()
    landed(SM.at[pl.ds(0, sz.n - 1)], srecv.at[0])
    landed(SM.at[pl.ds(0, sz.n - 1)], ssend.at[0])


def t_differs(sz, me, k):
    return me.t * sz.g + k != me.i


def run_gather(sz, x, go, win, tail, wout, sm):
    n, g, t, rows, d, cs, tl, parts = sz.n, sz.g, sz.t, sz.rows, sz.d, sz.cs, sz.tl, sz.parts
    dn, on = win.shape[0], wout.shape[0]
    any_ = pl.BlockSpec(memory_space=pl.ANY)
    dma = pltpu.SemaphoreType.DMA
    return pl.pallas_call(
        functools.partial(gather_kernel, sz),
        in_specs=[any_] * 6,
        out_specs=[any_] * 6,
        out_shape=[
            jax.ShapeDtypeStruct((t, rows, d), BF16),
            jax.ShapeDtypeStruct((t, rows, d), BF16),
            jax.ShapeDtypeStruct((n, dn, 2 * cs), BF16),
            jax.ShapeDtypeStruct((n, dn, tl), BF16),
            jax.ShapeDtypeStruct((g, on, d), BF16),
            jax.ShapeDtypeStruct((n,) + sm.shape, F32),
        ],
        scratch_shapes=[
            pltpu.VMEM((rows, d), BF16), pltpu.VMEM((rows, d), BF16), pltpu.VMEM((dn, 2 * cs), BF16), pltpu.VMEM((dn, tl), BF16),
            pltpu.VMEM((on, d), BF16), pltpu.VMEM(sm.shape, F32),
            dma((7, parts)), dma((t, parts)), dma((7, parts)), dma((t, parts)), dma((7, g)), dma((t, g)),
            dma((t, 2)), dma((t, 2)), dma((2, g, sz.fi)), dma((g, sz.fi)), dma((g,)), dma((g,)), dma((g,)), dma((g,)), dma((1,)), dma((1,)), dma((8,)),
        ],
        compiler_params=pltpu.CompilerParams(collective_id=0, has_side_effects=True),
        name="gather",
    )(x, go, win, tail, wout, sm)


def stats_kernel(sz, q, out, held, send, recv):
    me = Place(sz)
    barrier = pltpu.get_barrier_semaphore()
    for step in range(1, sz.t):
        f, p = device_of(sz, me.g, lax.rem(me.t + step, sz.t))
        pl.semaphore_signal(barrier, inc=1, device_id=(f, p), device_id_type=pl.DeviceIdType.MESH)
    pl.semaphore_wait(barrier, sz.t - 1)

    def copy(step):
        return remote(sz, q, held.at[me.t], send.at[step], recv.at[me.t], me.g, lax.rem(me.t + step, sz.t))

    for step in range(1, sz.t):
        copy(step).start()
    total = q[...]
    for step in range(1, sz.t):
        there = lax.rem(me.t + step, sz.t)
        landed(held.at[there], recv.at[there])
        total = total + held[there]
    out[...] = total
    for step in range(1, sz.t):
        copy(step).wait_send()


def run_stats(sz, q):
    vmem = pl.BlockSpec(memory_space=pltpu.VMEM)
    dma = pltpu.SemaphoreType.DMA
    return pl.pallas_call(
        functools.partial(stats_kernel, sz),
        in_specs=[vmem],
        out_specs=vmem,
        out_shape=jax.ShapeDtypeStruct(q.shape, F32),
        scratch_shapes=[pltpu.VMEM((sz.t,) + q.shape, F32), dma((sz.t,)), dma((sz.t,))],
        compiler_params=pltpu.CompilerParams(collective_id=1, has_side_effects=True),
        name="stats",
    )(q)


def reduce_kernel(sz, hp, gp, dwzx, dwtl, dwo, sm, hsum, gsum, gin, gtl, gout, gsm, hs, gs, r0h, r0g, r1h, r1g, r2h, r2g, rz, sz_, ro, rt, st, rtz, ra,
                  rs1, s1, rs2, p0send, p0recv, p1send, p1recv, p2send, p2recv, zsend, zrecv, asend, arecv, osend, orecv, tsend, trecv, uzsend, uzrecv,
                  s1send, s1recv, s2send, s2recv, usend, urecv):
    me = Place(sz)
    cs, rows, G, T, FI = sz.cs, sz.rows, sz.g, sz.t, sz.fi
    parts, pr = sz.rparts, sz.rows // sz.rparts
    greet_all(sz, me)

    def up32(v):
        return v.astype(F32)

    def s1_copy(step):
        return remote(sz, sm, rs1.at[me.g], s1send.at[step], s1recv.at[me.g], lax.rem(me.g + step, G), me.t)

    for step in range(1, G):
        s1_copy(step).start()

    arrays = [(hp, hs, r0h, r1h, r2h, hsum), (gp, gs, r0g, r1g, r2g, gsum)]
    order = (me.fa, me.fd, me.fb, me.fi)

    def p0_copy(k, which, part):
        src, _, r0 = arrays[k][:3]
        fi = order[which]
        rows_ = pl.ds(part * pr, pr)
        return remote(sz, src.at[fi * 2 + me.other, rows_], r0.at[fi, rows_], p0send.at[k, which, part], p0recv.at[k, fi, part], me.g, me.fi * 2 + me.other)

    for k in range(2):
        for which in range(4):
            for part in range(parts):
                p0_copy(k, which, part).start()

    def t_copy(step, g):
        there = lax.rem(me.t + step, T)
        return remote(sz, dwtl.at[index_of(sz, g, there)], rt.at[me.t, g], tsend.at[step, g], trecv.at[me.t, g], me.g, there)

    for step in range(1, T):
        for g in range(G):
            t_copy(step, g).start()

    def z_copy(step, fi):
        there = lax.rem(me.g + step, G)
        return remote(sz, dwzx.at[pl.ds(index_of(sz, there, jnp.int32(2 * fi)), 2)], rz.at[me.g, pl.ds(2 * fi, 2)], zsend.at[step, fi], zrecv.at[me.g, fi],
                      there, me.t)

    for step in range(1, G):
        for fi in range(FI):
            z_copy(step, fi).start()

    def o_copy(k):
        owner = me.t * G + k
        f, p = lax.div(owner, sz.p), lax.rem(owner, sz.p)
        return pltpu.make_async_remote_copy(src_ref=dwo.at[k], dst_ref=ro.at[me.g], send_sem=osend.at[k], recv_sem=orecv.at[me.g],
                                            device_id=(f, p), device_id_type=pl.DeviceIdType.MESH)

    for k in range(G):
        @pl.when(t_differs(sz, me, k))
        def _(k=k):
            o_copy(k).start()

    def p1_copy(k, which, part):
        _, s, _, r1 = arrays[k][:4]
        rows_ = pl.ds(part * pr, pr)
        return remote(sz, s.at[which, rows_], r1.at[which, rows_], p1send.at[k, which, part], p1recv.at[k, which, part], me.g, me.fa * 2 + me.c)

    def p2_copy(k, part):
        _, s, _, _, r2 = arrays[k][:5]
        rows_ = pl.ds(part * pr, pr)
        return remote(sz, s.at[2, rows_], r2.at[rows_], p2send.at[k, part], p2recv.at[k, part], me.g, me.fb * 2 + me.c)

    for k in range(2):
        src, s, r0, r1, r2, out = arrays[k]
        for which in range(4):
            fi = order[which]
            for part in range(parts):
                rows_ = pl.ds(part * pr, pr)
                landed(r0.at[fi, rows_], p0recv.at[k, fi, part])
                both = up32(src[fi * 2 + me.c, rows_]) + up32(r0[fi, rows_])
                if which < 2:
                    s[which, rows_] = both.astype(BF16)
                    p1_copy(k, which, part).start()
                elif which == 2:
                    s[2, rows_] = both.astype(BF16)
                else:
                    out[rows_] = both

    for step in range(1, T):
        for g in range(G):
            there = lax.rem(me.t + step, T)
            landed(rt.at[there, g], trecv.at[there, g])
    for g in range(G):
        total = up32(dwtl[index_of(sz, g, me.t)])
        for step in range(1, T):
            total = total + up32(rt[lax.rem(me.t + step, T), g])
        st[g] = total.astype(BF16)

    def uz_copy(step):
        there = lax.rem(me.g + step, G)
        return remote(sz, st.at[there], rtz.at[me.g], uzsend.at[step], uzrecv.at[me.g], there, me.t)

    for step in range(1, G):
        uz_copy(step).start()

    total = sm[...]
    for step in range(1, G):
        there = lax.rem(me.g + step, G)
        landed(rs1.at[there], s1recv.at[there])
        total = total + rs1[there]
    s1[...] = total
    rs2[me.t] = total

    def s2_copy(step):
        return remote(sz, s1, rs2.at[me.t], s2send.at[step], s2recv.at[me.t], me.g, lax.rem(me.t + step, T))

    for step in range(1, T):
        s2_copy(step).start()

    for k in range(2):
        src, s, r0, r1, r2, out = arrays[k]
        for part in range(parts):
            rows_ = pl.ds(part * pr, pr)
            landed(r1.at[1, rows_], p1recv.at[k, 1, part])
            s[2, rows_] = (up32(s[2, rows_]) + up32(r1[1, rows_])).astype(BF16)
            p2_copy(k, part).start()

    for fi in range(FI):
        for step in range(1, G):
            there = lax.rem(me.g + step, G)
            landed(rz.at[there, pl.ds(2 * fi, 2)], zrecv.at[there, fi])
        for c in range(2):
            total = up32(dwzx[index_of(sz, me.g, jnp.int32(2 * fi + c))])
            for step in range(1, G):
                total = total + up32(rz[lax.rem(me.g + step, G), 2 * fi + c])
            sz_[2 * fi + c] = total.astype(BF16)

    def a_copy(step):
        there = lax.rem(me.t + step, T)
        return remote(sz, sz_.at[there], ra.at[me.t], asend.at[step], arecv.at[me.t], me.g, there)

    for step in range(1, T):
        a_copy(step).start()
    ra[me.t] = sz_[me.t]

    total = jnp.zeros(gout.shape, F32)
    mine = lax.div(me.i, G) == me.t

    @pl.when(mine)
    def _():
        gout[...] = up32(dwo[lax.rem(me.i, G)])

    @pl.when(jnp.logical_not(mine))
    def _():
        gout[...] = jnp.zeros(gout.shape, F32)

    for g in range(G):
        other = jnp.logical_not(mine & (me.g == g))

        @pl.when(other)
        def _(g=g):
            landed(ro.at[g], orecv.at[g])
            gout[...] += up32(ro[g])

    total = up32(st[me.g])
    for step in range(1, G):
        there = lax.rem(me.g + step, G)
        landed(rtz.at[there], uzrecv.at[there])
        total = total + up32(rtz[there])
    gtl[...] = total

    for k in range(2):
        src, s, r0, r1, r2, out = arrays[k]
        for part in range(parts):
            rows_ = pl.ds(part * pr, pr)
            landed(r1.at[0, rows_], p1recv.at[k, 0, part])
            landed(r2.at[rows_], p2recv.at[k, part])
            out[rows_] = out[rows_] + up32(r1[0, rows_]) + up32(r2[rows_])

    for step in range(1, T):
        there = lax.rem(me.t + step, T)
        landed(ra.at[there], arecv.at[there])
        landed(rs2.at[there], s2recv.at[there])
    for t in range(T):
        gin[:, t * cs : (t + 1) * cs] = up32(ra[t, :, 0:cs])
        gin[:, sz.di + t * cs : sz.di + (t + 1) * cs] = up32(ra[t, :, cs:])
    total = rs2[0, 0 : sz.common]
    for t in range(1, T):
        total = total + rs2[t, 0 : sz.common]
    gsm[0 : sz.common] = total
    width = sz.small_rows - sz.common
    for t in range(T):
        gsm[sz.common + t * width : sz.common + (t + 1) * width] = rs2[t, sz.common :]

    for step in range(1, G):
        s1_copy(step).wait_send()
        uz_copy(step).wait_send()
        for fi in range(FI):
            z_copy(step, fi).wait_send()
    for step in range(1, T):
        s2_copy(step).wait_send()
        a_copy(step).wait_send()
        for g in range(G):
            t_copy(step, g).wait_send()
    for k in range(2):
        for part in range(parts):
            for which in range(4):
                p0_copy(k, which, part).wait_send()
            for which in range(2):
                p1_copy(k, which, part).wait_send()
            p2_copy(k, part).wait_send()
    for k in range(G):
        @pl.when(t_differs(sz, me, k))
        def _(k=k):
            o_copy(k).wait_send()


def run_reduce(sz, hp, gp, dwzx, dwtl, dwo, sm):
    n, g, t, rows, d, cs, tl, parts, fi = sz.n, sz.g, sz.t, sz.rows, sz.d, sz.cs, sz.tl, sz.rparts, sz.fi
    dn, on = dwzx.shape[1], dwo.shape[1]
    vmem = pl.BlockSpec(memory_space=pltpu.VMEM)
    dma = pltpu.SemaphoreType.DMA
    v = lambda *s: pltpu.VMEM(s, BF16)
    sr = sz.small_rows
    total_rows = sz.common + t * (sr - sz.common)
    return pl.pallas_call(
        functools.partial(reduce_kernel, sz),
        in_specs=[vmem] * 6,
        out_specs=[vmem] * 6,
        out_shape=[
            jax.ShapeDtypeStruct((rows, d), F32),
            jax.ShapeDtypeStruct((rows, d), F32),
            jax.ShapeDtypeStruct((dn, 2 * sz.di), F32),
            jax.ShapeDtypeStruct((dn, tl), F32),
            jax.ShapeDtypeStruct((on, d), F32),
            jax.ShapeDtypeStruct((total_rows, LANES), F32),
        ],
        scratch_shapes=[
            v(3, rows, d), v(3, rows, d), v(fi, rows, d), v(fi, rows, d), v(2, rows, d), v(2, rows, d), v(rows, d), v(rows, d),
            v(g, t, dn, 2 * cs), v(t, dn, 2 * cs), v(g, on, d), v(t, g, dn, tl), v(g, dn, tl), v(g, dn, tl), v(t, dn, 2 * cs),
            pltpu.VMEM((g, sr, LANES), F32), pltpu.VMEM((sr, LANES), F32), pltpu.VMEM((t, sr, LANES), F32),
            dma((2, 4, parts)), dma((2, fi, parts)), dma((2, 2, parts)), dma((2, 2, parts)), dma((2, parts)), dma((2, parts)),
            dma((g, fi)), dma((g, fi)), dma((t,)), dma((t,)), dma((g,)), dma((g,)), dma((t, g)), dma((t, g)), dma((g,)), dma((g,)),
            dma((g,)), dma((g,)), dma((t,)), dma((t,)), dma((1,)), dma((1,)),
        ],
        compiler_params=pltpu.CompilerParams(collective_id=2, has_side_effects=True, vmem_limit_bytes=63 << 20),
        name="reduce",
    )(hp, gp, dwzx, dwtl, dwo, sm)


def sizes(mesh, hidden, lengths, in_proj, conv_weight, gate_gain, decay_log):
    sz = Sizes()
    sz.f, sz.p = mesh.shape["fsdp"], mesh.shape["dp"]
    sz.n = sz.f * sz.p
    sz.rows, sz.d = hidden.shape
    sz.seqs = lengths.shape[1]
    sz.conv, sz.taps = conv_weight.shape[0] * sz.n, conv_weight.shape[1]
    sz.di = gate_gain.shape[0] * sz.n
    sz.state = (sz.conv - sz.di) // 2
    sz.heads = decay_log.shape[0]
    sz.hd = sz.di // sz.heads
    sz.fi = math.gcd(sz.f, sz.di // (2 * LANES))
    sz.t = 2 * sz.fi
    sz.z = sz.p // 2
    sz.g = sz.f // sz.fi * sz.z
    sz.cs, sz.nh = sz.di // sz.t, sz.heads // sz.t
    sz.tail = in_proj.shape[1] - 2 * sz.di
    sz.tl = -(-sz.tail // LANES) * LANES
    sz.parts, sz.rparts = 2, 2
    sz.part_rows = sz.rows // sz.parts
    small_layout(sz)
    return sz


def widen(a, rows, lanes):
    return jnp.pad(a, ((0, rows - a.shape[0]), (0, lanes - a.shape[1])))


def local(mesh, hidden_in, lengths, norm_gain, in_proj, conv_weight, conv_bias, gate_gain, out_proj, decay_log, step_bias, skip_gain, grad_out):
    sz = sizes(mesh, hidden_in, lengths, in_proj, conv_weight, gate_gain, decay_log)
    n, t, cs, di = sz.n, sz.t, sz.cs, sz.di
    f, p = lax.axis_index("fsdp"), lax.axis_index("dp")
    fo, fi, z, c = f // sz.fi, f % sz.fi, p // 2, p % 2
    rank, index = fi * 2 + c, f * sz.p + p
    dn, cn, kn = norm_gain.shape[0], conv_bias.shape[0], gate_gain.shape[0]

    small = [norm_gain, conv_weight.reshape(-1), conv_bias, gate_gain, lengths[0]]
    flat = jnp.concatenate([a.astype(F32) for a in small])
    lanes = -(-flat.shape[0] // (8 * LANES)) * 8 * LANES
    sm = jnp.pad(flat, (0, lanes - flat.shape[0])).reshape(-1, LANES)
    tail = jnp.pad(in_proj[:, 2 * di :], ((0, 0), (0, sz.tl - sz.tail)))
    x_all, go_all, wzx, wtl, wo, sm_all = run_gather(sz, hidden_in, grad_out, in_proj, tail, out_proj, sm)
    flat = sm_all.reshape(n, lanes)
    cuts = [0]
    for a in small:
        cuts.append(cuts[-1] + a.size)
    gain, cw, cb, gate, lens = (flat[:, lo:hi] for lo, hi in zip(cuts[:-1], cuts[1:]))
    gain = gain.reshape(1, sz.d)
    cw = cw.reshape(sz.conv, sz.taps)
    cb, gate = cb.reshape(-1), gate.reshape(-1)
    here = lambda a, width: lax.dynamic_slice_in_dim(a, rank * width, width)
    cw = widen(jnp.concatenate([here(cw, cs), cw[di:]]).T, 8, cs + 2 * sz.state)
    cb = jnp.concatenate([here(cb, cs), cb[di:]])[None]
    gate = widen(jnp.stack([here(gate, cs), jnp.repeat(here(skip_gain, sz.nh), sz.hd)]), 8, cs)
    head = widen(jnp.stack([here(step_bias, sz.nh), here(decay_log, sz.nh)]), 8, LANES)
    lens = lens.reshape(sz.f // sz.fi, sz.fi, sz.z, 2, sz.seqs)[fo, :, z].reshape(t, sz.seqs).astype(jnp.int32)
    ranks = jnp.stack([(LANES - sz.nh * rank) % LANES, sz.nh * rank]).astype(jnp.int32)
    wzx, wtl, wo = wzx.reshape(sz.d, 2 * cs), wtl.reshape(sz.d, sz.tl), wo.reshape(cs, sz.d)

    nrm, pzx, ptl, y, gm, q = run_fwd(sz, lens, ranks, x_all, go_all, wzx, wtl, wo, gain, cw, cb, gate, head)
    q = run_stats(sz, q)
    mix, hid, dzx, dtl, gn, small = run_bwd(sz, lens, ranks, nrm, x_all, go_all, pzx, ptl, y, gm, q, wzx, wtl, wo, cw, cb, gate, head)

    tall = lambda a: a.reshape(t * sz.rows, a.shape[2])
    dwzx = tn(tall(nrm), tall(dzx)).astype(BF16).reshape(n, dn, 2 * cs)
    dwtl = tn(tall(nrm), tall(dtl)).astype(BF16).reshape(n, dn, sz.tl)
    dwo = tn(tall(mix), tall(go_all)).astype(BF16).reshape(sz.g, cs // sz.g, sz.d)
    hsum, gsum, gin, gtl, gout, gsm = run_reduce(sz, hid, gn, dwzx, dwtl, dwo, small)

    x = hidden_in.astype(F32)
    hidden_out = (x + hsum).astype(BF16)
    scale = lax.rsqrt(jnp.mean(x * x, axis=1, keepdims=True) + EPS)
    dxhat = gsum * gain
    inner = jnp.mean(dxhat * x, axis=1, keepdims=True)
    grad_in = grad_out.astype(F32) + scale * (dxhat - x * (scale * scale * inner))
    grad_in_proj = jnp.concatenate([gin, gtl[:, : sz.tail]], axis=1)

    own = lambda a, width: lax.dynamic_slice_in_dim(a, index * width, width)
    common, slices = gsm[: sz.common], gsm[sz.common :].reshape(t, -1, LANES)
    at = lambda place: place - sz.common
    grad_norm_gain = own(common[: sz.d // LANES].reshape(-1), dn)
    conv_x = slices[:, : at(sz.at_gate)].reshape(-1, 8, LANES)
    conv = jnp.concatenate([conv_x, common[sz.at_bc :].reshape(-1, 8, LANES)])
    conv = conv[:, : sz.taps + 1].transpose(0, 2, 1).reshape(sz.conv, sz.taps + 1)
    conv = own(conv, cn)
    tiles = cs // LANES
    grad_gate = own(slices[:, at(sz.at_gate) : at(sz.at_gate) + tiles].reshape(-1), kn)
    heads = slices[:, at(sz.at_head) :]
    grad_decay = heads[:, 0, : sz.nh].reshape(-1)
    grad_bias = heads[:, 1, : sz.nh].reshape(-1)
    grad_skip = jnp.sum(heads[:, 3 : 3 + tiles].reshape(sz.heads, sz.hd), axis=1)
    return (hidden_out, grad_in, grad_norm_gain, grad_in_proj, conv[:, : sz.taps], conv[:, sz.taps], grad_gate, gout, grad_decay, grad_bias, grad_skip)


def solution(mesh):
    both = ("fsdp", "dp")
    wide, flat, free = P(both, None), P(both), P()
    in_specs = (wide, wide, flat, wide, wide, flat, flat, wide, free, free, free, wide)
    out_specs = (wide, wide, flat, wide, wide, flat, flat, wide, free, free, free)
    return jax.shard_map(functools.partial(local, mesh), mesh=mesh, in_specs=in_specs, out_specs=out_specs, check_vma=False)
```

time: 1070 us -> 311 us (0.29)
  waiting for transfers between devices: 724 us -> 0 us
  Pallas kernels: 0 us -> 266 us
  matrix products: 144 us -> 18.1 us
  blocking collectives: 85.6 us -> 0 us
  other arithmetic: 50.8 us -> 10.2 us
  local copies, waits for them, and re-layouts: 47.6 us -> 15.5 us
  between operations: 15.5 us -> 0.94 us
    reduce_scatter x2 -> x0, waiting for transfers between devices: 579 us -> none  [the longest x1 370 us: local(): lax.psum_scatter(left_product(columns, proj_low), ('fsdp', 'dp'), scatter...]
    pallas_call x0 -> x5, Pallas kernels: none -> 266 us  [the longest x1 98.4 us: run_reduce(): pl.pallas_call(functools.partial(reduce_kernel, sz), in_specs=[vmem] * 6,...]
    dot_general x18 -> x3, matrix products: 144 us -> 18.1 us  [tn(): lax.dot_general(a, b, (((0,), (0,)), ((), ())), preferred_element_type=F32)]
    unnamed x6 -> x0, waiting for transfers between devices: 86.2 us -> none
    all_gather x2 -> x0, waiting for transfers between devices: 58.4 us -> none  [the longest x1 40.5 us: local(): lax.all_gather(in_proj, ('fsdp', 'dp'), axis=0, tiled=True)]
    unnamed x1 -> x0, blocking collectives: 44.1 us -> none
    all_gather x1 -> x0, blocking collectives: 41.5 us -> none  [local(): lax.all_gather(conv_weight, ('fsdp', 'dp'), axis=0, tiled=True)]
    unnamed x109 -> x25, local copies, waits for them, and re-layouts: 17.9 us -> 2.09 us
  transfers between devices with their start and end apart: 5 -> 0, of which waited for: 5 -> 0; matrix products, arithmetic and copies ran while one was open for 11% -> 0% of each run, Pallas kernels for 0% -> 0%
where the time goes in v1:
time: 311 us
  Pallas kernels  266 us (86%)
  matrix products  18.1 us (6%)
  local copies, waits for them, and re-layouts  15.5 us (5%)
  other arithmetic  10.2 us (3%)
    pallas_call x1, Pallas kernels, run_reduce(): pl.pallas_call(functools.partial(reduce_kernel, sz), in_specs=[vmem] * 6,...  98.4 us
    pallas_call x1, Pallas kernels, run_gather(): pl.pallas_call(functools.partial(gather_kernel, sz), in_specs=[any_] * 6,...  82.8 us
    pallas_call x1, Pallas kernels, run_bwd(): pl.pallas_call(kernel, grid=(t,), in_specs=[smem, block(d), block(d), blo...  47.4 us
    pallas_call x1, Pallas kernels, run_fwd(): pl.pallas_call(kernel, grid=(t,), in_specs=[smem, block(d), block(d), who...  27.6 us
    dot_general x3, matrix products, tn(): lax.dot_general(a, b, (((0,), (0,)), ((), ())), preferred_element_type=F32)  18.1 us
    pallas_call x1, Pallas kernels, run_stats(): pl.pallas_call(functools.partial(stats_kernel, sz), in_specs=[vmem], out_...  9.8 us

profile of v1, /device:TPU:0, one launch (start us, length us, event | category | flops | bytes accessed | tf_op | source)
XLA Modules:
  0.0 310.8 jit_solution(2667242969633989534)
XLA Ops:
  0.7 0.6 pad_add_fusion.rank_ref
  1.3 0.7 convert_bitcast_fusion
  2.0 0.7 dynamic_slice.35
  2.7 0.7 dynamic-slice_bitcast_fusion
  3.4 0.6 select_maximum_fusion.1.head_ref
  4.0 0.1 broadcast_in_dim.9
  4.1 0.1 stack_reshape.3
  4.2 0.8 slice.67
  5.0 0.6 pad.20.tail
  5.6 0.8 copy.30
  6.4 0.1 reshape.132
  6.5 2.1 concatenate.15
  8.6 0.6 pad_bitcast_fusion.sm
  9.2 82.8 %gather.1 = (bf16[8,256,1536]{2,1,0:T(8,128)(2,1)}, bf16[8,256,1536]{2,1,0:T(8,128)(2,1)}, bf16[32,48,768]{2,1,0:T(8,128)(2,1)}, bf16[32,48,384]{2,1,0:T(8,128)(...) custom-call(bf16[256,1536]{1,0:T(8,128)(2,1)} %x.11, bf16[256,1536]{1,0:T(8,128)(2,1)} %go.1, ...), custom_call_target="tpu_custom_call" | custom-call | tf_op jit(solution)/shard_map/gather/pallas_call | solution.py:602
  92.0 0.9 copy.47
  92.9 0.7 reshape.118.gain_ref
  93.6 0.1 mul.80
  93.7 0.1 slice.93
  93.7 0.1 reshape.121
  93.8 0.1 dynamic_slice.34
  93.9 0.6 select_maximum_fusion.gate_ref
  94.5 0.1 slice.91
  94.6 0.1 reshape.120
  94.7 0.1 dynamic_slice.33
  94.8 0.5 broadcast_in_dim.8.cb_ref
  95.3 0.1 slice.87
  95.4 0.1 slice.89
  95.5 0.6 dynamic-slice_convert_fusion
  96.1 0.5 reshape.119
  96.7 0.1 copy.41
  96.7 0.1 copy.42
  96.9 0.6 pad.22.cw_ref
  97.5 27.6 %fwd.1 = (bf16[8,256,1536]{2,1,0:T(8,128)(2,1)}, f32[8,256,768]{2,1,0:T(8,128)}, f32[8,256,384]{2,1,0:T(8,128)}, f32[8,256,384]{2,1,0:T(8,128)}, f32[8,256,384]{2,1,0:T(8,128)}, /*index=5*/f32[8,8,256]{2,1,0:T(8,128)}) custom-call(s32[8,4]{1,0:T(8,128)} %bitcast.78, bf16[8,256,1536]{2,1,0:T(8,128)(2,1)} %get-tuple-element.36.x_ref, ...), custom_call_target="tpu_custom_call" | custom-call | tf_op jit(solution)/shard_map/fwd/pallas_call | solution.py:290
  125.1 9.8 %stats.1.q_ref = f32[8,8,256]{2,1,0:T(8,128)} custom-call(f32[8,8,256]{2,1,0:T(8,128)} %get-tuple-element.46.q), custom_call_target="tpu_custom_call" | custom-call | tf_op jit(solution)/shard_map/stats/pallas_call | solution.py:651
  134.9 47.4 %bwd.1 = (bf16[8,256,384]{2,1,0:T(8,128)(2,1)}, bf16[8,256,1536]{2,1,0:T(8,128)(2,1)}, bf16[8,256,768]{2,1,0:T(8,128)(2,1)}, bf16[8,256,384]{2,1,0:T(8,128)(2,1)...) custom-call(s32[8,4]{1,0:T(8,128)} %bitcast.79, bf16[8,256,1536]{2,1,0:T(8,128)(2,1)} %get-tuple-element.41.nrm_ref, ...), custom_call_target="tpu_custom_call" | custom-call | tf_op jit(solution)/shard_map/bwd/pallas_call | solution.py:314
  182.3 0.0 copy-start.2
  182.3 0.0 copy-start.9
  182.4 7.1 %fusion.1 = bf16[384,1536]{1,0:T(8,128)(2,1)} fusion(bf16[8,256,384]{2,1,0:T(8,128)(2,1)} %get-tuple-element.51, bf16[8,256,1536]{2,1,0:T(8,128)(2,1)} %get-tuple-element.37.go_ref), kind=kOutput, calls=%fused_computation.4 | convolution fusion | flops 2416508928 | bytes 9043968 | tf_op jit(solution)/shard_map/dot_general | solution.py:27
  189.5 0.0 copy-done.2
  189.5 0.0 copy-done.9
  189.5 4.6 %fusion = bf16[1536,384]{1,0:T(8,128)(2,1)} fusion(bf16[8,256,1536]{2,1,0:T(8,128)(2,1)S(1)} %copy-done.2, bf16[8,256,384]{2,1,0:T(8,128)(2,1)S(1)} %copy-done.9), kind=kOutput, calls=%fused_computation.3 | convolution fusion | flops 2416508928 | bytes 9043968 | tf_op jit(solution)/shard_map/dot_general | solution.py:27
  194.0 0.0 copy-done.8
  194.0 6.5 %bitcast_convert_fusion = bf16[1536,768]{1,0:T(8,128)(2,1)} fusion(bf16[8,256,1536]{2,1,0:T(8,128)(2,1)S(1)} %copy-done.2, bf16[8,256,768]{2,1,0:T(8,128)(2,1)S(1)} %copy-done.8), kind=kOutput, calls=%fused_computation | convolution fusion | flops 4833017856 | bytes 11796480 | tf_op jit(solution)/shard_map/dot_general | solution.py:27
  200.5 98.4 %reduce.9 = (f32[256,1536]{1,0:T(8,128)}, f32[256,1536]{1,0:T(8,128)}, f32[48,6144]{1,0:T(8,128)}, f32[48,384]{1,0:T(8,128)}, f32[96,1536]{1,0:T(8,128)}, /*index=5*/f32[352,128]{1,0:T(8,128)}) custom-call(bf16[8,256,1536]{2,1,0:T(8,128)(2,1)} %get-tuple-element.47.hp, bf16[8,256,1536]{2,1,0:T(8,128)(2,1)} %get-tuple-element.48.gp, ...), custom_call_target="tpu_custom_call" | custom-call | tf_op jit(solution)/shard_map/reduce/pallas_call | solution.py:884
  298.9 0.0 copy-start.1
  298.9 0.0 copy-start.3
  298.9 0.0 copy-done
  298.9 2.0 fusion.3
  300.9 0.0 copy-done.1
  300.9 0.1 copy-done.3
  301.0 3.4 %fusion.7 = (f32[256,1536]{1,0:T(8,128)}, bf16[256,1536]{1,0:T(8,128)(2,1)}) fusion(bf16[256,1536]{1,0:T(8,128)(2,1)S(1)} %copy-done, bf16[256,1536]{1,0:T(8,128)(2,1)S(1)} %copy-done.3, f32[256,1536]{1,0:T(8,128)S(1)} %copy-done.1, f32[256]{0:T(256)S(1)} %get-tuple-element.68, f32[1536]{0:T(1024)S(1)} %mul.80, f32[256]{0:T(256)S(1)} %get-tuple-element.67, ...), kind=kLoop, calls=%fused_computation.14 | loop fusion | flops 3538944 | bytes 7086080 | tf_op jit(solution)/shard_map/add | solution.py:983
  304.4 0.0 copy-done.6
  304.5 0.6 dynamic_slice.38
  305.1 0.6 reshape_squeeze.8
  305.7 0.6 reshape_squeeze.7
  306.3 0.1 reshape.131
  306.4 0.6 reduce_sum.29
  307.1 0.6 dynamic_slice.40
  307.7 0.1 constant_dynamic-slice_fusion
  307.8 0.5 slice_bitcast_fusion.2
  308.3 0.6 slice.81
  308.9 1.1 pad_maximum_fusion
  310.0 0.0 copy-done.5
  310.0 0.8 copy.50
  (27 shorter events, 0.2 us)
Async XLA Ops:
  182.3 7.1 %copy-start.2 = (bf16[8,256,1536]{2,1,0:T(8,128)(2,1)S(1)}, bf16[8,256,1536]{2,1,0:T(8,128)(2,1)}, u32[]{:S(2)}) copy-start(bf16[8,256,1536]{2,1,0:T(8,128)(2,1)} %get-tuple-element.41.nrm_ref) | copy-start | bytes 18874372
  182.3 7.1 %copy-start.9 = (bf16[8,256,384]{2,1,0:T(8,128)(2,1)S(1)}, bf16[8,256,384]{2,1,0:T(8,128)(2,1)}, u32[]{:S(2)}) copy-start(bf16[8,256,384]{2,1,0:T(8,128)(2,1)} %get-tuple-element.50) | copy-start | bytes 4718596
  189.5 4.6 %copy-start.8 = (bf16[8,256,768]{2,1,0:T(8,128)(2,1)S(1)}, bf16[8,256,768]{2,1,0:T(8,128)(2,1)}, u32[]{:S(2)}) copy-start(bf16[8,256,768]{2,1,0:T(8,128)(2,1)} %get-tuple-element.49) | copy-start | bytes 9437188
  200.5 98.4 %copy-start = (bf16[256,1536]{1,0:T(8,128)(2,1)S(1)}, bf16[256,1536]{1,0:T(8,128)(2,1)}, u32[]{:S(2)}) copy-start(bf16[256,1536]{1,0:T(8,128)(2,1)} %x.11) | copy-start | bytes 2359300
  298.9 2.0 copy-start.1
  298.9 2.1 copy-start.3
  301.0 3.4 %copy-start.6 = (f32[352,128]{1,0:T(8,128)S(1)}, f32[352,128]{1,0:T(8,128)}, u32[]{:S(2)}) copy-start(f32[352,128]{1,0:T(8,128)} %get-tuple-element.55) | copy-start | bytes 540676
  301.0 7.9 %copy-start.7 = (f32[48,384]{1,0:T(8,128)S(1)}, f32[48,384]{1,0:T(8,128)}, u32[]{:S(2)}) copy-start(f32[48,384]{1,0:T(8,128)} %get-tuple-element.57) | copy-start | bytes 221188
  304.4 4.5 %copy-start.4 = (f32[48,6144]{1,0:T(8,128)S(1)}, f32[48,6144]{1,0:T(8,128)}, u32[]{:S(2)}) copy-start(f32[48,6144]{1,0:T(8,128)} %get-tuple-element.56) | copy-start | bytes 3538948
  306.3 3.7 %copy-start.5 = (f32[96,1536]{1,0:T(8,128)S(1)}, f32[96,1536]{1,0:T(8,128)}, u32[]{:S(2)}) copy-start(f32[96,1536]{1,0:T(8,128)} %get-tuple-element.89) | copy-start | bytes 1769476

commit v2 on v1

v2 whole, which is shorter than its diff:
```python
import functools
import math

import jax
import jax.numpy as jnp
from jax import lax
from jax.experimental import pallas as pl
from jax.experimental.pallas import tpu as pltpu
from jax.sharding import PartitionSpec as P

EPS = 1e-05
F32 = jnp.float32
BF16 = jnp.bfloat16
EXACT = lax.Precision.HIGHEST
LANES = 128


def nn(a, b):
    return lax.dot_general(a, b, (((1,), (0,)), ((), ())), preferred_element_type=F32)


def nt(a, b):
    return lax.dot_general(a, b, (((1,), (1,)), ((), ())), preferred_element_type=F32)


def tn(a, b):
    return lax.dot_general(a, b, (((0,), (0,)), ((), ())), preferred_element_type=F32)


def iota(shape, dim):
    return lax.broadcasted_iota(jnp.int32, shape, dim)


def conv_tile(u, weights, bias, keeps, taps):
    pre = bias + u * weights[taps - 1 : taps, :]
    for off in range(1, taps):
        pre = pre + pltpu.roll(u, off, 0) * keeps[off - 1] * weights[taps - 1 - off : taps - off, :]
    return pre


def softplus(v):
    return jnp.maximum(v, 0.0) + jnp.log1p(jnp.exp(-jnp.abs(v)))


def split(a):
    hi = a.astype(BF16)
    return hi, (a - hi.astype(F32)).astype(BF16)


def three(product, a, b):
    ah, al = split(a)
    bh, bl = split(b)
    return product(ah, bh) + (product(ah, bl) + product(al, bh))


class Sizes:
    pass


def up8(count):
    return -(-count // 8) * 8


def small_layout(sz):
    tiles = sz.cs // LANES
    sz.at_gain = 0
    sz.at_bc = up8(sz.d // LANES)
    sz.common = sz.at_bc + 2 * sz.state // LANES * 8
    sz.at_conv = sz.common
    sz.at_gate = sz.at_conv + tiles * 8
    sz.at_head = sz.at_gate + up8(tiles)
    sz.small_rows = sz.at_head + up8(3 + tiles)


def device_of(sz, g, t):
    return (lax.div(g, sz.z) * sz.fi + lax.div(t, 2), lax.rem(g, sz.z) * 2 + lax.rem(t, 2))


def index_of(sz, g, t):
    f, p = device_of(sz, g, t)
    return f * sz.p + p


class Place:
    def __init__(self, sz):
        f, p = lax.axis_index("fsdp"), lax.axis_index("dp")
        fi, z = lax.rem(f, sz.fi), lax.div(p, 2)
        self.c = lax.rem(p, 2)
        self.g = lax.div(f, sz.fi) * sz.z + z
        self.t = fi * 2 + self.c
        self.i = f * sz.p + p
        u, v = lax.rem(fi, 2), lax.div(fi, 2)
        across, along = v * 2 + 1 - u, (1 - v) * 2 + u
        self.fi = fi
        self.fa = across * (1 - self.c) + along * self.c
        self.fb = along * (1 - self.c) + across * self.c
        self.fd = sz.fi - 1 - fi
        self.other = 1 - self.c


def remote(sz, src, dst, send, recv, g, t):
    return pltpu.make_async_remote_copy(
        src_ref=src, dst_ref=dst, send_sem=send, recv_sem=recv, device_id=device_of(sz, g, t), device_id_type=pl.DeviceIdType.MESH
    )


def landed(ref, sem):
    pltpu.make_async_copy(ref, ref, sem).wait()


def greet_all(sz, me):
    barrier = pltpu.get_barrier_semaphore()

    @pl.loop(1, sz.n)
    def _(step):
        there = lax.rem(me.i + step, sz.n)
        pl.semaphore_signal(barrier, inc=1, device_id=(lax.div(there, sz.p), lax.rem(there, sz.p)), device_id_type=pl.DeviceIdType.MESH)

    pl.semaphore_wait(barrier, sz.n - 1)


def greet_near(sz, me):
    barrier = pltpu.get_barrier_semaphore()
    near = [(me.g, lax.rem(me.t + step, sz.t)) for step in range(1, sz.t)] + [(lax.rem(me.g + step, sz.g), me.t) for step in range(1, sz.g)]
    for g, t in near:
        pl.semaphore_signal(barrier, inc=1, device_id=device_of(sz, g, t), device_id_type=pl.DeviceIdType.MESH)
    pl.semaphore_wait(barrier, len(near))


class PlaneGather:
    def __init__(self, sz, me, parts, own, views, gauge, bulk, send, recv):
        self.sz, self.me, self.parts, self.own, self.views, self.gauge, self.bulk, self.send, self.recv = sz, me, parts, own, views, gauge, bulk, send, recv
        self.a, self.b, self.d = me.fa * 2 + me.c, me.fb * 2 + me.c, me.fd * 2 + me.c
        self.pair = me.fi * 2 + me.other

    def push(self, kind, part):
        slot = (self.me.t, self.me.t, self.me.t, self.a, self.a, self.b, self.d)[kind]
        target = (self.a, self.b, self.pair, self.b, self.pair, self.pair, self.pair)[kind]
        views = self.views(slot, part)
        for src, dst in zip(self.own(part) if kind < 3 else views, views):
            remote(self.sz, src, dst, self.send.at[0], self.recv.at[slot, part], self.me.g, target).start()

    def arrived(self, slot, part):
        landed(self.gauge, self.recv.at[slot, part])

    def start(self, part):
        for kind in range(3):
            self.push(kind, part)

    def relay(self, part):
        self.arrived(self.a, part)
        self.push(3, part)
        self.push(4, part)
        self.arrived(self.b, part)
        self.push(5, part)

    def relay_far(self, part):
        self.arrived(self.d, part)
        self.push(6, part)

    def sent(self):
        landed(self.bulk, self.send.at[0])


def t_differs(sz, me, k):
    return me.t * sz.g + k != me.i


def select_rows(sz, packed, channel, per):
    n = packed.shape[0]
    wide = channel.shape[1]
    owner = jnp.floor((channel + 0.5) * (1.0 / per))
    place = channel - owner * per
    pick = (iota((LANES, wide), 0).astype(F32) == place).astype(BF16)
    spread = nn(packed.reshape(n * 8, LANES).astype(BF16), pick).reshape(n, 8, wide)
    over = lambda v, by: jnp.floor((v + 0.5) * (1.0 / by))
    spot = iota((n, 8, LANES), 0).astype(F32)
    rank = over(spot, sz.g)
    plane = spot - sz.g * rank
    fi, fo = over(rank, 2), over(plane, sz.z)
    device = ((fo * sz.fi + fi) * sz.z + plane - sz.z * fo) * 2 + rank - 2 * fi
    total = jnp.zeros((8, wide), F32)
    parts = []
    for at in range(0, wide, LANES):
        hit = device == owner[None, :, at : at + LANES]
        parts.append(jnp.sum(jnp.where(hit, spread[:, :, at : at + LANES], 0.0), axis=0))
    return jnp.concatenate(parts, axis=1)


def lanes_of(wide):
    return iota((1, wide), 1).astype(F32)


def slot_of(me, k):
    flip = lambda bit, other: bit + other - 2 * bit * other
    v, u, c = lax.div(me.t, 4), lax.rem(lax.div(me.t, 2), 2), me.c
    kv, ku, kc = lax.div(k, 4), lax.rem(lax.div(k, 2), 2), lax.rem(k, 2)
    return (flip(v, kv) * 2 + flip(u, ku)) * 2 + flip(c, kc)


def ends_of(row, count):
    ends, total = [], jnp.zeros((1, 1), F32)
    for slot in range(count):
        total = total + row[:, slot : slot + 1]
        ends.append(total)
    return ends


def segments(pos, ends):
    total = jnp.zeros(pos.shape, F32)
    for end in ends:
        total = total + (pos >= end).astype(F32)
    return total


def masks(rows, ends, taps):
    pos = iota((rows, LANES), 0).astype(F32)
    seg = segments(pos, ends)
    keeps = []
    for off in range(1, taps):
        same = (segments(pos - off, ends) == seg) & (pos >= off)
        keeps.append(same.astype(F32))
    valid = (seg < len(ends)).astype(F32)
    seg_row = segments(lanes_of(rows), ends)
    same = jnp.concatenate([(seg == seg_row[:, at : at + LANES]) for at in range(0, rows, LANES)], axis=1)
    return keeps, valid, same


def triangle(rows):
    return iota((rows, rows), 0) >= iota((rows, rows), 1)


def front_kernel(sz, x, go, win, tail, wout, norm, cw, cb, gate, lens, decay, bias, skip,
                 NRM, GO, PX, PT, PZ, Y, GM, WX, WZ, WT, WO, Q, PAR, HEAD, TILE,
                 xv, nv, gov, px, pt, pz, yv, gmv, wxv, wzv, wtv, wov, pack, smv, par, head, qv, qr, tilev,
                 xsend, xrecv, gsend, grecv, wsend, wrecv, axsend, axrecv, azsend, azrecv, zxsend, zxrecv, zzsend, zzrecv,
                 tsend, trecv, osend, orecv, ssend, srecv, qsend, qrecv, lsem, esem, wsem):
    me = Place(sz)
    cs, rows, G, T, st, taps = sz.cs, sz.rows, sz.g, sz.t, sz.state, sz.taps
    tiles = cs // LANES
    pack[...] = jnp.zeros(pack.shape, F32)
    dn, cn, kn = norm.shape[1], cb.shape[1], gate.shape[1]
    pack[0:taps, 0:cn] = cw[...].astype(F32)
    pack[taps : taps + 1, 0:cn] = cb[...].astype(F32)
    pack[taps + 1 : taps + 2, 0:kn] = gate[...].astype(F32)
    pack[taps + 2 : taps + 3, 0:dn] = norm[...].astype(F32)
    pack[taps + 3 : taps + 4, 0 : sz.seqs] = lens[...].astype(F32)
    (greet_near if sz.aligned else greet_all)(sz, me)

    tile_of = lambda g, t: smv.at[t * G + g]

    def pack_line(step):
        return remote(sz, pack, tile_of(me.g, me.t), ssend.at[0], srecv.at[0], lax.rem(me.g + step, G), me.t)

    def pack_plane(step):
        mine = smv.at[pl.ds(me.t * G, G)]
        return remote(sz, mine, mine, ssend.at[1], srecv.at[1], me.g, lax.rem(me.t + step, T))

    def columns(half, t):
        return win.at[:, pl.ds(pl.multiple_of(half * sz.di + t * cs, LANES), cs)]

    def exchange(half, step):
        there = lax.rem(me.t + step, T)
        wv, send, recv = ((wzv, azsend, azrecv), (wxv, axsend, axrecv))[half]
        return remote(sz, columns(half, there), wv.at[me.i], send.at[0], recv.at[0], me.g, there)

    def tail_copy(step):
        there = lax.rem(me.g + step, G)
        return remote(sz, tail, wtv.at[me.i], tsend.at[0], trecv.at[0], there, me.t)

    for step in range(1, G):
        tail_copy(step).start()
        pack_line(step).start()
    for step in range(1, T):
        exchange(1, step).start()

    part = lambda ref, k: ref.at[pl.ds(k * sz.part_rows, sz.part_rows)]
    gx = PlaneGather(sz, me, sz.parts, lambda k: [part(x, k)], lambda s, k: [part(xv.at[s], k)], part(xv.at[0], 0), xv.at[pl.ds(0, T - 1)], xsend, xrecv)
    gg = PlaneGather(sz, me, sz.parts, lambda k: [part(go, k)], lambda s, k: [part(gov.at[s], k)], part(gov.at[0], 0), gov.at[pl.ds(0, T - 1)], gsend, grecv)
    tails_of = lambda s, k: [wtv.at[index_of(sz, jnp.int32(g), s)] for g in range(G)]
    gt = PlaneGather(sz, me, 1, lambda k: tails_of(me.t, k), tails_of, wtv.at[pl.ds(0, G)], wtv.at[pl.ds(0, (T - 1) * G)], wsend, wrecv)

    owner_t, piece = lax.div(me.i, G), lax.rem(me.i, G)

    def out_copy(g):
        return remote(sz, wout, wov.at[piece], osend.at[2, g], orecv.at[piece], g, owner_t)

    def out_targets():
        planes = (me.g,) if sz.aligned else tuple(range(G))
        for g in planes:
            elsewhere = (owner_t != me.t) | (me.g != g)
            yield elsewhere, (lambda g=g: out_copy(jnp.int32(0) + g))

    def out_line(step, half, up):
        plane = me.g - step if up else me.g + step
        first = 2 * plane - me.c * sz.z
        have = (plane >= 0 if up else plane < G) & (first >= 0) & (first < G)
        more = (me.g < G - 1) if up else (me.g > 0)
        k = jnp.clip(first, 0, G - 2) + half
        nxt = jnp.clip(me.g + 1 if up else me.g - 1, 0, G - 1)
        copy = lambda: remote(sz, wov.at[k], wov.at[k], osend.at[int(up), k], orecv.at[k], nxt, me.t)
        return have, more, k, copy

    def out_advance(step):
        for half in range(2):
            if step == 0:
                have, _, k, _ = out_line(0, half, True)

                @pl.when(have & t_differs(sz, me, k))
                def _(k=k):
                    landed(wov.at[k], orecv.at[k])
            for up in (True, False):
                have, more, k, copy = out_line(step, half, up)
                if step > 0:
                    @pl.when(have)
                    def _(k=k):
                        landed(wov.at[k], orecv.at[k])
                if step < G - 1:
                    @pl.when(have & more)
                    def _(copy=copy):
                        copy().start()

    def out_steps(*steps):
        if sz.aligned:
            for step in steps:
                out_advance(step)

    for elsewhere, copy in out_targets():
        @pl.when(elsewhere)
        def _(copy=copy):
            copy().start()

    ins = [
        pltpu.make_async_copy(columns(1, me.t), wxv.at[me.i], lsem.at[0]),
        pltpu.make_async_copy(columns(0, me.t), wzv.at[me.i], lsem.at[1]),
        pltpu.make_async_copy(tail, wtv.at[me.i], lsem.at[2]),
        pltpu.make_async_copy(pack, tile_of(me.g, me.t), lsem.at[3]),
        pltpu.make_async_copy(x, xv.at[me.t], lsem.at[4]),
        pltpu.make_async_copy(go, gov.at[me.t], lsem.at[5]),
    ]
    for copy in ins:
        copy.start()
    for copy in ins:
        copy.wait()

    @pl.when(owner_t == me.t)
    def _():
        copy = pltpu.make_async_copy(wout, wov.at[piece], lsem.at[6])
        copy.start()
        copy.wait()

    head[...] = jnp.zeros(head.shape, F32)
    head[0:1, 0 : sz.heads] = bias[...]
    head[1:2, 0 : sz.heads] = decay[...]
    head[2:3, 0 : sz.heads] = skip[...]
    lead = lax.rem(LANES - sz.nh * me.t, LANES)
    head[...] = pltpu.roll(head[...], lead, 1)

    landed(smv.at[pl.ds(0, G - 1)], srecv.at[0])
    landed(wtv.at[pl.ds(0, G - 1)], trecv.at[0])
    for step in range(1, T):
        pack_plane(step).start()
    gt.start(0)
    gx.start(0)

    def arrive(half):
        wv, _, recv = ((wzv, azsend, azrecv), (wxv, axsend, axrecv))[half]
        landed(wv.at[pl.ds(0, T - 1)], recv.at[0])

    def line(half, step, up):
        wv, send, recv = ((wzv, zzsend, zzrecv), (wxv, zxsend, zxrecv))[half]
        plane = me.g - step if up else me.g + step
        have = (plane >= 0) if up else (plane < G)
        more = (me.g < G - 1) if up else (me.g > 0)
        plane = jnp.clip(plane, 0, G - 1)
        nxt = jnp.clip(me.g + 1 if up else me.g - 1, 0, G - 1)

        def push():
            for fi in range(sz.fi):
                block = wv.at[pl.ds(index_of(sz, plane, jnp.int32(2 * fi)), 2)]
                remote(sz, block, block, send.at[int(up), plane], recv.at[plane], nxt, me.t).start()

        return have, more, plane, push, wv.at[pl.ds(0, T)], send, recv

    def advance(half, step):
        for up in (True, False):
            have, more, plane, push, gauge, _, recv = line(half, step, up)
            if step > 0:
                @pl.when(have)
                def _(gauge=gauge, recv=recv, plane=plane):
                    landed(gauge, recv.at[plane])
            if step < G - 1:
                pl.when(have & more)(push)

    arrive(1)
    advance(1, 0)
    gt.relay(0)
    for step in range(1, T):
        exchange(0, step).start()
    for p in range(1, sz.parts):
        gx.start(p)
    advance(1, 1)
    landed(smv.at[pl.ds(0, (T - 1) * G)], srecv.at[1])
    packed = smv[...]
    ch = lanes_of(cs + 2 * st)
    start_ch = (me.t * cs).astype(F32)
    ch = jnp.where(ch < cs, ch + start_ch, ch + (sz.di - cs))
    par[:, 0 : cs + 2 * st] = select_rows(sz, packed, ch, cn)
    picked = select_rows(sz, packed, lanes_of(cs) + start_ch, kn)
    par[taps + 1 : taps + 2, 0:cs] = picked[taps + 1 : taps + 2]
    gains = select_rows(sz, packed, lanes_of(sz.d), dn)
    par[taps + 2 : taps + 3, 0 : sz.d] = gains[taps + 2 : taps + 3]

    def normalize(k):
        slot = slot_of(me, k)
        xb = xv[slot].astype(F32)
        mean = jnp.mean(xb * xb, axis=1, keepdims=True)
        nv[slot] = (xb * lax.rsqrt(mean + EPS) * par[taps + 2 : taps + 3, 0 : sz.d]).astype(BF16)
        pltpu.make_async_copy(nv.at[slot], NRM.at[slot], esem.at[0]).start()

    def wait_pair(gather, k):
        slot = slot_of(me, k)
        for p in range(sz.parts):
            gather.arrived(slot, p)

    normalize(jnp.int32(0))
    wait_pair(gx, jnp.int32(1))
    normalize(jnp.int32(1))
    gx.relay(0)
    for step in range(2, G - 1):
        advance(1, step)
    arrive(0)
    advance(0, 0)
    gt.relay_far(0)
    advance(1, G - 1)
    for p in range(1, sz.parts):
        gx.relay(p)
    for p in range(sz.parts):
        gg.start(p)
    for fi in (me.fi, me.fa, me.fb, me.fd):
        gt.arrived(fi * 2 + me.other, 0)

    low = iota((rows, LANES), 1) < sz.hd
    tri = triangle(rows)
    half_rows = rows // 2

    def scan(k):
        slot = slot_of(me, k)

        @pl.when((k > 2) & (lax.rem(k, 2) == 1))
        def _():
            wait_pair(gx, k)

        @pl.when(k > 1)
        def _():
            normalize(k)

        keeps, _, same = masks(rows, ends_of(smv[slot * G + me.g, taps + 3 : taps + 4, :], sz.seqs), taps)
        nrm = nv[slot]
        pxv = nn(nrm, wxv[...].reshape(sz.d, cs))
        ptl = nn(nrm, wtv[...].reshape(sz.d, sz.tl))
        px[slot] = pxv
        pt[slot] = ptl
        pltpu.make_async_copy(px.at[slot], PX.at[slot], esem.at[1]).start()
        pltpu.make_async_copy(pt.at[slot], PT.at[slot], esem.at[2]).start()

        def act(u, at):
            return jax.nn.silu(conv_tile(u, par[0:taps, at : at + LANES], par[taps : taps + 1, at : at + LANES], keeps, taps))

        bm = act(ptl[:, 0:st], cs)
        cm = act(ptl[:, st : 2 * st], cs + st)
        raw = pltpu.roll(ptl[:, 2 * st : 2 * st + LANES], lead, 1)
        dt = softplus(raw + head[0:1, :])
        rate = -jnp.exp(head[1:2, :])
        log_decay = jnp.dot(tri.astype(F32), dt * rate, precision=EXACT, preferred_element_type=F32)
        log_t = log_decay.T
        drop = jnp.where(same & tri, 0.0, -jnp.inf)
        inner = three(nt, cm, bm)
        for j in range(tiles):
            at = j * LANES
            xa = act(pxv[:, at : at + LANES], at)
            dt2 = jnp.where(low, dt[:, 2 * j : 2 * j + 1], dt[:, 2 * j + 1 : 2 * j + 2])
            xd = xa * dt2
            tops, bottoms = [], []
            for e in range(2):
                h = 2 * j + e
                mine = low if e == 0 else jnp.logical_not(low)
                xm = jnp.where(mine, xd, 0.0).astype(BF16)
                for r, wide, into in ((slice(0, half_rows), half_rows, tops), (slice(half_rows, rows), rows, bottoms)):
                    spread = log_decay[r, h : h + 1] - log_t[h : h + 1, 0:wide]
                    f = (jnp.exp(spread + drop[r, 0:wide]) * inner[r, 0:wide]).astype(BF16)
                    into.append(nn(f, xm[0:wide]))
            y = jnp.concatenate([tops[0] + tops[1], bottoms[0] + bottoms[1]], axis=0)
            skip2 = jnp.where(low[0:1], head[2:3, 2 * j : 2 * j + 1], head[2:3, 2 * j + 1 : 2 * j + 2])
            yv[slot, :, at : at + LANES] = y + xa * skip2
        pltpu.make_async_copy(yv.at[slot], Y.at[slot], esem.at[3]).start()

    def between(k, *steps):
        @pl.when(k)
        def _():
            for step in steps:
                step()

    whole = [(wxv, WX), (wtv, WT), (par, PAR), (head, HEAD), (wzv, WZ), (wov, WO), (tilev, TILE)]

    def save(*picked):
        for k in picked:
            pltpu.make_async_copy(*whole[k], wsem.at[k]).start()

    save(0, 1, 2, 3)

    @pl.loop(0, T)
    def _(k):
        between(k == 1, lambda: advance(0, 1), lambda: out_steps(0))
        between(k == 2, lambda: gx.relay_far(0))
        between(k == 4, lambda: [gx.relay_far(p) for p in range(1, sz.parts)], lambda: [advance(0, step) for step in range(2, G - 1)])
        between(k == 5, lambda: gg.relay(0))
        between(k == 6, lambda: [gg.relay(p) for p in range(1, sz.parts)], lambda: out_steps(1))
        between(k == 7, lambda: advance(0, G - 1))
        scan(k)

    out_steps(*range(2, G - 1))
    save(4)

    @pl.loop(0, T)
    def _(k):
        slot = slot_of(me, k)
        pz[slot] = nn(nv[slot], wzv[...].reshape(sz.d, cs))
        pltpu.make_async_copy(pz.at[slot], PZ.at[slot], esem.at[4]).start()

    for p in range(sz.parts):
        gg.relay_far(p)
    out_steps(G - 1)
    if not sz.aligned:
        for k in range(G):
            @pl.when(t_differs(sz, me, k))
            def _(k=k):
                landed(wov.at[k], orecv.at[k])

    save(5)

    @pl.loop(0, T)
    def _(k):
        slot = slot_of(me, k)

        between(lax.rem(k, 2) == 1, lambda: wait_pair(gg, k))
        pos = iota((rows, LANES), 0).astype(F32)
        seg = segments(pos, ends_of(smv[slot * G + me.g, taps + 3 : taps + 4, :], sz.seqs))
        valid = (seg < sz.seqs).astype(F32)
        tilev[slot] = smv[slot * G + me.g]
        zt = pz[slot]
        gm = nt(gov[slot], wov[...].reshape(cs, sz.d))
        gmv[slot] = gm
        pltpu.make_async_copy(gmv.at[slot], GM.at[slot], esem.at[5]).start()
        pltpu.make_async_copy(gov.at[slot], GO.at[slot], esem.at[6]).start()
        q1 = jnp.zeros((rows, LANES), F32)
        q2 = jnp.zeros((rows, LANES), F32)
        for j in range(tiles):
            tile = slice(j * LANES, (j + 1) * LANES)
            gated = yv[slot, :, tile] * (zt[:, tile] * jax.nn.sigmoid(zt[:, tile]))
            q1 = q1 + gated * gated
            q2 = q2 + gated * gm[:, tile] * par[taps + 1 : taps + 2, tile]
        q2 = q2 * valid
        lane = iota((rows, LANES), 1)
        stats = jnp.where(lane == 0, jnp.sum(q1, axis=1, keepdims=True), jnp.sum(q2, axis=1, keepdims=True)).T
        qv[pl.ds(slot, 1), :] = stats[0:1, :]
        qv[pl.ds(T + slot, 1), :] = stats[1:2, :]

    save(6)

    def q_copy(step):
        return remote(sz, qv, qr.at[me.t], qsend.at[0], qrecv.at[0], me.g, lax.rem(me.t + step, T))

    for step in range(1, T):
        q_copy(step).start()

    landed(qr.at[pl.ds(0, T - 1)], qrecv.at[0])
    total = qv[...]
    for step in range(1, T):
        total = total + qr[lax.rem(me.t + step, T)]
    Q[...] = total

    landed(qr.at[pl.ds(0, T - 1)], qsend.at[0])
    landed(wxv.at[pl.ds(0, T - 1)], axsend.at[0])
    landed(wzv.at[pl.ds(0, T - 1)], azsend.at[0])
    landed(wtv.at[pl.ds(0, G - 1)], tsend.at[0])
    landed(smv.at[pl.ds(0, G - 1)], ssend.at[0])
    landed(smv.at[pl.ds(0, (T - 1) * G)], ssend.at[1])
    for gather in (gx, gg, gt):
        gather.sent()
    for elsewhere, copy in out_targets():
        @pl.when(elsewhere)
        def _(copy=copy):
            copy().wait_send()
    if sz.aligned:
        for step in range(G - 1):
            for half in range(2):
                for up in (True, False):
                    have, more, _, copy = out_line(step, half, up)

                    @pl.when(have & more)
                    def _(copy=copy):
                        copy().wait_send()
    for half in range(2):
        for step in range(G - 1):
            for up in (True, False):
                have, more, plane, _, gauge, send, _ = line(half, step, up)

                @pl.when(have & more)
                def _(gauge=gauge, send=send, plane=plane, up=up):
                    landed(gauge, send.at[int(up), plane])
    for k, (src, dst) in enumerate(whole):
        pltpu.make_async_copy(src, dst, wsem.at[k]).wait()
    for a, (src, dst) in enumerate([(nv, NRM), (px, PX), (pt, PT), (yv, Y), (pz, PZ), (gmv, GM), (gov, GO)]):
        pltpu.make_async_copy(src, dst, esem.at[a]).wait()


def run_front(sz, x, go, win, tail, wout, norm, cw, cb, gate, lens, decay, bias, skip):
    n, g, t, rows, d, cs, tl, parts, fi = sz.n, sz.g, sz.t, sz.rows, sz.d, sz.cs, sz.tl, sz.parts, sz.fi
    dn, on = win.shape[0], wout.shape[0]
    any_ = pl.BlockSpec(memory_space=pl.ANY)
    vmem = pl.BlockSpec(memory_space=pltpu.VMEM)
    dma = pltpu.SemaphoreType.DMA
    shapes = dict(
        nrm=((t, rows, d), BF16), go=((t, rows, d), BF16), px=((t, rows, cs), F32), pt=((t, rows, tl), F32), pz=((t, rows, cs), F32),
        y=((t, rows, cs), F32), gm=((t, rows, cs), F32), wx=((n, dn, cs), BF16), wz=((n, dn, cs), BF16), wt=((n, dn, tl), BF16),
        wo=((g, on, d), BF16), q=((2 * t, rows), F32), par=((8, d), F32), head=((8, LANES), F32), tile=((t, 8, LANES), F32),
    )
    out = lambda *names: [jax.ShapeDtypeStruct(*shapes[name]) for name in names]
    scr = lambda *names: [pltpu.VMEM(*shapes[name]) for name in names]
    return pl.pallas_call(
        functools.partial(front_kernel, sz),
        in_specs=[any_] * 5 + [vmem] * 8,
        out_specs=[any_] * 11 + [vmem] + [any_] * 3,
        out_shape=out("nrm", "go", "px", "pt", "pz", "y", "gm", "wx", "wz", "wt", "wo", "q", "par", "head", "tile"),
        scratch_shapes=scr("nrm", "nrm", "go", "px", "pt", "pz", "y", "gm", "wx", "wz", "wt", "wo")
        + [pltpu.VMEM((8, LANES), F32), pltpu.VMEM((n, 8, LANES), F32)]
        + scr("par", "head", "q")
        + [pltpu.VMEM((t, 2 * t, rows), F32), pltpu.VMEM((t, 8, LANES), F32)]
        + [dma((1,)), dma((t, parts)), dma((1,)), dma((t, parts)), dma((1,)), dma((t, 1)), dma((1,)), dma((1,)), dma((1,)), dma((1,)),
           dma((2, g)), dma((g,)), dma((2, g)), dma((g,)), dma((1,)), dma((1,)), dma((3, g)), dma((g,)), dma((2,)), dma((2,)),
           dma((1,)), dma((1,)), dma((7,)), dma((7,)), dma((7,))],
        compiler_params=pltpu.CompilerParams(collective_id=0, has_side_effects=True, vmem_limit_bytes=63 << 20),
        name="front",
    )(x, go, win, tail, wout, norm, cw, cb, gate, lens, decay, bias, skip)


def bwd_kernel(sz, nrm_ref, px_ref, pt_ref, pz_ref, y_ref, gm_ref, q_ref, wx_ref, wz_ref, wt_ref, wo_ref, par_ref, head_ref, tile_ref,
               mix_ref, hid_ref, dz_ref, dx_ref, dt_ref, gn_ref, small_ref):
    b = pl.program_id(0)
    me = Place(sz)
    rows, cs, st, taps = sz.rows, sz.cs, sz.state, sz.taps
    tiles = cs // LANES
    keeps, valid, same = masks(rows, ends_of(tile_ref[0, taps + 3 : taps + 4, :], sz.seqs), taps)
    at_gate, at_conv, at_head, at_gain = sz.at_gate, sz.at_conv, sz.at_head, sz.at_gain
    lead = lax.rem(LANES - sz.nh * me.t, LANES)

    @pl.when(b == 0)
    def _():
        small_ref[...] = jnp.zeros(small_ref.shape, F32)

    def colsum(v):
        return jnp.sum(v, axis=0, keepdims=True)

    def conv_pre(u, at):
        return conv_tile(u, par_ref[0:taps, at : at + LANES], par_ref[taps : taps + 1, at : at + LANES], keeps, taps)

    def silu_pair(v):
        s = jax.nn.sigmoid(v)
        return v * s, s * (1.0 + v * (1.0 - s))

    def conv_back(u, dact, dsilu, at):
        dpre = dact * dsilu
        tile = at // LANES
        row = at_conv + tile * 8 if tile < tiles else sz.at_bc + (tile - tiles) * 8
        back = dpre * par_ref[taps - 1 : taps, at : at + LANES]
        small_ref[row + taps - 1 : row + taps, :] += colsum(dpre * u)
        small_ref[row + taps : row + taps + 1, :] += colsum(dpre)
        for off in range(1, taps):
            kept = dpre * keeps[off - 1]
            tap = taps - 1 - off
            small_ref[row + tap : row + tap + 1, :] += colsum(kept * pltpu.roll(u, off, 0))
            back = back + pltpu.roll(kept, rows - off, 0) * par_ref[tap : tap + 1, at : at + LANES]
        return back

    ub, uc = pt_ref[0, :, 0:st], pt_ref[0, :, st : 2 * st]
    bm, bslope = silu_pair(conv_pre(ub, cs))
    cm, cslope = silu_pair(conv_pre(uc, cs + st))
    raw = pltpu.roll(pt_ref[0, :, 2 * st : 2 * st + LANES], lead, 1) + head_ref[0:1, :]
    dt = softplus(raw)
    rate = -jnp.exp(head_ref[1:2, :])
    log_decay = jnp.dot(triangle(rows).astype(F32), dt * rate, precision=EXACT, preferred_element_type=F32)
    log_t = log_decay.T
    upper = iota((rows, rows), 1) >= iota((rows, rows), 0)
    drop = jnp.where(same & upper, 0.0, -jnp.inf)
    inner_t = three(nt, bm, cm)
    low = iota((rows, LANES), 1) < sz.hd
    lane = iota((rows, LANES), 1)
    q1 = jnp.broadcast_to(q_ref[pl.ds(b, 1), :], (LANES, rows)).T
    q2 = jnp.broadcast_to(q_ref[pl.ds(sz.t + b, 1), :], (LANES, rows)).T
    scale = lax.rsqrt(q1 / sz.di + EPS)
    pull = scale * scale * scale * q2 / sz.di

    dcb = jnp.zeros((rows, rows), F32)
    ddt = jnp.zeros((rows, LANES), F32)
    cols = jnp.zeros((rows, LANES), F32)
    rowsums = jnp.zeros((LANES, rows), F32)
    lane_row = iota((LANES, rows), 0)
    for j in range(tiles):
        at = j * LANES
        tile = slice(at, at + LANES)
        zt = pz_ref[0, :, tile]
        y = y_ref[0, :, tile]
        gm = gm_ref[0, :, tile] * valid
        gate = par_ref[taps + 1 : taps + 2, tile]
        sz_, zslope = silu_pair(zt)
        gated = y * sz_
        unit = gated * scale
        mix_ref[0, :, tile] = (unit * gate * valid).astype(BF16)
        small_ref[at_gate + j : at_gate + j + 1, :] += colsum(gm * unit)
        dgated = scale * gm * gate - gated * pull
        dz_ref[0, :, tile] = (dgated * y * zslope).astype(BF16)
        dy = dgated * sz_
        ux = px_ref[0, :, tile]
        xa, xslope = silu_pair(conv_pre(ux, at))
        small_ref[at_head + 3 + j : at_head + 4 + j, :] += colsum(dy * xa)
        dt2 = jnp.where(low, dt[:, 2 * j : 2 * j + 1], dt[:, 2 * j + 1 : 2 * j + 2])
        xd = xa * dt2
        dxd = []
        for e in range(2):
            h = 2 * j + e
            mine = low if e == 0 else jnp.logical_not(low)
            decay = jnp.exp(log_t[h : h + 1, :] - log_decay[:, h : h + 1] + drop)
            df = three(nt, jnp.where(mine, xd, 0.0), dy) * decay
            dcb = dcb + df
            p = df * inner_t
            cols = jnp.where(lane == h, jnp.sum(p, axis=1, keepdims=True), cols)
            rowsums = jnp.where(lane_row == h, colsum(p), rowsums)
            dxd.append(nn((decay * inner_t).astype(BF16), jnp.where(mine, dy, 0.0).astype(BF16)))
        dxd = dxd[0] + dxd[1]
        both = dxd * xa
        ddt = jnp.where(lane == 2 * j, jnp.sum(jnp.where(low, both, 0.0), axis=1, keepdims=True), ddt)
        ddt = jnp.where(lane == 2 * j + 1, jnp.sum(jnp.where(low, 0.0, both), axis=1, keepdims=True), ddt)
        skip2 = jnp.where(low[0:1], head_ref[2:3, 2 * j : 2 * j + 1], head_ref[2:3, 2 * j + 1 : 2 * j + 2])
        dx = dxd * dt2 + dy * skip2
        dx_ref[0, :, tile] = conv_back(ux, dx, xslope, at).astype(BF16)

    ga = jnp.dot(upper.astype(F32), rowsums.T - cols, precision=EXACT, preferred_element_type=F32)
    ddt = ddt + ga * rate
    small_ref[at_head : at_head + 1, :] += rate * colsum(ga * dt)
    draw = jnp.where(lane < sz.nh, ddt * jax.nn.sigmoid(raw), 0.0)
    small_ref[at_head + 1 : at_head + 2, :] += colsum(draw)
    dt_ref[0, :, 2 * st : 2 * st + LANES] = pltpu.roll(draw, sz.nh * me.t, 1).astype(BF16)
    dcb = dcb.astype(BF16)
    db = nn(dcb, cm.astype(BF16))
    dc = tn(dcb, bm.astype(BF16))
    dt_ref[0, :, 0:st] = conv_back(ub, db, bslope, cs).astype(BF16)
    dt_ref[0, :, st : 2 * st] = conv_back(uc, dc, cslope, cs + st).astype(BF16)

    hid_ref[0] = nn(mix_ref[0], wo_ref[...]).astype(BF16)
    gn = nt(dz_ref[0], wz_ref[...]) + nt(dx_ref[0], wx_ref[...]) + nt(dt_ref[0], wt_ref[...])
    gn_ref[0] = gn.astype(BF16)
    sums = colsum(gn * nrm_ref[0].astype(F32)) / par_ref[taps + 2 : taps + 3, 0 : sz.d]
    for k in range(sz.d // LANES):
        small_ref[at_gain + k : at_gain + k + 1, :] += sums[:, k * LANES : (k + 1) * LANES]


def run_bwd(sz, nrm, px, pt, pz, y, gm, q, wx, wz, wt, wo, par, head, tile):
    t, rows, d, cs, tl = sz.t, sz.rows, sz.d, sz.cs, sz.tl
    whole = lambda a: pl.BlockSpec(a.shape, lambda b: (0,) * a.ndim)
    block = lambda width: pl.BlockSpec((1, rows, width), lambda b: (b, 0, 0))
    return pl.pallas_call(
        functools.partial(bwd_kernel, sz),
        grid=(t,),
        in_specs=[block(d), block(cs), block(tl), block(cs), block(cs), block(cs), whole(q), whole(wx), whole(wz), whole(wt), whole(wo), whole(par),
                  whole(head), pl.BlockSpec((1, 8, LANES), lambda b: (b, 0, 0))],
        out_specs=[block(cs), block(d), block(cs), block(cs), block(tl), block(d), pl.BlockSpec((sz.small_rows, LANES), lambda b: (0, 0))],
        out_shape=[
            jax.ShapeDtypeStruct((t, rows, cs), BF16),
            jax.ShapeDtypeStruct((t, rows, d), BF16),
            jax.ShapeDtypeStruct((t, rows, cs), BF16),
            jax.ShapeDtypeStruct((t, rows, cs), BF16),
            jax.ShapeDtypeStruct((t, rows, tl), BF16),
            jax.ShapeDtypeStruct((t, rows, d), BF16),
            jax.ShapeDtypeStruct((sz.small_rows, LANES), F32),
        ],
        compiler_params=pltpu.CompilerParams(vmem_limit_bytes=60 << 20),
        name="bwd",
    )(nrm, px, pt, pz, y, gm, q, wx, wz, wt, wo, par, head, tile)


def reduce_kernel(sz, hp, gp, dwzx, dwtl, dwo, sm, hsum, gsum, gin, gtl, gout, gsm, hs, gs, r0h, r0g, r1h, r1g, r2h, r2g, rz, sz_, ro, rt, st, rtz, ra,
                  rs1, s1, rs2, p0send, p0recv, p1send, p1recv, p2send, p2recv, zsend, zrecv, asend, arecv, osend, orecv, tsend, trecv, uzsend, uzrecv,
                  s1send, s1recv, s2send, s2recv, usend, urecv):
    me = Place(sz)
    cs, rows, G, T, FI = sz.cs, sz.rows, sz.g, sz.t, sz.fi
    parts, pr = sz.rparts, sz.rows // sz.rparts
    greet_all(sz, me)

    def up32(v):
        return v.astype(F32)

    def s1_copy(step):
        return remote(sz, sm, rs1.at[me.g], s1send.at[step], s1recv.at[me.g], lax.rem(me.g + step, G), me.t)

    for step in range(1, G):
        s1_copy(step).start()

    arrays = [(hp, hs, r0h, r1h, r2h, hsum), (gp, gs, r0g, r1g, r2g, gsum)]
    order = (me.fa, me.fd, me.fb, me.fi)

    def p0_copy(k, which, part):
        src, _, r0 = arrays[k][:3]
        fi = order[which]
        rows_ = pl.ds(part * pr, pr)
        return remote(sz, src.at[fi * 2 + me.other, rows_], r0.at[fi, rows_], p0send.at[k, which, part], p0recv.at[k, fi, part], me.g, me.fi * 2 + me.other)

    for k in range(2):
        for which in range(4):
            for part in range(parts):
                p0_copy(k, which, part).start()

    def t_copy(step, g):
        there = lax.rem(me.t + step, T)
        return remote(sz, dwtl.at[index_of(sz, g, there)], rt.at[me.t, g], tsend.at[step, g], trecv.at[me.t, g], me.g, there)

    for step in range(1, T):
        for g in range(G):
            t_copy(step, g).start()

    def z_copy(step, fi):
        there = lax.rem(me.g + step, G)
        return remote(sz, dwzx.at[pl.ds(index_of(sz, there, jnp.int32(2 * fi)), 2)], rz.at[me.g, pl.ds(2 * fi, 2)], zsend.at[step, fi], zrecv.at[me.g, fi],
                      there, me.t)

    for step in range(1, G):
        for fi in range(FI):
            z_copy(step, fi).start()

    def o_copy(k):
        owner = me.t * G + k
        f, p = lax.div(owner, sz.p), lax.rem(owner, sz.p)
        return pltpu.make_async_remote_copy(src_ref=dwo.at[k], dst_ref=ro.at[me.g], send_sem=osend.at[k], recv_sem=orecv.at[me.g],
                                            device_id=(f, p), device_id_type=pl.DeviceIdType.MESH)

    for k in range(G):
        @pl.when(t_differs(sz, me, k))
        def _(k=k):
            o_copy(k).start()

    def p1_copy(k, which, part):
        _, s, _, r1 = arrays[k][:4]
        rows_ = pl.ds(part * pr, pr)
        return remote(sz, s.at[which, rows_], r1.at[which, rows_], p1send.at[k, which, part], p1recv.at[k, which, part], me.g, me.fa * 2 + me.c)

    def p2_copy(k, part):
        _, s, _, _, r2 = arrays[k][:5]
        rows_ = pl.ds(part * pr, pr)
        return remote(sz, s.at[2, rows_], r2.at[rows_], p2send.at[k, part], p2recv.at[k, part], me.g, me.fb * 2 + me.c)

    for k in range(2):
        src, s, r0, r1, r2, out = arrays[k]
        for which in range(4):
            fi = order[which]
            for part in range(parts):
                rows_ = pl.ds(part * pr, pr)
                landed(r0.at[fi, rows_], p0recv.at[k, fi, part])
                both = up32(src[fi * 2 + me.c, rows_]) + up32(r0[fi, rows_])
                if which < 2:
                    s[which, rows_] = both.astype(BF16)
                    p1_copy(k, which, part).start()
                elif which == 2:
                    s[2, rows_] = both.astype(BF16)
                else:
                    out[rows_] = both

    for step in range(1, T):
        for g in range(G):
            there = lax.rem(me.t + step, T)
            landed(rt.at[there, g], trecv.at[there, g])
    for g in range(G):
        total = up32(dwtl[index_of(sz, g, me.t)])
        for step in range(1, T):
            total = total + up32(rt[lax.rem(me.t + step, T), g])
        st[g] = total.astype(BF16)

    def uz_copy(step):
        there = lax.rem(me.g + step, G)
        return remote(sz, st.at[there], rtz.at[me.g], uzsend.at[step], uzrecv.at[me.g], there, me.t)

    for step in range(1, G):
        uz_copy(step).start()

    total = sm[...]
    for step in range(1, G):
        there = lax.rem(me.g + step, G)
        landed(rs1.at[there], s1recv.at[there])
        total = total + rs1[there]
    s1[...] = total
    rs2[me.t] = total

    def s2_copy(step):
        return remote(sz, s1, rs2.at[me.t], s2send.at[step], s2recv.at[me.t], me.g, lax.rem(me.t + step, T))

    for step in range(1, T):
        s2_copy(step).start()

    for k in range(2):
        src, s, r0, r1, r2, out = arrays[k]
        for part in range(parts):
            rows_ = pl.ds(part * pr, pr)
            landed(r1.at[1, rows_], p1recv.at[k, 1, part])
            s[2, rows_] = (up32(s[2, rows_]) + up32(r1[1, rows_])).astype(BF16)
            p2_copy(k, part).start()

    for fi in range(FI):
        for step in range(1, G):
            there = lax.rem(me.g + step, G)
            landed(rz.at[there, pl.ds(2 * fi, 2)], zrecv.at[there, fi])
        for c in range(2):
            total = up32(dwzx[index_of(sz, me.g, jnp.int32(2 * fi + c))])
            for step in range(1, G):
                total = total + up32(rz[lax.rem(me.g + step, G), 2 * fi + c])
            sz_[2 * fi + c] = total.astype(BF16)

    def a_copy(step):
        there = lax.rem(me.t + step, T)
        return remote(sz, sz_.at[there], ra.at[me.t], asend.at[step], arecv.at[me.t], me.g, there)

    for step in range(1, T):
        a_copy(step).start()
    ra[me.t] = sz_[me.t]

    total = jnp.zeros(gout.shape, F32)
    mine = lax.div(me.i, G) == me.t

    @pl.when(mine)
    def _():
        gout[...] = up32(dwo[lax.rem(me.i, G)])

    @pl.when(jnp.logical_not(mine))
    def _():
        gout[...] = jnp.zeros(gout.shape, F32)

    for g in range(G):
        other = jnp.logical_not(mine & (me.g == g))

        @pl.when(other)
        def _(g=g):
            landed(ro.at[g], orecv.at[g])
            gout[...] += up32(ro[g])

    total = up32(st[me.g])
    for step in range(1, G):
        there = lax.rem(me.g + step, G)
        landed(rtz.at[there], uzrecv.at[there])
        total = total + up32(rtz[there])
    gtl[...] = total

    for k in range(2):
        src, s, r0, r1, r2, out = arrays[k]
        for part in range(parts):
            rows_ = pl.ds(part * pr, pr)
            landed(r1.at[0, rows_], p1recv.at[k, 0, part])
            landed(r2.at[rows_], p2recv.at[k, part])
            out[rows_] = out[rows_] + up32(r1[0, rows_]) + up32(r2[rows_])

    for step in range(1, T):
        there = lax.rem(me.t + step, T)
        landed(ra.at[there], arecv.at[there])
        landed(rs2.at[there], s2recv.at[there])
    for t in range(T):
        gin[:, t * cs : (t + 1) * cs] = up32(ra[t, :, 0:cs])
        gin[:, sz.di + t * cs : sz.di + (t + 1) * cs] = up32(ra[t, :, cs:])
    total = rs2[0, 0 : sz.common]
    for t in range(1, T):
        total = total + rs2[t, 0 : sz.common]
    gsm[0 : sz.common] = total
    width = sz.small_rows - sz.common
    for t in range(T):
        gsm[sz.common + t * width : sz.common + (t + 1) * width] = rs2[t, sz.common :]

    for step in range(1, G):
        s1_copy(step).wait_send()
        uz_copy(step).wait_send()
        for fi in range(FI):
            z_copy(step, fi).wait_send()
    for step in range(1, T):
        s2_copy(step).wait_send()
        a_copy(step).wait_send()
        for g in range(G):
            t_copy(step, g).wait_send()
    for k in range(2):
        for part in range(parts):
            for which in range(4):
                p0_copy(k, which, part).wait_send()
            for which in range(2):
                p1_copy(k, which, part).wait_send()
            p2_copy(k, part).wait_send()
    for k in range(G):
        @pl.when(t_differs(sz, me, k))
        def _(k=k):
            o_copy(k).wait_send()


def run_reduce(sz, hp, gp, dwzx, dwtl, dwo, sm):
    n, g, t, rows, d, cs, tl, parts, fi = sz.n, sz.g, sz.t, sz.rows, sz.d, sz.cs, sz.tl, sz.rparts, sz.fi
    dn, on = dwzx.shape[1], dwo.shape[1]
    vmem = pl.BlockSpec(memory_space=pltpu.VMEM)
    dma = pltpu.SemaphoreType.DMA
    v = lambda *s: pltpu.VMEM(s, BF16)
    sr = sz.small_rows
    total_rows = sz.common + t * (sr - sz.common)
    return pl.pallas_call(
        functools.partial(reduce_kernel, sz),
        in_specs=[vmem] * 6,
        out_specs=[vmem] * 6,
        out_shape=[
            jax.ShapeDtypeStruct((rows, d), F32),
            jax.ShapeDtypeStruct((rows, d), F32),
            jax.ShapeDtypeStruct((dn, 2 * sz.di), F32),
            jax.ShapeDtypeStruct((dn, tl), F32),
            jax.ShapeDtypeStruct((on, d), F32),
            jax.ShapeDtypeStruct((total_rows, LANES), F32),
        ],
        scratch_shapes=[
            v(3, rows, d), v(3, rows, d), v(fi, rows, d), v(fi, rows, d), v(2, rows, d), v(2, rows, d), v(rows, d), v(rows, d),
            v(g, t, dn, 2 * cs), v(t, dn, 2 * cs), v(g, on, d), v(t, g, dn, tl), v(g, dn, tl), v(g, dn, tl), v(t, dn, 2 * cs),
            pltpu.VMEM((g, sr, LANES), F32), pltpu.VMEM((sr, LANES), F32), pltpu.VMEM((t, sr, LANES), F32),
            dma((2, 4, parts)), dma((2, fi, parts)), dma((2, 2, parts)), dma((2, 2, parts)), dma((2, parts)), dma((2, parts)),
            dma((g, fi)), dma((g, fi)), dma((t,)), dma((t,)), dma((g,)), dma((g,)), dma((t, g)), dma((t, g)), dma((g,)), dma((g,)),
            dma((g,)), dma((g,)), dma((t,)), dma((t,)), dma((1,)), dma((1,)),
        ],
        compiler_params=pltpu.CompilerParams(collective_id=2, has_side_effects=True, vmem_limit_bytes=63 << 20),
        name="reduce",
    )(hp, gp, dwzx, dwtl, dwo, sm)


def sizes(mesh, hidden, lengths, in_proj, conv_weight, gate_gain, decay_log):
    sz = Sizes()
    sz.f, sz.p = mesh.shape["fsdp"], mesh.shape["dp"]
    sz.n = sz.f * sz.p
    sz.rows, sz.d = hidden.shape
    sz.seqs = lengths.shape[1]
    sz.conv, sz.taps = conv_weight.shape[0] * sz.n, conv_weight.shape[1]
    sz.di = gate_gain.shape[0] * sz.n
    sz.state = (sz.conv - sz.di) // 2
    sz.heads = decay_log.shape[0]
    sz.hd = sz.di // sz.heads
    sz.fi = math.gcd(sz.f, sz.di // (2 * LANES))
    sz.t = 2 * sz.fi
    sz.z = sz.p // 2
    sz.g = sz.f // sz.fi * sz.z
    sz.aligned = sz.f == sz.fi
    sz.cs, sz.nh = sz.di // sz.t, sz.heads // sz.t
    sz.tail = in_proj.shape[1] - 2 * sz.di
    sz.tl = -(-sz.tail // LANES) * LANES
    sz.parts, sz.rparts = 2, 2
    sz.part_rows = sz.rows // sz.parts
    small_layout(sz)
    return sz


def local(mesh, hidden_in, lengths, norm_gain, in_proj, conv_weight, conv_bias, gate_gain, out_proj, decay_log, step_bias, skip_gain, grad_out):
    sz = sizes(mesh, hidden_in, lengths, in_proj, conv_weight, gate_gain, decay_log)
    n, t, cs, di = sz.n, sz.t, sz.cs, sz.di
    f, p = lax.axis_index("fsdp"), lax.axis_index("dp")
    index = f * sz.p + p
    dn, cn, kn = norm_gain.shape[0], conv_bias.shape[0], gate_gain.shape[0]

    tail = jnp.pad(in_proj[:, 2 * di :], ((0, 0), (0, sz.tl - sz.tail)))
    row = lambda a: a.reshape(1, -1)
    nrm, go_all, px, pt, pz, y, gm, wx, wz, wt, wo, q, par, head, tile = run_front(
        sz, hidden_in, grad_out, in_proj, tail, out_proj, row(norm_gain), conv_weight.T, row(conv_bias), row(gate_gain), lengths,
        row(decay_log), row(step_bias), row(skip_gain))
    wx, wz, wt, wo = wx.reshape(sz.d, cs), wz.reshape(sz.d, cs), wt.reshape(sz.d, sz.tl), wo.reshape(cs, sz.d)
    gain = par[sz.taps + 2 : sz.taps + 3]
    mix, hid, dz, dx, dtl, gn, small = run_bwd(sz, nrm, px, pt, pz, y, gm, q, wx, wz, wt, wo, par, head, tile)

    tall = lambda a: a.reshape(t * sz.rows, a.shape[2])
    dwzx = jnp.concatenate([tn(tall(nrm), tall(a)).astype(BF16) for a in (dz, dx)], axis=1).reshape(n, dn, 2 * cs)
    dwtl = tn(tall(nrm), tall(dtl)).astype(BF16).reshape(n, dn, sz.tl)
    dwo = tn(tall(mix), tall(go_all)).astype(BF16).reshape(sz.g, cs // sz.g, sz.d)
    hsum, gsum, gin, gtl, gout, gsm = run_reduce(sz, hid, gn, dwzx, dwtl, dwo, small)

    x = hidden_in.astype(F32)
    hidden_out = (x + hsum).astype(BF16)
    scale = lax.rsqrt(jnp.mean(x * x, axis=1, keepdims=True) + EPS)
    dxhat = gsum * gain
    inner = jnp.mean(dxhat * x, axis=1, keepdims=True)
    grad_in = grad_out.astype(F32) + scale * (dxhat - x * (scale * scale * inner))
    grad_in_proj = jnp.concatenate([gin, gtl[:, : sz.tail]], axis=1)

    own = lambda a, width: lax.dynamic_slice_in_dim(a, index * width, width)
    common, slices = gsm[: sz.common], gsm[sz.common :].reshape(t, -1, LANES)
    at = lambda place: place - sz.common
    grad_norm_gain = own(common[: sz.d // LANES].reshape(-1), dn)
    conv_x = slices[:, : at(sz.at_gate)].reshape(-1, 8, LANES)
    conv = jnp.concatenate([conv_x, common[sz.at_bc :].reshape(-1, 8, LANES)])
    conv = conv[:, : sz.taps + 1].transpose(0, 2, 1).reshape(sz.conv, sz.taps + 1)
    conv = own(conv, cn)
    tiles = cs // LANES
    grad_gate = own(slices[:, at(sz.at_gate) : at(sz.at_gate) + tiles].reshape(-1), kn)
    heads = slices[:, at(sz.at_head) :]
    grad_decay = heads[:, 0, : sz.nh].reshape(-1)
    grad_bias = heads[:, 1, : sz.nh].reshape(-1)
    grad_skip = jnp.sum(heads[:, 3 : 3 + tiles].reshape(sz.heads, sz.hd), axis=1)
    return (hidden_out, grad_in, grad_norm_gain, grad_in_proj, conv[:, : sz.taps], conv[:, sz.taps], grad_gate, gout, grad_decay, grad_bias, grad_skip)


def solution(mesh):
    both = ("fsdp", "dp")
    wide, flat, free = P(both, None), P(both), P()
    in_specs = (wide, wide, flat, wide, wide, flat, flat, wide, free, free, free, wide)
    out_specs = (wide, wide, flat, wide, wide, flat, flat, wide, free, free, free)
    return jax.shard_map(functools.partial(local, mesh), mesh=mesh, in_specs=in_specs, out_specs=out_specs, check_vma=False)
```

time: 311 us -> 276 us (0.89)
  Pallas kernels: 266 us -> 237 us
  other arithmetic: 10.2 us -> 5.18 us
    pallas_call x4 -> x2, Pallas kernels: 168 us -> 139 us  [the longest x1 88.4 us: run_front(): pl.pallas_call(functools.partial(front_kernel, sz), in_specs=[any_] * 5 +...]
    dot_general x3 -> x4, matrix products: 18.1 us -> 16.9 us  [tn(): lax.dot_general(a, b, (((0,), (0,)), ((), ())), preferred_element_type=F32)]
where the time goes in v2:
time: 276 us
  Pallas kernels  237 us (86%)
  matrix products  16.9 us (6%)
  local copies, waits for them, and re-layouts  15.8 us (6%)
  other arithmetic  5.18 us (2%)
    pallas_call x1, Pallas kernels, run_reduce(): pl.pallas_call(functools.partial(reduce_kernel, sz), in_specs=[vmem] * 6,...  98.4 us
    pallas_call x1, Pallas kernels, run_front(): pl.pallas_call(functools.partial(front_kernel, sz), in_specs=[any_] * 5 +...  88.4 us
    pallas_call x1, Pallas kernels, run_bwd(): pl.pallas_call(functools.partial(bwd_kernel, sz), grid=(t,), in_specs=[bl...  50.2 us
    dot_general x4, matrix products, tn(): lax.dot_general(a, b, (((0,), (0,)), ((), ())), preferred_element_type=F32)  16.9 us

profile of v2, /device:TPU:0, one launch (start us, length us, event | category | flops | bytes accessed | tf_op | source)
XLA Modules:
  0.0 275.8 jit_solution(661173588374694912)
XLA Ops:
  0.6 0.8 slice.49
  1.4 0.6 pad.4.tail
  2.0 88.4 %front.1 = (bf16[8,256,1536]{2,1,0:T(8,128)(2,1)}, bf16[8,256,1536]{2,1,0:T(8,128)(2,1)}, f32[8,256,384]{2,1,0:T(8,128)}, f32[8,256,384]{2,1,0:T(8,128)}, f32[8,...) custom-call(bf16[256,1536]{1,0:T(8,128)(2,1)} %x.3, ...), custom_call_target="tpu_custom_call" | custom-call | tf_op jit(solution)/shard_map/front/pallas_call | solution.py:631
  90.5 50.2 %bwd.1 = (bf16[8,256,384]{2,1,0:T(8,128)(2,1)}, bf16[8,256,1536]{2,1,0:T(8,128)(2,1)}, bf16[8,256,384]{2,1,0:T(8,128)(2,1)}, bf16[8,256,384]{2,1,0:T(8,128)(2,1)...) custom-call(bf16[8,256,1536]{2,1,0:T(8,128)(2,1)} %get-tuple-element.39.nrm_ref, ...), custom_call_target="tpu_custom_call" | custom-call | tf_op jit(solution)/shard_map/bwd/pallas_call | solution.py:772
  140.7 0.0 copy-start.1
  140.7 0.0 copy-start.10
  140.7 7.1 %fusion.3 = bf16[384,1536]{1,0:T(8,128)(2,1)} fusion(bf16[8,256,384]{2,1,0:T(8,128)(2,1)} %get-tuple-element.58, bf16[8,256,1536]{2,1,0:T(8,128)(2,1)} %get-tuple-element.59), kind=kOutput, calls=%fused_computation.7 | convolution fusion | flops 2416508928 | bytes 9043968 | tf_op jit(solution)/shard_map/dot_general | solution.py:27
  147.8 0.0 copy-done.1
  147.8 0.0 copy-done.10
  147.8 0.0 copy-start.9
  147.8 4.5 %fusion.2 = bf16[1536,384]{1,0:T(8,128)(2,1)} fusion(bf16[8,256,1536]{2,1,0:T(8,128)(2,1)S(1)} %copy-done.1, bf16[8,256,384]{2,1,0:T(8,128)(2,1)S(1)} %copy-done.10), kind=kOutput, calls=%fused_computation.6 | convolution fusion | flops 2416508928 | bytes 9043968 | tf_op jit(solution)/shard_map/dot_general | solution.py:27
  152.3 0.0 copy-done.9
  152.3 0.0 copy-start.8
  152.3 2.6 fusion
  155.0 0.0 copy-done.8
  155.0 2.6 fusion.1
  157.6 0.2 pad_maximum_fusion
  157.8 2.5 copy.34
  160.3 98.4 %reduce.11 = (f32[256,1536]{1,0:T(8,128)}, f32[256,1536]{1,0:T(8,128)}, f32[48,6144]{1,0:T(8,128)}, f32[48,384]{1,0:T(8,128)}, f32[96,1536]{1,0:T(8,128)}, /*index=5*/f32[352,128]{1,0:T(8,128)}) custom-call(bf16[8,256,1536]{2,1,0:T(8,128)(2,1)} %get-tuple-element.53.hp, bf16[8,256,1536]{2,1,0:T(8,128)(2,1)} %get-tuple-element.54.gp, ...), custom_call_target="tpu_custom_call" | custom-call | tf_op jit(solution)/shard_map/reduce/pallas_call | solution.py:1014
  258.7 0.0 copy-start.5
  258.7 1.0 slice.53
  259.7 0.0 copy-start.7
  259.8 0.6 copy-done.7
  260.4 0.0 copy-start
  260.4 0.0 copy-start.2
  260.4 0.8 slice_bitcast_fusion
  261.3 0.7 copy.45
  262.0 0.8 constant_dynamic-slice_fusion
  262.8 0.6 slice.57
  263.3 0.5 slice_bitcast_fusion.2
  263.9 0.0 copy-done.5
  263.9 2.0 pad_maximum_fusion.1
  265.9 0.0 copy-start.3
  265.9 0.0 copy-start.4
  265.9 1.0 slice_reduce_fusion
  266.8 0.0 copy-done
  266.9 0.0 copy-done.2
  266.9 0.4 fusion.5
  267.3 0.0 copy-done.3
  267.3 0.3 copy-done.4
  267.5 0.0 copy-start.6
  267.5 2.0 fusion.9
  269.5 0.8 fusion.11
  270.3 0.6 dynamic_slice.11
  270.9 0.1 reshape.127
  271.0 0.6 reduce_sum.29
  271.6 0.9 slice_reduce_fusion.1
  272.5 0.6 reshape_squeeze.6
  273.1 0.6 reshape_squeeze.7
  273.7 0.7 slice_bitcast_fusion.1
  274.4 0.6 dynamic_slice.9
  274.9 0.0 copy-done.6
  274.9 0.8 copy.47
  (6 shorter events, 0.1 us)
Async XLA Ops:
  140.7 7.2 %copy-start.1 = (bf16[8,256,1536]{2,1,0:T(8,128)(2,1)S(1)}, bf16[8,256,1536]{2,1,0:T(8,128)(2,1)}, u32[]{:S(2)}) copy-start(bf16[8,256,1536]{2,1,0:T(8,128)(2,1)} %get-tuple-element.39.nrm_ref) | copy-start | bytes 18874372
  140.7 7.2 %copy-start.10 = (bf16[8,256,384]{2,1,0:T(8,128)(2,1)S(1)}, bf16[8,256,384]{2,1,0:T(8,128)(2,1)}, u32[]{:S(2)}) copy-start(bf16[8,256,384]{2,1,0:T(8,128)(2,1)} %get-tuple-element.57) | copy-start | bytes 4718596
  147.8 4.5 %copy-start.9 = (bf16[8,256,384]{2,1,0:T(8,128)(2,1)S(1)}, bf16[8,256,384]{2,1,0:T(8,128)(2,1)}, u32[]{:S(2)}) copy-start(bf16[8,256,384]{2,1,0:T(8,128)(2,1)} %get-tuple-element.55) | copy-start | bytes 4718596
  152.3 2.6 copy-start.8
  258.7 5.2 %copy-start.5 = (f32[48,6144]{1,0:T(8,128)S(1)}, f32[48,6144]{1,0:T(8,128)}, u32[]{:S(2)}) copy-start(f32[48,6144]{1,0:T(8,128)} %get-tuple-element.64) | copy-start | bytes 3538948
  259.7 0.7 copy-start.7
  260.4 6.4 %copy-start = (bf16[256,1536]{1,0:T(8,128)(2,1)S(1)}, bf16[256,1536]{1,0:T(8,128)(2,1)}, u32[]{:S(2)}) copy-start(bf16[256,1536]{1,0:T(8,128)(2,1)} %x.3) | copy-start | bytes 2359300
  260.4 6.4 %copy-start.2 = (f32[256,1536]{1,0:T(8,128)S(1)}, f32[256,1536]{1,0:T(8,128)}, u32[]{:S(2)}) copy-start(f32[256,1536]{1,0:T(8,128)} %get-tuple-element.62) | copy-start | bytes 4718596
  265.9 1.4 copy-start.3
  265.9 1.7 copy-start.4
  267.5 7.4 %copy-start.6 = (f32[96,1536]{1,0:T(8,128)S(1)}, f32[96,1536]{1,0:T(8,128)}, u32[]{:S(2)}) copy-start(f32[96,1536]{1,0:T(8,128)} %get-tuple-element.95) | copy-start | bytes 1769476

commit v3 on v2

--- a/solution.py
+++ b/solution.py
@@ -63,9 +63,8 @@
 
 def small_layout(sz):
     tiles = sz.cs // LANES
-    sz.at_gain = 0
-    sz.at_bc = up8(sz.d // LANES)
-    sz.common = sz.at_bc + 2 * sz.state // LANES * 8
+    sz.at_bc = 0
+    sz.common = 2 * sz.state // LANES * 8
     sz.at_conv = sz.common
     sz.at_gate = sz.at_conv + tiles * 8
     sz.at_head = sz.at_gate + up8(tiles)
@@ -231,8 +230,8 @@
 
 
 def front_kernel(sz, x, go, win, tail, wout, norm, cw, cb, gate, lens, decay, bias, skip,
-                 NRM, GO, PX, PT, PZ, Y, GM, WX, WZ, WT, WO, Q, PAR, HEAD, TILE,
-                 xv, nv, gov, px, pt, pz, yv, gmv, wxv, wzv, wtv, wov, pack, smv, par, head, qv, qr, tilev,
+                 NT, GO, PX, PT, PZ, Y, GM, WX, WZ, WT, WO, Q, PAR, HEAD, TILE,
+                 xv, nv, gov, px, pt, pz, yv, gmv, wxv, wzv, wtv, wov, pack, smv, par, head, qv, qr, tilev, flip,
                  xsend, xrecv, gsend, grecv, wsend, wrecv, axsend, axrecv, azsend, azrecv, zxsend, zxrecv, zzsend, zzrecv,
                  tsend, trecv, osend, orecv, ssend, srecv, qsend, qrecv, lsem, esem, wsem):
     me = Place(sz)
@@ -415,8 +414,12 @@
         slot = slot_of(me, k)
         xb = xv[slot].astype(F32)
         mean = jnp.mean(xb * xb, axis=1, keepdims=True)
-        nv[slot] = (xb * lax.rsqrt(mean + EPS) * par[taps + 2 : taps + 3, 0 : sz.d]).astype(BF16)
-        pltpu.make_async_copy(nv.at[slot], NRM.at[slot], esem.at[0]).start()
+        nrm = (xb * lax.rsqrt(mean + EPS) * par[taps + 2 : taps + 3, 0 : sz.d]).astype(BF16)
+        nv[slot] = nrm
+        flip[...] = nrm.T
+        turn = pltpu.make_async_copy(flip, NT.at[:, pl.ds(pl.multiple_of(slot * rows, LANES), rows)], esem.at[0])
+        turn.start()
+        turn.wait()
 
     def wait_pair(gather, k):
         slot = slot_of(me, k)
@@ -611,8 +614,8 @@
                     landed(gauge, send.at[int(up), plane])
     for k, (src, dst) in enumerate(whole):
         pltpu.make_async_copy(src, dst, wsem.at[k]).wait()
-    for a, (src, dst) in enumerate([(nv, NRM), (px, PX), (pt, PT), (yv, Y), (pz, PZ), (gmv, GM), (gov, GO)]):
-        pltpu.make_async_copy(src, dst, esem.at[a]).wait()
+    for a, (src, dst) in enumerate([(px, PX), (pt, PT), (yv, Y), (pz, PZ), (gmv, GM), (gov, GO)]):
+        pltpu.make_async_copy(src, dst, esem.at[a + 1]).wait()
 
 
 def run_front(sz, x, go, win, tail, wout, norm, cw, cb, gate, lens, decay, bias, skip):
@@ -622,7 +625,7 @@
     vmem = pl.BlockSpec(memory_space=pltpu.VMEM)
     dma = pltpu.SemaphoreType.DMA
     shapes = dict(
-        nrm=((t, rows, d), BF16), go=((t, rows, d), BF16), px=((t, rows, cs), F32), pt=((t, rows, tl), F32), pz=((t, rows, cs), F32),
+        nrm=((t, rows, d), BF16), nt=((d, t * rows), BF16), go=((t, rows, d), BF16), px=((t, rows, cs), F32), pt=((t, rows, tl), F32), pz=((t, rows, cs), F32),
         y=((t, rows, cs), F32), gm=((t, rows, cs), F32), wx=((n, dn, cs), BF16), wz=((n, dn, cs), BF16), wt=((n, dn, tl), BF16),
         wo=((g, on, d), BF16), q=((2 * t, rows), F32), par=((8, d), F32), head=((8, LANES), F32), tile=((t, 8, LANES), F32),
     )
@@ -632,346 +635,469 @@
         functools.partial(front_kernel, sz),
         in_specs=[any_] * 5 + [vmem] * 8,
         out_specs=[any_] * 11 + [vmem] + [any_] * 3,
-        out_shape=out("nrm", "go", "px", "pt", "pz", "y", "gm", "wx", "wz", "wt", "wo", "q", "par", "head", "tile"),
+        out_shape=out("nt", "go", "px", "pt", "pz", "y", "gm", "wx", "wz", "wt", "wo", "q", "par", "head", "tile"),
         scratch_shapes=scr("nrm", "nrm", "go", "px", "pt", "pz", "y", "gm", "wx", "wz", "wt", "wo")
         + [pltpu.VMEM((8, LANES), F32), pltpu.VMEM((n, 8, LANES), F32)]
         + scr("par", "head", "q")
-        + [pltpu.VMEM((t, 2 * t, rows), F32), pltpu.VMEM((t, 8, LANES), F32)]
+        + [pltpu.VMEM((t, 2 * t, rows), F32), pltpu.VMEM((t, 8, LANES), F32), pltpu.VMEM((d, rows), BF16)]
         + [dma((1,)), dma((t, parts)), dma((1,)), dma((t, parts)), dma((1,)), dma((t, 1)), dma((1,)), dma((1,)), dma((1,)), dma((1,)),
            dma((2, g)), dma((g,)), dma((2, g)), dma((g,)), dma((1,)), dma((1,)), dma((3, g)), dma((g,)), dma((2,)), dma((2,)),
            dma((1,)), dma((1,)), dma((7,)), dma((7,)), dma((7,))],
-        compiler_params=pltpu.CompilerParams(collective_id=0, has_side_effects=True, vmem_limit_bytes=63 << 20),
+        compiler_params=pltpu.CompilerParams(collective_id=0, has_side_effects=True, vmem_limit_bytes=67043328),
         name="front",
     )(x, go, win, tail, wout, norm, cw, cb, gate, lens, decay, bias, skip)
 
 
-def bwd_kernel(sz, nrm_ref, px_ref, pt_ref, pz_ref, y_ref, gm_ref, q_ref, wx_ref, wz_ref, wt_ref, wo_ref, par_ref, head_ref, tile_ref,
-               mix_ref, hid_ref, dz_ref, dx_ref, dt_ref, gn_ref, small_ref):
-    b = pl.program_id(0)
+class LineReduce:
+    def __init__(self, sz, me, own, recv, send_sem, recv_sem):
+        self.sz, self.me, self.own, self.recv, self.send_sem, self.recv_sem = sz, me, own, recv, send_sem, recv_sem
+
+    def leg(self, step, up):
+        g, last = self.me.g, self.sz.g - 1
+        late = step - g if up else step - (last - g)
+        p = last - late if up else late
+        moves = (late >= 0) & ((p > g) if up else (p < g))
+        p = jnp.clip(p, 0, last)
+        inner = (g > 0) if up else (g < last)
+        nxt = jnp.clip(g + 1 if up else g - 1, 0, last)
+        there = p if up else jnp.where(p == nxt, last + 1, p)
+        copy = lambda: remote(self.sz, self.own.at[p], self.recv.at[there], self.send_sem.at[p], self.recv_sem.at[there], nxt, self.me.t)
+        return p, moves, inner, copy
+
+    def step(self, step):
+        for up in (True, False):
+            p, moves, inner, copy = self.leg(step, up)
+
+            @pl.when(moves & inner)
+            def _(p=p):
+                landed(self.recv.at[p], self.recv_sem.at[p])
+                self.own[p] = (self.own[p].astype(F32) + self.recv[p].astype(F32)).astype(BF16)
+
+            @pl.when(moves)
+            def _(copy=copy):
+                copy().start()
+
+    def total(self, acc):
+        g = self.me.g
+        acc[...] = self.own[g].astype(F32)
+        for k, there in ((g, g > 0), (self.sz.g, g < self.sz.g - 1)):
+            @pl.when(there)
+            def _(k=k):
+                landed(self.recv.at[k], self.recv_sem.at[k])
+                acc[...] += self.recv[k].astype(F32)
+
+    def sent(self):
+        for step in range(self.sz.g - 1):
+            for up in (True, False):
+                _, moves, _, copy = self.leg(step, up)
+
+                @pl.when(moves)
+                def _(copy=copy):
+                    copy().wait_send()
+
+
+class PlaneReduce:
+    def __init__(self, sz, me, stage, r0, s, r1, r2, out, sems):
+        self.sz, self.me, self.stage, self.r0, self.s, self.r1, self.r2, self.out = sz, me, stage, r0, s, r1, r2, out
+        self.send0, self.recv0, self.send1, self.recv1, self.send2, self.recv2 = sems
+
+    def chip(self, w):
+        m = self.me
+        return jnp.where(w == 0, m.fa, jnp.where(w == 1, m.fd, jnp.where(w == 2, m.fb, m.fi)))
+
+    def slot(self, k):
+        w = lax.rem(k, 4)
+        core = jnp.where(k < 4, self.me.other, self.me.c)
+        return self.chip(w) * 2 + core
+
+    def put0(self, w):
+        return remote(self.sz, self.stage.at[w], self.r0.at[w], self.send0.at[w], self.recv0.at[w], self.me.g, self.me.fi * 2 + self.me.other)
+
+    def put1(self, w):
+        return remote(self.sz, self.s.at[w], self.r1.at[w], self.send1.at[w], self.recv1.at[w], self.me.g, self.me.fa * 2 + self.me.c)
+
+    def put2(self):
+        return remote(self.sz, self.s.at[2], self.r2, self.send2.at[0], self.recv2.at[0], self.me.g, self.me.fb * 2 + self.me.c)
+
+    def block(self, k, value):
+        w = lax.rem(k, 4)
+
+        @pl.when(k < 4)
+        def _():
+            self.stage[w] = value.astype(BF16)
+            self.put0(w).start()
+
+        @pl.when(k >= 4)
+        def _():
+            there = jnp.where(w == 0, 2, jnp.where(w == 2, 0, w))
+            landed(self.r0.at[there], self.recv0.at[there])
+            total = value + self.r0[there].astype(F32)
+
+            @pl.when(w < 3)
+            def _():
+                self.s[w] = total.astype(BF16)
+
+            @pl.when(w < 2)
+            def _():
+                self.put1(w).start()
+
+            @pl.when(w == 3)
+            def _():
+                self.out(total, False)
+
+    def middle(self):
+        landed(self.r1.at[1], self.recv1.at[1])
+        self.s[2] = (self.s[2].astype(F32) + self.r1[1].astype(F32)).astype(BF16)
+        self.put2().start()
+
+    def finish(self):
+        landed(self.r1.at[0], self.recv1.at[0])
+        landed(self.r2, self.recv2.at[0])
+        self.out(self.r1[0].astype(F32) + self.r2[...].astype(F32), True)
+
+    def sent0(self):
+        for w in range(4):
+            self.put0(w).wait_send()
+
+    def sent(self):
+        for w in range(2):
+            self.put1(w).wait_send()
+        self.put2().wait_send()
+
+
+def back_kernel(sz, NT, GO, PX, PT, PZ, Y, GM, WX, WZ, WT, WO, q_ref, par, head, tile_ref,
+                HS, GS, RAZ, RAX, GTL, GOUT, GSM,
+                nt_, gov, ra, rx, rt_, wx, wz, wt, wo, mix, dz, dtv, dyv, r0h, sh, r1h, r2h, r0g, r1g, r2g, gs,
+                dwz, dwx, dwo, rzz, rzx, acc, szz, szx, raz, rax, ro, gout, rtt, st, rtz, gtl, small, rs1, s1, rs2, gsm,
+                lsem, asem, bsem, h0s, h0r, h1s, h1r, h2s, h2r, g0s, g0r, g1s, g1r, g2s, g2r, zzs, zzr, zxs, zxr, os_, or_, as_, ar_, ts, tr, us, ur, ss, sr, wsem):
     me = Place(sz)
-    rows, cs, st, taps = sz.rows, sz.cs, sz.state, sz.taps
+    rows, cs, st_dim, taps, T, G, d = sz.rows, sz.cs, sz.state, sz.taps, sz.t, sz.g, sz.d
     tiles = cs // LANES
-    keeps, valid, same = masks(rows, ends_of(tile_ref[0, taps + 3 : taps + 4, :], sz.seqs), taps)
-    at_gate, at_conv, at_head, at_gain = sz.at_gate, sz.at_conv, sz.at_head, sz.at_gain
-    lead = lax.rem(LANES - sz.nh * me.t, LANES)
-
-    @pl.when(b == 0)
-    def _():
-        small_ref[...] = jnp.zeros(small_ref.shape, F32)
+    half = rows // 2
+    barrier = pltpu.get_barrier_semaphore()
+
+    @pl.loop(1, sz.n)
+    def _(step):
+        there = lax.rem(me.i + step, sz.n)
+        pl.semaphore_signal(barrier, inc=1, device_id=(lax.div(there, sz.p), lax.rem(there, sz.p)), device_id_type=pl.DeviceIdType.MESH)
+
+    stage = gov.at[pl.ds(0, 4)]
+    dx = mix
+    pieces = d // cs
+
+    class Folded:
+        def at(self, c):
+            return ra.at[c // (pieces // 2), pl.ds(c % (pieces // 2) * rows, rows)]
+
+        def put(self, value, more):
+            for c in range(pieces):
+                part = value[:, c * cs : (c + 1) * cs]
+                self.at(c)[...] = self.at(c)[...] + part if more else part
+
+    hid = PlaneReduce(sz, me, stage, r0h, sh, r1h, r2h, Folded().put, (h0s, h0r, h1s, h1r, h2s, h2r))
+    def put_gs(value, more):
+        gs[...] = gs[...] + value if more else value
+
+    gn = PlaneReduce(sz, me, stage, r0g, gov.at[pl.ds(4, 3)], r1g, r2g, put_gs, (g0s, g0r, g1s, g1r, g2s, g2r))
+
+    def fetch_a(k):
+        slot, par_ = hid.slot(k), lax.rem(k, 2)
+        return [pltpu.make_async_copy(src.at[slot], ra.at[par_, pl.ds(a * rows, rows)], asem.at[par_]) for a, src in enumerate((PZ, Y, GM))]
+
+    def fetch_b(k):
+        slot, par_ = gn.slot(k), lax.rem(k, 2)
+        return [pltpu.make_async_copy(PX.at[slot], rx.at[par_], bsem.at[0, par_]), pltpu.make_async_copy(PT.at[slot], rt_.at[par_], bsem.at[1, par_])]
+
+    for k in range(2):
+        for copy in fetch_a(jnp.int32(k)):
+            copy.start()
+    loads = [pltpu.make_async_copy(src, dst, lsem.at[k]) for k, (src, dst) in enumerate(((NT, nt_), (WO, wo), (GO, gov), (WX, wx), (WZ, wz), (WT, wt)))]
+    for copy in loads[:1]:
+        copy.start()
+    for copy in fetch_b(jnp.int32(0)):
+        copy.start()
+    small[...] = jnp.zeros(small.shape, F32)
 
     def colsum(v):
         return jnp.sum(v, axis=0, keepdims=True)
-
-    def conv_pre(u, at):
-        return conv_tile(u, par_ref[0:taps, at : at + LANES], par_ref[taps : taps + 1, at : at + LANES], keeps, taps)
 
     def silu_pair(v):
         s = jax.nn.sigmoid(v)
         return v * s, s * (1.0 + v * (1.0 - s))
 
-    def conv_back(u, dact, dsilu, at):
-        dpre = dact * dsilu
-        tile = at // LANES
-        row = at_conv + tile * 8 if tile < tiles else sz.at_bc + (tile - tiles) * 8
-        back = dpre * par_ref[taps - 1 : taps, at : at + LANES]
-        small_ref[row + taps - 1 : row + taps, :] += colsum(dpre * u)
-        small_ref[row + taps : row + taps + 1, :] += colsum(dpre)
-        for off in range(1, taps):
-            kept = dpre * keeps[off - 1]
-            tap = taps - 1 - off
-            small_ref[row + tap : row + tap + 1, :] += colsum(kept * pltpu.roll(u, off, 0))
-            back = back + pltpu.roll(kept, rows - off, 0) * par_ref[tap : tap + 1, at : at + LANES]
-        return back
-
-    ub, uc = pt_ref[0, :, 0:st], pt_ref[0, :, st : 2 * st]
-    bm, bslope = silu_pair(conv_pre(ub, cs))
-    cm, cslope = silu_pair(conv_pre(uc, cs + st))
-    raw = pltpu.roll(pt_ref[0, :, 2 * st : 2 * st + LANES], lead, 1) + head_ref[0:1, :]
-    dt = softplus(raw)
-    rate = -jnp.exp(head_ref[1:2, :])
-    log_decay = jnp.dot(triangle(rows).astype(F32), dt * rate, precision=EXACT, preferred_element_type=F32)
-    log_t = log_decay.T
-    upper = iota((rows, rows), 1) >= iota((rows, rows), 0)
-    drop = jnp.where(same & upper, 0.0, -jnp.inf)
-    inner_t = three(nt, bm, cm)
+    @pl.loop(0, T)
+    def _(k):
+        slot, par_ = hid.slot(k), lax.rem(k, 2)
+
+        @pl.when(k == T // 2)
+        def _():
+            for copy in loads[1:]:
+                copy.start()
+
+        landed(ra.at[par_, pl.ds(0, 3 * rows)], asem.at[par_])
+        pos = iota((rows, LANES), 0).astype(F32)
+        valid = (segments(pos, ends_of(tile_ref[slot, taps + 3 : taps + 4, :], sz.seqs)) < sz.seqs).astype(F32)
+        q1 = jnp.broadcast_to(q_ref[pl.ds(slot, 1), :], (LANES, rows)).T
+        q2 = jnp.broadcast_to(q_ref[pl.ds(T + slot, 1), :], (LANES, rows)).T
+        scale = lax.rsqrt(q1 / sz.di + EPS)
+        pull = scale * scale * scale * q2 / sz.di
+        for j in range(tiles):
+            tile = slice(j * LANES, (j + 1) * LANES)
+            zt, y, gm = (ra[par_, a * rows : (a + 1) * rows, tile] for a in range(3))
+            gm = gm * valid
+            gate = par[taps + 1 : taps + 2, tile]
+            up, slope = silu_pair(zt)
+            gated = y * up
+            unit = gated * scale
+            mix[slot, :, tile] = (unit * gate * valid).astype(BF16)
+            small[sz.at_gate + j : sz.at_gate + j + 1, :] += colsum(gm * unit)
+            dgated = scale * gm * gate - gated * pull
+            dz[slot, :, tile] = (dgated * y * slope).astype(BF16)
+            dyv[slot, :, tile] = dgated * up
+
+        @pl.when(k + 2 < T)
+        def _():
+            for copy in fetch_a(k + 2):
+                copy.start()
+
+    def weight_grad(values, into):
+        dn = sz.d // sz.n
+        for at in range(0, sz.n, sz.n // 4):
+            span = sz.n // 4 * dn
+            got = nn(nt_[at * dn : at * dn + span, :], values[...].reshape(T * rows, values.shape[2]))
+            for i in range(at, at + sz.n // 4):
+                f, p = i // sz.p, i % sz.p
+                fo, fi, z, c = f // sz.fi, f % sz.fi, p // 2, p % 2
+                into[fo * sz.z + z, fi * 2 + c, :, 0 : got.shape[1]] = got[(i - at) * dn : (i - at + 1) * dn].astype(BF16)
+
+    line_z = LineReduce(sz, me, dwz.at[:, :, :, pl.ds(0, cs)], rzz, zzs, zzr)
+    line_x = LineReduce(sz, me, dwx, rzx, zxs, zxr)
+    loads[0].wait()
+    weight_grad(dz, dwz)
+    pl.semaphore_wait(barrier, sz.n - 1)
+    line_z.step(0)
+    loads[1].wait()
+
+    loads[2].wait()
+
+    def o_copy(k):
+        owner = me.t * G + k
+        return pltpu.make_async_remote_copy(src_ref=dwo.at[k], dst_ref=ro.at[me.g], send_sem=os_.at[k], recv_sem=or_.at[me.g],
+                                            device_id=(lax.div(owner, sz.p), lax.rem(owner, sz.p)), device_id_type=pl.DeviceIdType.MESH)
+
+    for at in range(0, d, d // 3):
+        got = tn(mix[...].reshape(T * rows, cs), gov[:, :, at : at + d // 3].reshape(T * rows, d // 3))
+        for k in range(G):
+            dwo[k, :, at : at + d // 3] = got[k * (cs // G) : (k + 1) * (cs // G)].astype(BF16)
+    def out_sends():
+        for k in range(G):
+            @pl.when(t_differs(sz, me, k))
+            def _(k=k):
+                o_copy(k).start()
+
+    @pl.loop(0, T)
+    def _(k):
+        hid.block(k, nn(mix[hid.slot(k)], wo[...].reshape(cs, d)))
+
+    for copy in loads[3:]:
+        copy.wait()
+
     low = iota((rows, LANES), 1) < sz.hd
     lane = iota((rows, LANES), 1)
-    q1 = jnp.broadcast_to(q_ref[pl.ds(b, 1), :], (LANES, rows)).T
-    q2 = jnp.broadcast_to(q_ref[pl.ds(sz.t + b, 1), :], (LANES, rows)).T
-    scale = lax.rsqrt(q1 / sz.di + EPS)
-    pull = scale * scale * scale * q2 / sz.di
-
-    dcb = jnp.zeros((rows, rows), F32)
-    ddt = jnp.zeros((rows, LANES), F32)
-    cols = jnp.zeros((rows, LANES), F32)
-    rowsums = jnp.zeros((LANES, rows), F32)
-    lane_row = iota((LANES, rows), 0)
+    lead = lax.rem(LANES - sz.nh * me.t, LANES)
+    quads = ((slice(0, half), slice(0, rows)), (slice(half, rows), slice(half, rows)))
+
+    def between(k, *steps):
+        @pl.when(k)
+        def _():
+            for step in steps:
+                step()
+
+    def scan_back(k):
+        slot, par_ = gn.slot(k), lax.rem(k, 2)
+
+        @pl.when(k + 1 < T)
+        def _():
+            for copy in fetch_b(k + 1):
+                copy.start()
+
+        landed(rx.at[par_], bsem.at[0, par_])
+        landed(rt_.at[par_], bsem.at[1, par_])
+        keeps, _, same = masks(rows, ends_of(tile_ref[slot, taps + 3 : taps + 4, :], sz.seqs), taps)
+
+        def conv_pre(u, at):
+            return conv_tile(u, par[0:taps, at : at + LANES], par[taps : taps + 1, at : at + LANES], keeps, taps)
+
+        def conv_back(u, dact, dsilu, at):
+            dpre = dact * dsilu
+            tile = at // LANES
+            row = sz.at_conv + tile * 8 if tile < tiles else sz.at_bc + (tile - tiles) * 8
+            back = dpre * par[taps - 1 : taps, at : at + LANES]
+            small[row + taps - 1 : row + taps, :] += colsum(dpre * u)
+            small[row + taps : row + taps + 1, :] += colsum(dpre)
+            for off in range(1, taps):
+                kept = dpre * keeps[off - 1]
+                tap = taps - 1 - off
+                small[row + tap : row + tap + 1, :] += colsum(kept * pltpu.roll(u, off, 0))
+                back = back + pltpu.roll(kept, rows - off, 0) * par[tap : tap + 1, at : at + LANES]
+            return back
+
+        ub, uc = rt_[par_, :, 0:st_dim], rt_[par_, :, st_dim : 2 * st_dim]
+        bm, bslope = silu_pair(conv_pre(ub, cs))
+        cm, cslope = silu_pair(conv_pre(uc, cs + st_dim))
+        raw = pltpu.roll(rt_[par_, :, 2 * st_dim : 2 * st_dim + LANES], lead, 1) + head[0:1, :]
+        dt = softplus(raw)
+        rate = -jnp.exp(head[1:2, :])
+        log_decay = jnp.dot(triangle(rows).astype(F32), dt * rate, precision=EXACT, preferred_element_type=F32)
+        log_t = log_decay.T
+        upper = iota((rows, rows), 1) >= iota((rows, rows), 0)
+        drop = jnp.where(same & upper, 0.0, -jnp.inf)
+        inner_t = three(nt, bm, cm)
+        dcb = [jnp.zeros((half, rows), F32), jnp.zeros((half, half), F32)]
+        ddt = jnp.zeros((rows, LANES), F32)
+        cols = jnp.zeros((rows, LANES), F32)
+        rowsums = jnp.zeros((LANES, rows), F32)
+        lane_row = iota((LANES, rows), 0)
+        for j in range(tiles):
+            at = j * LANES
+            tile = slice(at, at + LANES)
+            dy = dyv[slot, :, tile]
+            ux = rx[par_, :, tile]
+            xa, xslope = silu_pair(conv_pre(ux, at))
+            small[sz.at_head + 3 + j : sz.at_head + 4 + j, :] += colsum(dy * xa)
+            dt2 = jnp.where(low, dt[:, 2 * j : 2 * j + 1], dt[:, 2 * j + 1 : 2 * j + 2])
+            xd = xa * dt2
+            dyh, dyl = split(dy)
+            tops = []
+            for e in range(2):
+                h = 2 * j + e
+                mine = low if e == 0 else jnp.logical_not(low)
+                xh, xl = split(jnp.where(mine, xd, 0.0))
+                dym = jnp.where(mine, dy, 0.0).astype(BF16)
+                parts, psums, tsum = [], [], []
+                for quad, (r, c) in enumerate(quads):
+                    decay = jnp.exp(log_t[h : h + 1, c] - log_decay[r, h : h + 1] + drop[r, c])
+                    df = (nt(xh[r], dyh[c]) + (nt(xh[r], dyl[c]) + nt(xl[r], dyh[c]))) * decay
+                    dcb[quad] = dcb[quad] + df
+                    p = df * inner_t[r, c]
+                    psums.append(jnp.sum(p, axis=1, keepdims=True))
+                    tsum.append(colsum(p))
+                    parts.append(nn((decay * inner_t[r, c]).astype(BF16), dym[c]))
+                cols = jnp.where(lane == h, jnp.concatenate(psums, axis=0), cols)
+                tsum = tsum[0] + jnp.concatenate([jnp.zeros((1, half), F32), tsum[1]], axis=1)
+                rowsums = jnp.where(lane_row == h, tsum, rowsums)
+                tops.append(jnp.concatenate(parts, axis=0))
+            dxd = tops[0] + tops[1]
+            both = dxd * xa
+            ddt = jnp.where(lane == 2 * j, jnp.sum(jnp.where(low, both, 0.0), axis=1, keepdims=True), ddt)
+            ddt = jnp.where(lane == 2 * j + 1, jnp.sum(jnp.where(low, 0.0, both), axis=1, keepdims=True), ddt)
+            skip2 = jnp.where(low[0:1], head[2:3, 2 * j : 2 * j + 1], head[2:3, 2 * j + 1 : 2 * j + 2])
+            dx[slot, :, tile] = conv_back(ux, dxd * dt2 + dy * skip2, xslope, at).astype(BF16)
+
+        ga = jnp.dot(upper.astype(F32), rowsums.T - cols, precision=EXACT, preferred_element_type=F32)
+        ddt = ddt + ga * rate
+        small[sz.at_head : sz.at_head + 1, :] += rate * colsum(ga * dt)
+        draw = jnp.where(lane < sz.nh, ddt * jax.nn.sigmoid(raw), 0.0)
+        small[sz.at_head + 1 : sz.at_head + 2, :] += colsum(draw)
+        dtv[slot, :, 2 * st_dim : 2 * st_dim + LANES] = pltpu.roll(draw, sz.nh * me.t, 1).astype(BF16)
+        top, bottom = dcb[0].astype(BF16), dcb[1].astype(BF16)
+        bb, cb = bm.astype(BF16), cm.astype(BF16)
+        db = jnp.concatenate([nn(top, cb), nn(bottom, cb[half:])], axis=0)
+        dc = tn(top, bb[:half]) + jnp.concatenate([jnp.zeros((half, st_dim), F32), tn(bottom, bb[half:])], axis=0)
+        dtv[slot, :, 0:st_dim] = conv_back(ub, db, bslope, cs).astype(BF16)
+        dtv[slot, :, st_dim : 2 * st_dim] = conv_back(uc, dc, cslope, cs + st_dim).astype(BF16)
+        between(k == 0, hid.sent0)
+        gn.block(k, nt(dz[slot], wz[...].reshape(d, cs)) + nt(dx[slot], wx[...].reshape(d, cs)) + nt(dtv[slot], wt[...].reshape(d, sz.tl)))
+
+    @pl.loop(0, T)
+    def _(k):
+        between(k == 0, lambda: line_z.step(1))
+        between(k == 1, lambda: [line_z.step(step) for step in range(2, G - 1)], out_sends)
+        between(k == 3, hid.middle)
+        between(k == 6, hid.finish)
+        scan_back(k)
+
+    weight_grad(dx, dwx)
+    line_x.step(0)
+    line_z.total(acc)
+    szz[...] = acc[...].astype(BF16)
+
+    def hand(sums, into, k):
+        for step in range(1, T):
+            there = lax.rem(me.t + step, T)
+            remote(sz, sums.at[there], into.at[me.t], as_.at[k], ar_.at[k], me.g, there).start()
+        into[me.t] = sums[me.t]
+
+    hand(szz, raz, 0)
+    line_z.sent()
+    dwt = dwz.at[:, :, :, pl.ds(0, sz.tl)]
+    weight_grad(dtv, dwz)
+
+    def t_copy(step):
+        there = lax.rem(me.t + step, T)
+        return [remote(sz, dwt.at[g, there], rtt.at[me.t, g], ts.at[0], tr.at[0], me.g, there) for g in range(G)]
+
+    for step in range(1, T):
+        for copy in t_copy(step):
+            copy.start()
+
     for j in range(tiles):
-        at = j * LANES
-        tile = slice(at, at + LANES)
-        zt = pz_ref[0, :, tile]
-        y = y_ref[0, :, tile]
-        gm = gm_ref[0, :, tile] * valid
-        gate = par_ref[taps + 1 : taps + 2, tile]
-        sz_, zslope = silu_pair(zt)
-        gated = y * sz_
-        unit = gated * scale
-        mix_ref[0, :, tile] = (unit * gate * valid).astype(BF16)
-        small_ref[at_gate + j : at_gate + j + 1, :] += colsum(gm * unit)
-        dgated = scale * gm * gate - gated * pull
-        dz_ref[0, :, tile] = (dgated * y * zslope).astype(BF16)
-        dy = dgated * sz_
-        ux = px_ref[0, :, tile]
-        xa, xslope = silu_pair(conv_pre(ux, at))
-        small_ref[at_head + 3 + j : at_head + 4 + j, :] += colsum(dy * xa)
-        dt2 = jnp.where(low, dt[:, 2 * j : 2 * j + 1], dt[:, 2 * j + 1 : 2 * j + 2])
-        xd = xa * dt2
-        dxd = []
-        for e in range(2):
-            h = 2 * j + e
-            mine = low if e == 0 else jnp.logical_not(low)
-            decay = jnp.exp(log_t[h : h + 1, :] - log_decay[:, h : h + 1] + drop)
-            df = three(nt, jnp.where(mine, xd, 0.0), dy) * decay
-            dcb = dcb + df
-            p = df * inner_t
-            cols = jnp.where(lane == h, jnp.sum(p, axis=1, keepdims=True), cols)
-            rowsums = jnp.where(lane_row == h, colsum(p), rowsums)
-            dxd.append(nn((decay * inner_t).astype(BF16), jnp.where(mine, dy, 0.0).astype(BF16)))
-        dxd = dxd[0] + dxd[1]
-        both = dxd * xa
-        ddt = jnp.where(lane == 2 * j, jnp.sum(jnp.where(low, both, 0.0), axis=1, keepdims=True), ddt)
-        ddt = jnp.where(lane == 2 * j + 1, jnp.sum(jnp.where(low, 0.0, both), axis=1, keepdims=True), ddt)
-        skip2 = jnp.where(low[0:1], head_ref[2:3, 2 * j : 2 * j + 1], head_ref[2:3, 2 * j + 1 : 2 * j + 2])
-        dx = dxd * dt2 + dy * skip2
-        dx_ref[0, :, tile] = conv_back(ux, dx, xslope, at).astype(BF16)
-
-    ga = jnp.dot(upper.astype(F32), rowsums.T - cols, precision=EXACT, preferred_element_type=F32)
-    ddt = ddt + ga * rate
-    small_ref[at_head : at_head + 1, :] += rate * colsum(ga * dt)
-    draw = jnp.where(lane < sz.nh, ddt * jax.nn.sigmoid(raw), 0.0)
-    small_ref[at_head + 1 : at_head + 2, :] += colsum(draw)
-    dt_ref[0, :, 2 * st : 2 * st + LANES] = pltpu.roll(draw, sz.nh * me.t, 1).astype(BF16)
-    dcb = dcb.astype(BF16)
-    db = nn(dcb, cm.astype(BF16))
-    dc = tn(dcb, bm.astype(BF16))
-    dt_ref[0, :, 0:st] = conv_back(ub, db, bslope, cs).astype(BF16)
-    dt_ref[0, :, st : 2 * st] = conv_back(uc, dc, cslope, cs + st).astype(BF16)
-
-    hid_ref[0] = nn(mix_ref[0], wo_ref[...]).astype(BF16)
-    gn = nt(dz_ref[0], wz_ref[...]) + nt(dx_ref[0], wx_ref[...]) + nt(dt_ref[0], wt_ref[...])
-    gn_ref[0] = gn.astype(BF16)
-    sums = colsum(gn * nrm_ref[0].astype(F32)) / par_ref[taps + 2 : taps + 3, 0 : sz.d]
-    for k in range(sz.d // LANES):
-        small_ref[at_gain + k : at_gain + k + 1, :] += sums[:, k * LANES : (k + 1) * LANES]
-
-
-def run_bwd(sz, nrm, px, pt, pz, y, gm, q, wx, wz, wt, wo, par, head, tile):
-    t, rows, d, cs, tl = sz.t, sz.rows, sz.d, sz.cs, sz.tl
-    whole = lambda a: pl.BlockSpec(a.shape, lambda b: (0,) * a.ndim)
-    block = lambda width: pl.BlockSpec((1, rows, width), lambda b: (b, 0, 0))
-    return pl.pallas_call(
-        functools.partial(bwd_kernel, sz),
-        grid=(t,),
-        in_specs=[block(d), block(cs), block(tl), block(cs), block(cs), block(cs), whole(q), whole(wx), whole(wz), whole(wt), whole(wo), whole(par),
-                  whole(head), pl.BlockSpec((1, 8, LANES), lambda b: (b, 0, 0))],
-        out_specs=[block(cs), block(d), block(cs), block(cs), block(tl), block(d), pl.BlockSpec((sz.small_rows, LANES), lambda b: (0, 0))],
-        out_shape=[
-            jax.ShapeDtypeStruct((t, rows, cs), BF16),
-            jax.ShapeDtypeStruct((t, rows, d), BF16),
-            jax.ShapeDtypeStruct((t, rows, cs), BF16),
-            jax.ShapeDtypeStruct((t, rows, cs), BF16),
-            jax.ShapeDtypeStruct((t, rows, tl), BF16),
-            jax.ShapeDtypeStruct((t, rows, d), BF16),
-            jax.ShapeDtypeStruct((sz.small_rows, LANES), F32),
-        ],
-        compiler_params=pltpu.CompilerParams(vmem_limit_bytes=60 << 20),
-        name="bwd",
-    )(nrm, px, pt, pz, y, gm, q, wx, wz, wt, wo, par, head, tile)
-
-
-def reduce_kernel(sz, hp, gp, dwzx, dwtl, dwo, sm, hsum, gsum, gin, gtl, gout, gsm, hs, gs, r0h, r0g, r1h, r1g, r2h, r2g, rz, sz_, ro, rt, st, rtz, ra,
-                  rs1, s1, rs2, p0send, p0recv, p1send, p1recv, p2send, p2recv, zsend, zrecv, asend, arecv, osend, orecv, tsend, trecv, uzsend, uzrecv,
-                  s1send, s1recv, s2send, s2recv, usend, urecv):
-    me = Place(sz)
-    cs, rows, G, T, FI = sz.cs, sz.rows, sz.g, sz.t, sz.fi
-    parts, pr = sz.rparts, sz.rows // sz.rparts
-    greet_all(sz, me)
-
-    def up32(v):
-        return v.astype(F32)
-
-    def s1_copy(step):
-        return remote(sz, sm, rs1.at[me.g], s1send.at[step], s1recv.at[me.g], lax.rem(me.g + step, G), me.t)
-
+        spot = iota((LANES, LANES), 1) == 2 * j + (iota((LANES, LANES), 0) >= sz.hd).astype(jnp.int32)
+        part = jnp.dot(small[sz.at_head + 3 + j : sz.at_head + 4 + j, :], spot.astype(F32), precision=EXACT, preferred_element_type=F32)
+        small[sz.at_head + 2 : sz.at_head + 3, :] += part
+    s_line = lambda step: remote(sz, small, rs1.at[me.g], ss.at[0], sr.at[0], lax.rem(me.g + step, G), me.t)
     for step in range(1, G):
-        s1_copy(step).start()
-
-    arrays = [(hp, hs, r0h, r1h, r2h, hsum), (gp, gs, r0g, r1g, r2g, gsum)]
-    order = (me.fa, me.fd, me.fb, me.fi)
-
-    def p0_copy(k, which, part):
-        src, _, r0 = arrays[k][:3]
-        fi = order[which]
-        rows_ = pl.ds(part * pr, pr)
-        return remote(sz, src.at[fi * 2 + me.other, rows_], r0.at[fi, rows_], p0send.at[k, which, part], p0recv.at[k, fi, part], me.g, me.fi * 2 + me.other)
-
-    for k in range(2):
-        for which in range(4):
-            for part in range(parts):
-                p0_copy(k, which, part).start()
-
-    def t_copy(step, g):
-        there = lax.rem(me.t + step, T)
-        return remote(sz, dwtl.at[index_of(sz, g, there)], rt.at[me.t, g], tsend.at[step, g], trecv.at[me.t, g], me.g, there)
-
-    for step in range(1, T):
-        for g in range(G):
-            t_copy(step, g).start()
-
-    def z_copy(step, fi):
-        there = lax.rem(me.g + step, G)
-        return remote(sz, dwzx.at[pl.ds(index_of(sz, there, jnp.int32(2 * fi)), 2)], rz.at[me.g, pl.ds(2 * fi, 2)], zsend.at[step, fi], zrecv.at[me.g, fi],
-                      there, me.t)
-
-    for step in range(1, G):
-        for fi in range(FI):
-            z_copy(step, fi).start()
-
-    def o_copy(k):
-        owner = me.t * G + k
-        f, p = lax.div(owner, sz.p), lax.rem(owner, sz.p)
-        return pltpu.make_async_remote_copy(src_ref=dwo.at[k], dst_ref=ro.at[me.g], send_sem=osend.at[k], recv_sem=orecv.at[me.g],
-                                            device_id=(f, p), device_id_type=pl.DeviceIdType.MESH)
-
-    for k in range(G):
-        @pl.when(t_differs(sz, me, k))
-        def _(k=k):
-            o_copy(k).start()
-
-    def p1_copy(k, which, part):
-        _, s, _, r1 = arrays[k][:4]
-        rows_ = pl.ds(part * pr, pr)
-        return remote(sz, s.at[which, rows_], r1.at[which, rows_], p1send.at[k, which, part], p1recv.at[k, which, part], me.g, me.fa * 2 + me.c)
-
-    def p2_copy(k, part):
-        _, s, _, _, r2 = arrays[k][:5]
-        rows_ = pl.ds(part * pr, pr)
-        return remote(sz, s.at[2, rows_], r2.at[rows_], p2send.at[k, part], p2recv.at[k, part], me.g, me.fb * 2 + me.c)
-
-    for k in range(2):
-        src, s, r0, r1, r2, out = arrays[k]
-        for which in range(4):
-            fi = order[which]
-            for part in range(parts):
-                rows_ = pl.ds(part * pr, pr)
-                landed(r0.at[fi, rows_], p0recv.at[k, fi, part])
-                both = up32(src[fi * 2 + me.c, rows_]) + up32(r0[fi, rows_])
-                if which < 2:
-                    s[which, rows_] = both.astype(BF16)
-                    p1_copy(k, which, part).start()
-                elif which == 2:
-                    s[2, rows_] = both.astype(BF16)
-                else:
-                    out[rows_] = both
-
-    for step in range(1, T):
-        for g in range(G):
-            there = lax.rem(me.t + step, T)
-            landed(rt.at[there, g], trecv.at[there, g])
-    for g in range(G):
-        total = up32(dwtl[index_of(sz, g, me.t)])
-        for step in range(1, T):
-            total = total + up32(rt[lax.rem(me.t + step, T), g])
-        st[g] = total.astype(BF16)
-
-    def uz_copy(step):
-        there = lax.rem(me.g + step, G)
-        return remote(sz, st.at[there], rtz.at[me.g], uzsend.at[step], uzrecv.at[me.g], there, me.t)
-
-    for step in range(1, G):
-        uz_copy(step).start()
-
-    total = sm[...]
-    for step in range(1, G):
-        there = lax.rem(me.g + step, G)
-        landed(rs1.at[there], s1recv.at[there])
-        total = total + rs1[there]
-    s1[...] = total
-    rs2[me.t] = total
-
-    def s2_copy(step):
-        return remote(sz, s1, rs2.at[me.t], s2send.at[step], s2recv.at[me.t], me.g, lax.rem(me.t + step, T))
-
-    for step in range(1, T):
-        s2_copy(step).start()
-
-    for k in range(2):
-        src, s, r0, r1, r2, out = arrays[k]
-        for part in range(parts):
-            rows_ = pl.ds(part * pr, pr)
-            landed(r1.at[1, rows_], p1recv.at[k, 1, part])
-            s[2, rows_] = (up32(s[2, rows_]) + up32(r1[1, rows_])).astype(BF16)
-            p2_copy(k, part).start()
-
-    for fi in range(FI):
-        for step in range(1, G):
-            there = lax.rem(me.g + step, G)
-            landed(rz.at[there, pl.ds(2 * fi, 2)], zrecv.at[there, fi])
-        for c in range(2):
-            total = up32(dwzx[index_of(sz, me.g, jnp.int32(2 * fi + c))])
-            for step in range(1, G):
-                total = total + up32(rz[lax.rem(me.g + step, G), 2 * fi + c])
-            sz_[2 * fi + c] = total.astype(BF16)
-
-    def a_copy(step):
-        there = lax.rem(me.t + step, T)
-        return remote(sz, sz_.at[there], ra.at[me.t], asend.at[step], arecv.at[me.t], me.g, there)
-
-    for step in range(1, T):
-        a_copy(step).start()
-    ra[me.t] = sz_[me.t]
-
-    total = jnp.zeros(gout.shape, F32)
+        s_line(step).start()
+
+    saves = [pltpu.make_async_copy(Folded().at(c), HS.at[:, pl.ds(c * cs, cs)], wsem.at[7 + c]) for c in range(pieces)]
+    for copy in saves:
+        copy.start()
+    gn.middle()
+    line_x.step(1)
+
     mine = lax.div(me.i, G) == me.t
 
     @pl.when(mine)
     def _():
-        gout[...] = up32(dwo[lax.rem(me.i, G)])
+        gout[...] = dwo[lax.rem(me.i, G)].astype(F32)
 
     @pl.when(jnp.logical_not(mine))
     def _():
         gout[...] = jnp.zeros(gout.shape, F32)
 
     for g in range(G):
-        other = jnp.logical_not(mine & (me.g == g))
-
-        @pl.when(other)
+        @pl.when(jnp.logical_not(mine & (me.g == g)))
         def _(g=g):
-            landed(ro.at[g], orecv.at[g])
-            gout[...] += up32(ro[g])
-
-    total = up32(st[me.g])
+            landed(ro.at[g], or_.at[g])
+            gout[...] += ro[g].astype(F32)
+
+    saves.append(pltpu.make_async_copy(gout, GOUT, wsem.at[1]))
+    saves[-1].start()
+    landed(rs1.at[pl.ds(0, G - 1)], sr.at[0])
+    total = small[...]
     for step in range(1, G):
-        there = lax.rem(me.g + step, G)
-        landed(rtz.at[there], uzrecv.at[there])
-        total = total + up32(rtz[there])
-    gtl[...] = total
-
-    for k in range(2):
-        src, s, r0, r1, r2, out = arrays[k]
-        for part in range(parts):
-            rows_ = pl.ds(part * pr, pr)
-            landed(r1.at[0, rows_], p1recv.at[k, 0, part])
-            landed(r2.at[rows_], p2recv.at[k, part])
-            out[rows_] = out[rows_] + up32(r1[0, rows_]) + up32(r2[rows_])
-
+        total = total + rs1[lax.rem(me.g + step, G)]
+    s1[...] = total
+    rs2[me.t] = total
+    s_plane = lambda step: remote(sz, s1, rs2.at[me.t], ss.at[1], sr.at[1], me.g, lax.rem(me.t + step, T))
     for step in range(1, T):
-        there = lax.rem(me.t + step, T)
-        landed(ra.at[there], arecv.at[there])
-        landed(rs2.at[there], s2recv.at[there])
-    for t in range(T):
-        gin[:, t * cs : (t + 1) * cs] = up32(ra[t, :, 0:cs])
-        gin[:, sz.di + t * cs : sz.di + (t + 1) * cs] = up32(ra[t, :, cs:])
+        s_plane(step).start()
+
+    for step in range(2, G - 1):
+        line_x.step(step)
+    landed(rtt.at[pl.ds(0, T - 1)], tr.at[0])
+    for g in range(G):
+        total = dwt[g, me.t].astype(F32)
+        for step in range(1, T):
+            total = total + rtt[lax.rem(me.t + step, T), g].astype(F32)
+        st[g] = total.astype(BF16)
+    t_line = lambda step: remote(sz, st.at[lax.rem(me.g + step, G)], rtz.at[me.g], us.at[0], ur.at[0], lax.rem(me.g + step, G), me.t)
+    for step in range(1, G):
+        t_line(step).start()
+    gn.finish()
+    saves.append(pltpu.make_async_copy(gs, GS, wsem.at[2]))
+    saves[-1].start()
+    landed(rs2.at[pl.ds(0, T - 1)], sr.at[1])
     total = rs2[0, 0 : sz.common]
     for t in range(1, T):
         total = total + rs2[t, 0 : sz.common]
@@ -979,61 +1105,175 @@
     width = sz.small_rows - sz.common
     for t in range(T):
         gsm[sz.common + t * width : sz.common + (t + 1) * width] = rs2[t, sz.common :]
-
+    saves.append(pltpu.make_async_copy(gsm, GSM, wsem.at[3]))
+    saves[-1].start()
+
+    line_x.total(acc)
+    szx[...] = acc[...].astype(BF16)
+    hand(szx, rax, 1)
+    landed(raz.at[pl.ds(0, T - 1)], ar_.at[0])
+    saves.append(pltpu.make_async_copy(raz, RAZ, wsem.at[4]))
+    saves[-1].start()
+    landed(rtz.at[pl.ds(0, G - 1)], ur.at[0])
+    total = st[me.g].astype(F32)
     for step in range(1, G):
-        s1_copy(step).wait_send()
-        uz_copy(step).wait_send()
-        for fi in range(FI):
-            z_copy(step, fi).wait_send()
-    for step in range(1, T):
-        s2_copy(step).wait_send()
-        a_copy(step).wait_send()
-        for g in range(G):
-            t_copy(step, g).wait_send()
-    for k in range(2):
-        for part in range(parts):
-            for which in range(4):
-                p0_copy(k, which, part).wait_send()
-            for which in range(2):
-                p1_copy(k, which, part).wait_send()
-            p2_copy(k, part).wait_send()
+        total = total + rtz[lax.rem(me.g + step, G)].astype(F32)
+    gtl[...] = total
+    saves.append(pltpu.make_async_copy(gtl, GTL, wsem.at[5]))
+    saves[-1].start()
+    landed(rax.at[pl.ds(0, T - 1)], ar_.at[1])
+    saves.append(pltpu.make_async_copy(rax, RAX, wsem.at[6]))
+    saves[-1].start()
+
+    hid.sent()
+    gn.sent0()
+    gn.sent()
+    line_x.sent()
     for k in range(G):
         @pl.when(t_differs(sz, me, k))
         def _(k=k):
             o_copy(k).wait_send()
-
-
-def run_reduce(sz, hp, gp, dwzx, dwtl, dwo, sm):
-    n, g, t, rows, d, cs, tl, parts, fi = sz.n, sz.g, sz.t, sz.rows, sz.d, sz.cs, sz.tl, sz.rparts, sz.fi
-    dn, on = dwzx.shape[1], dwo.shape[1]
+    for k in range(2):
+        landed(raz.at[pl.ds(0, T - 1)], as_.at[k])
+    landed(rtt.at[pl.ds(0, T - 1)], ts.at[0])
+    landed(rtz.at[pl.ds(0, G - 1)], us.at[0])
+    landed(rs1.at[pl.ds(0, G - 1)], ss.at[0])
+    landed(rs2.at[pl.ds(0, T - 1)], ss.at[1])
+    for copy in saves:
+        copy.wait()
+
+
+def run_back(sz, nt, go, px, pt, pz, y, gm, wx, wz, wt, wo, q, par, head, tile):
+    n, g, t, rows, d, cs, tl = sz.n, sz.g, sz.t, sz.rows, sz.d, sz.cs, sz.tl
+    dn, on = d // n, sz.di // n
+    any_ = pl.BlockSpec(memory_space=pl.ANY)
     vmem = pl.BlockSpec(memory_space=pltpu.VMEM)
     dma = pltpu.SemaphoreType.DMA
-    v = lambda *s: pltpu.VMEM(s, BF16)
+    b = lambda *s: pltpu.VMEM(s, BF16)
+    f = lambda *s: pltpu.VMEM(s, F32)
     sr = sz.small_rows
     total_rows = sz.common + t * (sr - sz.common)
+    plane = lambda: [dma((4,)), dma((4,)), dma((2,)), dma((2,)), dma((1,)), dma((1,))]
     return pl.pallas_call(
-        functools.partial(reduce_kernel, sz),
-        in_specs=[vmem] * 6,
-        out_specs=[vmem] * 6,
+        functools.partial(back_kernel, sz),
+        in_specs=[any_] * 11 + [vmem] * 4,
+        out_specs=[any_] * 7,
         out_shape=[
             jax.ShapeDtypeStruct((rows, d), F32),
             jax.ShapeDtypeStruct((rows, d), F32),
-            jax.ShapeDtypeStruct((dn, 2 * sz.di), F32),
+            jax.ShapeDtypeStruct((t, dn, cs), BF16),
+            jax.ShapeDtypeStruct((t, dn, cs), BF16),
             jax.ShapeDtypeStruct((dn, tl), F32),
             jax.ShapeDtypeStruct((on, d), F32),
             jax.ShapeDtypeStruct((total_rows, LANES), F32),
         ],
         scratch_shapes=[
-            v(3, rows, d), v(3, rows, d), v(fi, rows, d), v(fi, rows, d), v(2, rows, d), v(2, rows, d), v(rows, d), v(rows, d),
-            v(g, t, dn, 2 * cs), v(t, dn, 2 * cs), v(g, on, d), v(t, g, dn, tl), v(g, dn, tl), v(g, dn, tl), v(t, dn, 2 * cs),
-            pltpu.VMEM((g, sr, LANES), F32), pltpu.VMEM((sr, LANES), F32), pltpu.VMEM((t, sr, LANES), F32),
-            dma((2, 4, parts)), dma((2, fi, parts)), dma((2, 2, parts)), dma((2, 2, parts)), dma((2, parts)), dma((2, parts)),
-            dma((g, fi)), dma((g, fi)), dma((t,)), dma((t,)), dma((g,)), dma((g,)), dma((t, g)), dma((t, g)), dma((g,)), dma((g,)),
-            dma((g,)), dma((g,)), dma((t,)), dma((t,)), dma((1,)), dma((1,)),
+            b(d, t * rows), b(t, rows, d), f(2, max(3 * rows, -(-d // (2 * cs)) * rows), cs), f(2, rows, cs), f(2, rows, tl), b(n, dn, cs), b(n, dn, cs), b(n, dn, tl), b(g, on, d),
+            b(t, rows, cs), b(t, rows, cs), b(t, rows, tl), f(t, rows, cs),
+            b(4, rows, d), b(3, rows, d), b(2, rows, d), b(rows, d), b(4, rows, d), b(2, rows, d), b(rows, d), f(rows, d),
+            b(g, t, dn, max(cs, tl)), b(g, t, dn, cs), b(g, on, d), b(g + 1, t, dn, cs), b(g + 1, t, dn, cs), f(t, dn, cs),
+            b(t, dn, cs), b(t, dn, cs), b(t, dn, cs), b(t, dn, cs), b(g, on, d), f(on, d), b(t, g, dn, tl), b(g, dn, tl), b(g, dn, tl), f(dn, tl),
+            f(sr, LANES), f(g, sr, LANES), f(sr, LANES), f(t, sr, LANES), f(total_rows, LANES),
+            dma((6,)), dma((2,)), dma((2, 2)), *plane(), *plane(), dma((g,)), dma((g + 1,)), dma((g,)), dma((g + 1,)), dma((g,)), dma((g,)),
+            dma((2,)), dma((2,)), dma((1,)), dma((1,)), dma((1,)), dma((1,)), dma((2,)), dma((2,)), dma((7 + d // cs,)),
         ],
-        compiler_params=pltpu.CompilerParams(collective_id=2, has_side_effects=True, vmem_limit_bytes=63 << 20),
-        name="reduce",
-    )(hp, gp, dwzx, dwtl, dwo, sm)
+        compiler_params=pltpu.CompilerParams(collective_id=1, has_side_effects=True, vmem_limit_bytes=67043328),
+        name="back",
+    )(nt, go, px, pt, pz, y, gm, wx, wz, wt, wo, q, par, head, tile)
+
+
+def finish_kernel(sz, HS, GS, X, GO, RAZ, RAX, GTL, GOUT, gsm, WIN, norm, par, HID, GIN, gnorm, GW, gcw, gcb, ggate, GWO, gdecay, gbias, gskip,
+                  hs, gs, x, go, raz, rax, gtl, gout, win, hidden, gin, gw, sem):
+    me = Place(sz)
+    cs, T, taps = sz.cs, sz.t, sz.taps
+    tiles = cs // LANES
+    width = sz.small_rows - sz.common
+    loads = [pltpu.make_async_copy(src, dst, sem.at[k]) for k, (src, dst) in enumerate(
+        ((X, x), (HS, hs), (GS, gs), (GO, go), (GOUT, gout), (WIN, win), (RAZ, raz), (RAX, rax), (GTL, gtl)))]
+    for copy in loads:
+        copy.start()
+    saves = [pltpu.make_async_copy(src, dst, sem.at[9 + k]) for k, (src, dst) in enumerate(((hidden, HID), (gin, GIN), (gout, GWO), (gw, GW)))]
+    loads[0].wait()
+    loads[1].wait()
+    xb = x[...].astype(F32)
+    hidden[...] = (xb + hs[...]).astype(BF16)
+    saves[0].start()
+    loads[2].wait()
+    loads[3].wait()
+    scale = lax.rsqrt(jnp.mean(xb * xb, axis=1, keepdims=True) + EPS)
+    dxhat = gs[...] * par[taps + 2 : taps + 3, 0 : sz.d]
+    inner = jnp.mean(dxhat * xb, axis=1, keepdims=True)
+    gin[...] = go[...].astype(F32) + scale * (dxhat - xb * (scale * scale * inner))
+    saves[1].start()
+    loads[4].wait()
+    saves[2].start()
+    for copy in loads[5:]:
+        copy.wait()
+    dot = jnp.zeros((gw.shape[0], LANES), F32)
+    for side, ref in ((0, raz), (1, rax)):
+        for t in range(T):
+            at = side * sz.di + t * cs
+            piece = ref[t].astype(F32)
+            gw[:, at : at + cs] = piece
+            both = piece * win[:, at : at + cs].astype(F32)
+            for j in range(tiles):
+                dot = dot + both[:, j * LANES : (j + 1) * LANES]
+    at = 2 * sz.di
+    gw[:, at:] = gtl[:, 0 : sz.tail]
+    saves[3].start()
+    last = jnp.sum(gtl[:, 0 : sz.tail] * win[:, at:].astype(F32), axis=1, keepdims=True)
+    dot = jnp.sum(dot, axis=1, keepdims=True) + last
+    gnorm[...] = jnp.broadcast_to(dot, (dot.shape[0], LANES)).T[0:1, :] / norm[...].astype(F32)
+
+    def window(row_of, rows, per):
+        first = lax.div(me.i * per, LANES)
+        off = lax.rem(me.i * per, LANES)
+        wide = jnp.concatenate([gsm[pl.ds(row_of(first), rows), :], gsm[pl.ds(row_of(first + 1), rows), :]], axis=1)
+        return pltpu.roll(wide, lax.rem(2 * LANES - off, 2 * LANES), 1)
+
+    def conv_row(q):
+        q = jnp.clip(q, 0, T * tiles + 2 * sz.state // LANES - 1)
+        inside = sz.common + lax.div(q, tiles) * width + 8 * lax.rem(q, tiles)
+        return pl.multiple_of(jnp.where(q < T * tiles, inside, sz.at_bc + 8 * (q - T * tiles)), 8)
+
+    def gate_row(q):
+        q = jnp.clip(q, 0, T * tiles - 1)
+        return sz.common + lax.div(q, tiles) * width + sz.at_gate - sz.common + lax.rem(q, tiles)
+
+    conv = window(conv_row, 8, gcb.shape[1])
+    gcw[...] = conv[0:taps, 0 : gcw.shape[1]]
+    gcb[...] = conv[taps : taps + 1, 0 : gcb.shape[1]]
+
+    def spread(q):
+        return jnp.broadcast_to(gsm[pl.ds(gate_row(q), 1), :], (8, LANES))
+
+    first, off = lax.div(me.i * ggate.shape[1], LANES), lax.rem(me.i * ggate.shape[1], LANES)
+    wide = jnp.concatenate([spread(first), spread(first + 1)], axis=1)
+    ggate[...] = pltpu.roll(wide, lax.rem(2 * LANES - off, 2 * LANES), 1)[0:1, 0 : ggate.shape[1]]
+    for t in range(T):
+        row = sz.common + t * width + sz.at_head - sz.common
+        for k, ref in enumerate((gdecay, gbias, gskip)):
+            ref[:, t * sz.nh : (t + 1) * sz.nh] = gsm[row + k : row + k + 1, 0 : sz.nh]
+    for copy in saves:
+        copy.wait()
+
+
+def run_finish(sz, hs, gs, x, go, raz, rax, gtl, gout, gsm, win, norm, par, kn, cn):
+    vmem, any_ = pl.BlockSpec(memory_space=pltpu.VMEM), pl.BlockSpec(memory_space=pltpu.HBM)
+    o = lambda *s: jax.ShapeDtypeStruct(s, F32)
+    dn = win.shape[0]
+    same = lambda a: pltpu.VMEM(a.shape, a.dtype)
+    return pl.pallas_call(
+        functools.partial(finish_kernel, sz),
+        in_specs=[any_] * 8 + [vmem, any_, vmem, vmem],
+        out_specs=[any_, any_, vmem, any_, vmem, vmem, vmem, any_, vmem, vmem, vmem],
+        out_shape=[jax.ShapeDtypeStruct(x.shape, BF16), o(*x.shape), o(1, dn), o(*win.shape), o(sz.taps, cn), o(1, cn), o(1, kn), o(*gout.shape),
+                   o(1, sz.heads), o(1, sz.heads), o(1, sz.heads)],
+        scratch_shapes=[same(hs), same(gs), same(x), same(go), same(raz), same(rax), same(gtl), same(gout), same(win),
+                        same(x), same(gs), pltpu.VMEM(win.shape, F32), pltpu.SemaphoreType.DMA((13,))],
+        compiler_params=pltpu.CompilerParams(vmem_limit_bytes=67043328),
+        name="finish",
+    )(hs, gs, x, go, raz, rax, gtl, gout, gsm, win, norm, par)
 
 
 def sizes(mesh, hidden, lengths, in_proj, conv_weight, gate_gain, decay_log):
@@ -1063,49 +1303,19 @@
 
 def local(mesh, hidden_in, lengths, norm_gain, in_proj, conv_weight, conv_bias, gate_gain, out_proj, decay_log, step_bias, skip_gain, grad_out):
     sz = sizes(mesh, hidden_in, lengths, in_proj, conv_weight, gate_gain, decay_log)
-    n, t, cs, di = sz.n, sz.t, sz.cs, sz.di
-    f, p = lax.axis_index("fsdp"), lax.axis_index("dp")
-    index = f * sz.p + p
+    di = sz.di
     dn, cn, kn = norm_gain.shape[0], conv_bias.shape[0], gate_gain.shape[0]
 
     tail = jnp.pad(in_proj[:, 2 * di :], ((0, 0), (0, sz.tl - sz.tail)))
     row = lambda a: a.reshape(1, -1)
-    nrm, go_all, px, pt, pz, y, gm, wx, wz, wt, wo, q, par, head, tile = run_front(
+    turned, go_all, px, pt, pz, y, gm, wx, wz, wt, wo, q, par, head, tile = run_front(
         sz, hidden_in, grad_out, in_proj, tail, out_proj, row(norm_gain), conv_weight.T, row(conv_bias), row(gate_gain), lengths,
         row(decay_log), row(step_bias), row(skip_gain))
-    wx, wz, wt, wo = wx.reshape(sz.d, cs), wz.reshape(sz.d, cs), wt.reshape(sz.d, sz.tl), wo.reshape(cs, sz.d)
-    gain = par[sz.taps + 2 : sz.taps + 3]
-    mix, hid, dz, dx, dtl, gn, small = run_bwd(sz, nrm, px, pt, pz, y, gm, q, wx, wz, wt, wo, par, head, tile)
-
-    tall = lambda a: a.reshape(t * sz.rows, a.shape[2])
-    dwzx = jnp.concatenate([tn(tall(nrm), tall(a)).astype(BF16) for a in (dz, dx)], axis=1).reshape(n, dn, 2 * cs)
-    dwtl = tn(tall(nrm), tall(dtl)).astype(BF16).reshape(n, dn, sz.tl)
-    dwo = tn(tall(mix), tall(go_all)).astype(BF16).reshape(sz.g, cs // sz.g, sz.d)
-    hsum, gsum, gin, gtl, gout, gsm = run_reduce(sz, hid, gn, dwzx, dwtl, dwo, small)
-
-    x = hidden_in.astype(F32)
-    hidden_out = (x + hsum).astype(BF16)
-    scale = lax.rsqrt(jnp.mean(x * x, axis=1, keepdims=True) + EPS)
-    dxhat = gsum * gain
-    inner = jnp.mean(dxhat * x, axis=1, keepdims=True)
-    grad_in = grad_out.astype(F32) + scale * (dxhat - x * (scale * scale * inner))
-    grad_in_proj = jnp.concatenate([gin, gtl[:, : sz.tail]], axis=1)
-
-    own = lambda a, width: lax.dynamic_slice_in_dim(a, index * width, width)
-    common, slices = gsm[: sz.common], gsm[sz.common :].reshape(t, -1, LANES)
-    at = lambda place: place - sz.common
-    grad_norm_gain = own(common[: sz.d // LANES].reshape(-1), dn)
-    conv_x = slices[:, : at(sz.at_gate)].reshape(-1, 8, LANES)
-    conv = jnp.concatenate([conv_x, common[sz.at_bc :].reshape(-1, 8, LANES)])
-    conv = conv[:, : sz.taps + 1].transpose(0, 2, 1).reshape(sz.conv, sz.taps + 1)
-    conv = own(conv, cn)
-    tiles = cs // LANES
-    grad_gate = own(slices[:, at(sz.at_gate) : at(sz.at_gate) + tiles].reshape(-1), kn)
-    heads = slices[:, at(sz.at_head) :]
-    grad_decay = heads[:, 0, : sz.nh].reshape(-1)
-    grad_bias = heads[:, 1, : sz.nh].reshape(-1)
-    grad_skip = jnp.sum(heads[:, 3 : 3 + tiles].reshape(sz.heads, sz.hd), axis=1)
-    return (hidden_out, grad_in, grad_norm_gain, grad_in_proj, conv[:, : sz.taps], conv[:, sz.taps], grad_gate, gout, grad_decay, grad_bias, grad_skip)
+    hs, gs, raz, rax, gtl, gout, gsm = run_back(sz, turned, go_all, px, pt, pz, y, gm, wx, wz, wt, wo, q, par, head, tile)
+    hidden, gin, gnorm, gw, gcw, gcb, ggate, gwo, gdecay, gbias, gskip = run_finish(
+        sz, hs, gs, hidden_in, grad_out, raz, rax, gtl, gout, gsm, in_proj, row(norm_gain), par, kn, cn)
+    flat = lambda a: a.reshape(-1)
+    return hidden, gin, flat(gnorm), gw, gcw.T, flat(gcb), flat(ggate), gwo, flat(gdecay), flat(gbias), flat(gskip)
 
 
 def solution(mesh):

time: 276 us -> 217 us (0.79)
  Pallas kernels: 237 us -> 213 us
  matrix products: 16.9 us -> 0 us
  local copies, waits for them, and re-layouts: 15.8 us -> 1.4 us
  other arithmetic: 5.18 us -> 0 us
    pallas_call x2, Pallas kernels: 149 us -> 122 us  [the longest x1 116 us: run_back(): pl.pallas_call(functools.partial(back_kernel, sz), in_specs=[any_] * 11 +...]
    dot_general x4 -> x0, matrix products: 16.9 us -> none  [tn(): lax.dot_general(a, b, (((0,), (0,)), ((), ())), preferred_element_type=F32)]
    slice x6 -> x0, local copies, waits for them, and re-layouts: 4.22 us -> none  [the longest x1 1.02 us: local(): common, slices = (gsm[:sz.common], gsm[sz.common:].reshape(t, -1, LANES))]
where the time goes in v3:
time: 217 us; the launch traced here: 215 us
  Pallas kernels  213 us (98%)
    pallas_call x1, Pallas kernels, run_back(): pl.pallas_call(functools.partial(back_kernel, sz), in_specs=[any_] * 11 +...  116 us
    pallas_call x1, Pallas kernels, run_front(): pl.pallas_call(functools.partial(front_kernel, sz), in_specs=[any_] * 5 +...  90.9 us
    pallas_call x1, Pallas kernels, run_finish(): pl.pallas_call(functools.partial(finish_kernel, sz), in_specs=[any_] * 8...  6.3 us

profile of v3, /device:TPU:0, one launch (start us, length us, event | category | flops | bytes accessed | tf_op | source)
XLA Modules:
  0.0 215.4 jit_solution(7757739156882184350)
XLA Ops:
  0.6 0.8 slice.3
  1.4 0.6 pad.4.tail
  2.0 90.9 %front.1 = (bf16[1536,2048]{1,0:T(8,128)(2,1)}, bf16[8,256,1536]{2,1,0:T(8,128)(2,1)}, f32[8,256,384]{2,1,0:T(8,128)}, f32[8,256,384]{2,1,0:T(8,128)}, f32[8,256...) custom-call(bf16[256,1536]{1,0:T(8,128)(2,1)} %X.1, ...), custom_call_target="tpu_custom_call" | custom-call | tf_op jit(solution)/shard_map/front/pallas_call | solution.py:634
  92.9 116.0 %back.1 = (f32[256,1536]{1,0:T(8,128)}, f32[256,1536]{1,0:T(8,128)}, bf16[8,48,384]{2,1,0:T(8,128)(2,1)}, bf16[8,48,384]{2,1,0:T(8,128)(2,1)}, f32[48,384]{1,0:T...) custom-call(bf16[1536,2048]{1,0:T(8,128)(2,1)} %get-tuple-element.44.NT, bf16[8,256,1536]{2,1,0:T(8,128)(2,1)} %get-tuple-element.45.GO, ...), custom_call_target="tpu_custom_call" | custom-call | tf_op jit(solution)/shard_map/back/pallas_call | solution.py:1157
  208.9 6.3 %finish.1 = (bf16[256,1536]{1,0:T(8,128)(2,1)}, f32[256,1536]{1,0:T(8,128)}, f32[1,48]{1,0:T(1,128)}, f32[48,6448]{1,0:T(8,128)}, f32[4,104]{1,0:T(4,128)}, /*in...) custom-call(f32[256,1536]{1,0:T(8,128)} %get-tuple-element.59.HS, ...), custom_call_target="tpu_custom_call" | custom-call | tf_op jit(solution)/shard_map/finish/pallas_call | solution.py:1266

commit v4 on v3

--- a/solution.py
+++ b/solution.py
@@ -13,6 +13,7 @@
 BF16 = jnp.bfloat16
 EXACT = lax.Precision.HIGHEST
 LANES = 128
+LOG2E = math.log2(math.e)
 
 
 def nn(a, b):
@@ -51,6 +52,13 @@
     ah, al = split(a)
     bh, bl = split(b)
     return product(ah, bh) + (product(ah, bl) + product(al, bh))
+
+
+def running(mask, a):
+    hi, mid = split(a)
+    rest = a - hi.astype(F32) - mid.astype(F32)
+    ones = jnp.where(mask, 1.0, 0.0).astype(BF16)
+    return nn(ones, hi) + (nn(ones, mid) + nn(ones, rest.astype(BF16)))
 
 
 class Sizes:
@@ -279,6 +287,7 @@
     tails_of = lambda s, k: [wtv.at[index_of(sz, jnp.int32(g), s)] for g in range(G)]
     gt = PlaneGather(sz, me, 1, lambda k: tails_of(me.t, k), tails_of, wtv.at[pl.ds(0, G)], wtv.at[pl.ds(0, (T - 1) * G)], wsend, wrecv)
 
+    gx.start(0)
     owner_t, piece = lax.div(me.i, G), lax.rem(me.i, G)
 
     def out_copy(g):
@@ -360,7 +369,8 @@
     for step in range(1, T):
         pack_plane(step).start()
     gt.start(0)
-    gx.start(0)
+    for step in range(1, T):
+        exchange(0, step).start()
 
     def arrive(half):
         wv, _, recv = ((wzv, azsend, azrecv), (wxv, axsend, axrecv))[half]
@@ -393,11 +403,6 @@
 
     arrive(1)
     advance(1, 0)
-    gt.relay(0)
-    for step in range(1, T):
-        exchange(0, step).start()
-    for p in range(1, sz.parts):
-        gx.start(p)
     advance(1, 1)
     landed(smv.at[pl.ds(0, (T - 1) * G)], srecv.at[1])
     packed = smv[...]
@@ -426,6 +431,9 @@
         for p in range(sz.parts):
             gather.arrived(slot, p)
 
+    gt.relay(0)
+    for p in range(1, sz.parts):
+        gx.start(p)
     normalize(jnp.int32(0))
     wait_pair(gx, jnp.int32(1))
     normalize(jnp.int32(1))
@@ -436,10 +444,6 @@
     advance(0, 0)
     gt.relay_far(0)
     advance(1, G - 1)
-    for p in range(1, sz.parts):
-        gx.relay(p)
-    for p in range(sz.parts):
-        gg.start(p)
     for fi in (me.fi, me.fa, me.fb, me.fd):
         gt.arrived(fi * 2 + me.other, 0)
 
@@ -463,19 +467,21 @@
         pxv = nn(nrm, wxv[...].reshape(sz.d, cs))
         ptl = nn(nrm, wtv[...].reshape(sz.d, sz.tl))
         px[slot] = pxv
-        pt[slot] = ptl
         pltpu.make_async_copy(px.at[slot], PX.at[slot], esem.at[1]).start()
-        pltpu.make_async_copy(pt.at[slot], PT.at[slot], esem.at[2]).start()
 
         def act(u, at):
             return jax.nn.silu(conv_tile(u, par[0:taps, at : at + LANES], par[taps : taps + 1, at : at + LANES], keeps, taps))
 
         bm = act(ptl[:, 0:st], cs)
         cm = act(ptl[:, st : 2 * st], cs + st)
-        raw = pltpu.roll(ptl[:, 2 * st : 2 * st + LANES], lead, 1)
-        dt = softplus(raw + head[0:1, :])
+        raw = pltpu.roll(ptl[:, 2 * st : 2 * st + LANES], lead, 1) + head[0:1, :]
+        dt = softplus(raw)
         rate = -jnp.exp(head[1:2, :])
-        log_decay = jnp.dot(tri.astype(F32), dt * rate, precision=EXACT, preferred_element_type=F32)
+        log_decay = running(tri, dt * rate) * LOG2E
+        pt[slot, :, 0 : 2 * st] = ptl[:, 0 : 2 * st]
+        for a, kept in enumerate((raw, dt, log_decay)):
+            pt[slot, :, 2 * st + a * LANES : 2 * st + (a + 1) * LANES] = kept
+        pltpu.make_async_copy(pt.at[slot], PT.at[slot], esem.at[2]).start()
         log_t = log_decay.T
         drop = jnp.where(same & tri, 0.0, -jnp.inf)
         inner = three(nt, cm, bm)
@@ -491,7 +497,7 @@
                 xm = jnp.where(mine, xd, 0.0).astype(BF16)
                 for r, wide, into in ((slice(0, half_rows), half_rows, tops), (slice(half_rows, rows), rows, bottoms)):
                     spread = log_decay[r, h : h + 1] - log_t[h : h + 1, 0:wide]
-                    f = (jnp.exp(spread + drop[r, 0:wide]) * inner[r, 0:wide]).astype(BF16)
+                    f = (jnp.exp2(spread + drop[r, 0:wide]) * inner[r, 0:wide]).astype(BF16)
                     into.append(nn(f, xm[0:wide]))
             y = jnp.concatenate([tops[0] + tops[1], bottoms[0] + bottoms[1]], axis=0)
             skip2 = jnp.where(low[0:1], head[2:3, 2 * j : 2 * j + 1], head[2:3, 2 * j + 1 : 2 * j + 2])
@@ -514,14 +520,15 @@
 
     @pl.loop(0, T)
     def _(k):
-        between(k == 1, lambda: advance(0, 1), lambda: out_steps(0))
-        between(k == 2, lambda: gx.relay_far(0))
-        between(k == 4, lambda: [gx.relay_far(p) for p in range(1, sz.parts)], lambda: [advance(0, step) for step in range(2, G - 1)])
-        between(k == 5, lambda: gg.relay(0))
-        between(k == 6, lambda: [gg.relay(p) for p in range(1, sz.parts)], lambda: out_steps(1))
-        between(k == 7, lambda: advance(0, G - 1))
+        between(k == 2, lambda: advance(0, 1), lambda: out_steps(0), lambda: [gx.relay(p) for p in range(1, sz.parts)],
+                lambda: [gg.start(p) for p in range(sz.parts)])
+        between(k == 3, lambda: gx.relay_far(0))
+        between(k == 4, lambda: [advance(0, step) for step in range(2, G - 1)])
+        between(k == 6, lambda: [gx.relay_far(p) for p in range(1, sz.parts)], lambda: out_steps(1))
+        between(k == 7, lambda: [gg.relay(p) for p in range(sz.parts)])
         scan(k)
 
+    advance(0, G - 1)
     out_steps(*range(2, G - 1))
     save(4)
 
@@ -531,8 +538,6 @@
         pz[slot] = nn(nv[slot], wzv[...].reshape(sz.d, cs))
         pltpu.make_async_copy(pz.at[slot], PZ.at[slot], esem.at[4]).start()
 
-    for p in range(sz.parts):
-        gg.relay_far(p)
     out_steps(G - 1)
     if not sz.aligned:
         for k in range(G):
@@ -546,6 +551,7 @@
     def _(k):
         slot = slot_of(me, k)
 
+        between(k == 6, lambda: [gg.relay_far(p) for p in range(sz.parts)])
         between(lax.rem(k, 2) == 1, lambda: wait_pair(gg, k))
         pos = iota((rows, LANES), 0).astype(F32)
         seg = segments(pos, ends_of(smv[slot * G + me.g, taps + 3 : taps + 4, :], sz.seqs))
@@ -625,7 +631,7 @@
     vmem = pl.BlockSpec(memory_space=pltpu.VMEM)
     dma = pltpu.SemaphoreType.DMA
     shapes = dict(
-        nrm=((t, rows, d), BF16), nt=((d, t * rows), BF16), go=((t, rows, d), BF16), px=((t, rows, cs), F32), pt=((t, rows, tl), F32), pz=((t, rows, cs), F32),
+        nrm=((t, rows, d), BF16), nt=((d, t * rows), BF16), go=((t, rows, d), BF16), px=((t, rows, cs), F32), pt=((t, rows, 2 * sz.state + 3 * LANES), F32), pz=((t, rows, cs), F32),
         y=((t, rows, cs), F32), gm=((t, rows, cs), F32), wx=((n, dn, cs), BF16), wz=((n, dn, cs), BF16), wt=((n, dn, tl), BF16),
         wo=((g, on, d), BF16), q=((2 * t, rows), F32), par=((8, d), F32), head=((8, LANES), F32), tile=((t, 8, LANES), F32),
     )
@@ -652,6 +658,9 @@
     def __init__(self, sz, me, own, recv, send_sem, recv_sem):
         self.sz, self.me, self.own, self.recv, self.send_sem, self.recv_sem = sz, me, own, recv, send_sem, recv_sem
 
+    def piece(self, p):
+        return self.own.at[pl.ds(p * self.sz.t, self.sz.t)]
+
     def leg(self, step, up):
         g, last = self.me.g, self.sz.g - 1
         late = step - g if up else step - (last - g)
@@ -661,7 +670,7 @@
         inner = (g > 0) if up else (g < last)
         nxt = jnp.clip(g + 1 if up else g - 1, 0, last)
         there = p if up else jnp.where(p == nxt, last + 1, p)
-        copy = lambda: remote(self.sz, self.own.at[p], self.recv.at[there], self.send_sem.at[p], self.recv_sem.at[there], nxt, self.me.t)
+        copy = lambda: remote(self.sz, self.piece(p), self.recv.at[there], self.send_sem.at[p], self.recv_sem.at[there], nxt, self.me.t)
         return p, moves, inner, copy
 
     def step(self, step):
@@ -671,7 +680,8 @@
             @pl.when(moves & inner)
             def _(p=p):
                 landed(self.recv.at[p], self.recv_sem.at[p])
-                self.own[p] = (self.own[p].astype(F32) + self.recv[p].astype(F32)).astype(BF16)
+                piece = self.piece(p)
+                piece[...] = (piece[...].astype(F32) + self.recv[p].astype(F32)).astype(BF16)
 
             @pl.when(moves)
             def _(copy=copy):
@@ -679,7 +689,7 @@
 
     def total(self, acc):
         g = self.me.g
-        acc[...] = self.own[g].astype(F32)
+        acc[...] = self.piece(g)[...].astype(F32)
         for k, there in ((g, g > 0), (self.sz.g, g < self.sz.g - 1)):
             @pl.when(there)
             def _(k=k):
@@ -759,16 +769,18 @@
         for w in range(4):
             self.put0(w).wait_send()
 
-    def sent(self):
+    def sent1(self):
         for w in range(2):
             self.put1(w).wait_send()
+
+    def sent2(self):
         self.put2().wait_send()
 
 
 def back_kernel(sz, NT, GO, PX, PT, PZ, Y, GM, WX, WZ, WT, WO, q_ref, par, head, tile_ref,
                 HS, GS, RAZ, RAX, GTL, GOUT, GSM,
-                nt_, gov, ra, rx, rt_, wx, wz, wt, wo, mix, dz, dtv, dyv, r0h, sh, r1h, r2h, r0g, r1g, r2g, gs,
-                dwz, dwx, dwo, rzz, rzx, acc, szz, szx, raz, rax, ro, gout, rtt, st, rtz, gtl, small, rs1, s1, rs2, gsm,
+                nt_, gov, ra, rx, rt_, wall, wo, dp, dyv, r0h, r1h, r2h, r0g, r1g, r2g, gs,
+                dwz, dwx, dwo, rzz, rzx, acc, szz, raz, rax, ro, gout, rtp, rtt, st, rtz, gtl, small, rs1, s1, rs2, gsm,
                 lsem, asem, bsem, h0s, h0r, h1s, h1r, h2s, h2r, g0s, g0r, g1s, g1r, g2s, g2r, zzs, zzr, zxs, zxr, os_, or_, as_, ar_, ts, tr, us, ur, ss, sr, wsem):
     me = Place(sz)
     rows, cs, st_dim, taps, T, G, d = sz.rows, sz.cs, sz.state, sz.taps, sz.t, sz.g, sz.d
@@ -781,8 +793,7 @@
         there = lax.rem(me.i + step, sz.n)
         pl.semaphore_signal(barrier, inc=1, device_id=(lax.div(there, sz.p), lax.rem(there, sz.p)), device_id_type=pl.DeviceIdType.MESH)
 
-    stage = gov.at[pl.ds(0, 4)]
-    dx = mix
+    stage, sums = gov.at[pl.ds(0, 4)], gov.at[pl.ds(4, 3)]
     pieces = d // cs
 
     class Folded:
@@ -794,11 +805,11 @@
                 part = value[:, c * cs : (c + 1) * cs]
                 self.at(c)[...] = self.at(c)[...] + part if more else part
 
-    hid = PlaneReduce(sz, me, stage, r0h, sh, r1h, r2h, Folded().put, (h0s, h0r, h1s, h1r, h2s, h2r))
+    hid = PlaneReduce(sz, me, stage, r0h, sums, r1h, r2h, Folded().put, (h0s, h0r, h1s, h1r, h2s, h2r))
     def put_gs(value, more):
         gs[...] = gs[...] + value if more else value
 
-    gn = PlaneReduce(sz, me, stage, r0g, gov.at[pl.ds(4, 3)], r1g, r2g, put_gs, (g0s, g0r, g1s, g1r, g2s, g2r))
+    gn = PlaneReduce(sz, me, stage, r0g, sums, r1g, r2g, put_gs, (g0s, g0r, g1s, g1r, g2s, g2r))
 
     def fetch_a(k):
         slot, par_ = hid.slot(k), lax.rem(k, 2)
@@ -811,9 +822,8 @@
     for k in range(2):
         for copy in fetch_a(jnp.int32(k)):
             copy.start()
-    loads = [pltpu.make_async_copy(src, dst, lsem.at[k]) for k, (src, dst) in enumerate(((NT, nt_), (WO, wo), (GO, gov), (WX, wx), (WZ, wz), (WT, wt)))]
-    for copy in loads[:1]:
-        copy.start()
+    loads = [pltpu.make_async_copy(src, dst, lsem.at[k]) for k, (src, dst) in enumerate((
+        (NT, nt_), (WO, wo), (GO, gov), (WX, wall.at[:, :, pl.ds(cs, cs)]), (WZ, wall.at[:, :, pl.ds(0, cs)]), (WT, wall.at[:, :, pl.ds(2 * cs, sz.tl)])))]
     for copy in fetch_b(jnp.int32(0)):
         copy.start()
     small[...] = jnp.zeros(small.shape, F32)
@@ -825,14 +835,19 @@
         s = jax.nn.sigmoid(v)
         return v * s, s * (1.0 + v * (1.0 - s))
 
+    def between(k, *steps):
+        @pl.when(k)
+        def _():
+            for step in steps:
+                step()
+
     @pl.loop(0, T)
     def _(k):
         slot, par_ = hid.slot(k), lax.rem(k, 2)
 
         @pl.when(k == T // 2)
         def _():
-            for copy in loads[1:]:
-                copy.start()
+            loads[0].start()
 
         landed(ra.at[par_, pl.ds(0, 3 * rows)], asem.at[par_])
         pos = iota((rows, LANES), 0).astype(F32)
@@ -842,17 +857,18 @@
         scale = lax.rsqrt(q1 / sz.di + EPS)
         pull = scale * scale * scale * q2 / sz.di
         for j in range(tiles):
-            tile = slice(j * LANES, (j + 1) * LANES)
+            at = j * LANES
+            tile = slice(at, at + LANES)
             zt, y, gm = (ra[par_, a * rows : (a + 1) * rows, tile] for a in range(3))
             gm = gm * valid
             gate = par[taps + 1 : taps + 2, tile]
             up, slope = silu_pair(zt)
             gated = y * up
             unit = gated * scale
-            mix[slot, :, tile] = (unit * gate * valid).astype(BF16)
+            dp[slot, :, cs + at : cs + at + LANES] = (unit * gate * valid).astype(BF16)
             small[sz.at_gate + j : sz.at_gate + j + 1, :] += colsum(gm * unit)
             dgated = scale * gm * gate - gated * pull
-            dz[slot, :, tile] = (dgated * y * slope).astype(BF16)
+            dp[slot, :, tile] = (dgated * y * slope).astype(BF16)
             dyv[slot, :, tile] = dgated * up
 
         @pl.when(k + 2 < T)
@@ -860,20 +876,26 @@
             for copy in fetch_a(k + 2):
                 copy.start()
 
-    def weight_grad(values, into):
+    for copy in loads[1:3]:
+        copy.start()
+
+    def weight_grad(first, wide, into, place):
         dn = sz.d // sz.n
         for at in range(0, sz.n, sz.n // 4):
             span = sz.n // 4 * dn
-            got = nn(nt_[at * dn : at * dn + span, :], values[...].reshape(T * rows, values.shape[2]))
+            got = nn(nt_[at * dn : at * dn + span, :], dp[:, :, first : first + wide].reshape(T * rows, wide))
             for i in range(at, at + sz.n // 4):
                 f, p = i // sz.p, i % sz.p
                 fo, fi, z, c = f // sz.fi, f % sz.fi, p // 2, p % 2
-                into[fo * sz.z + z, fi * 2 + c, :, 0 : got.shape[1]] = got[(i - at) * dn : (i - at + 1) * dn].astype(BF16)
-
-    line_z = LineReduce(sz, me, dwz.at[:, :, :, pl.ds(0, cs)], rzz, zzs, zzr)
+                into[place(fo * sz.z + z, fi * 2 + c), :, 0:wide] = got[(i - at) * dn : (i - at + 1) * dn].astype(BF16)
+
+    line_z = LineReduce(sz, me, dwz.at[:, :, pl.ds(0, cs)], rzz, zzs, zzr)
     line_x = LineReduce(sz, me, dwx, rzx, zxs, zxr)
     loads[0].wait()
-    weight_grad(dz, dwz)
+    by_plane, by_rank = lambda g, t: g * T + t, lambda g, t: t * G + g
+    weight_grad(0, cs, dwz, by_plane)
+    for copy in loads[3:]:
+        copy.start()
     pl.semaphore_wait(barrier, sz.n - 1)
     line_z.step(0)
     loads[1].wait()
@@ -886,7 +908,7 @@
                                             device_id=(lax.div(owner, sz.p), lax.rem(owner, sz.p)), device_id_type=pl.DeviceIdType.MESH)
 
     for at in range(0, d, d // 3):
-        got = tn(mix[...].reshape(T * rows, cs), gov[:, :, at : at + d // 3].reshape(T * rows, d // 3))
+        got = tn(dp[:, :, cs : 2 * cs].reshape(T * rows, cs), gov[:, :, at : at + d // 3].reshape(T * rows, d // 3))
         for k in range(G):
             dwo[k, :, at : at + d // 3] = got[k * (cs // G) : (k + 1) * (cs // G)].astype(BF16)
     def out_sends():
@@ -897,7 +919,7 @@
 
     @pl.loop(0, T)
     def _(k):
-        hid.block(k, nn(mix[hid.slot(k)], wo[...].reshape(cs, d)))
+        hid.block(k, nn(dp[hid.slot(k), :, cs : 2 * cs], wo[...].reshape(cs, d)))
 
     for copy in loads[3:]:
         copy.wait()
@@ -906,12 +928,6 @@
     lane = iota((rows, LANES), 1)
     lead = lax.rem(LANES - sz.nh * me.t, LANES)
     quads = ((slice(0, half), slice(0, rows)), (slice(half, rows), slice(half, rows)))
-
-    def between(k, *steps):
-        @pl.when(k)
-        def _():
-            for step in steps:
-                step()
 
     def scan_back(k):
         slot, par_ = gn.slot(k), lax.rem(k, 2)
@@ -945,10 +961,8 @@
         ub, uc = rt_[par_, :, 0:st_dim], rt_[par_, :, st_dim : 2 * st_dim]
         bm, bslope = silu_pair(conv_pre(ub, cs))
         cm, cslope = silu_pair(conv_pre(uc, cs + st_dim))
-        raw = pltpu.roll(rt_[par_, :, 2 * st_dim : 2 * st_dim + LANES], lead, 1) + head[0:1, :]
-        dt = softplus(raw)
+        raw, dt, log_decay = (rt_[par_, :, 2 * st_dim + a * LANES : 2 * st_dim + (a + 1) * LANES] for a in range(3))
         rate = -jnp.exp(head[1:2, :])
-        log_decay = jnp.dot(triangle(rows).astype(F32), dt * rate, precision=EXACT, preferred_element_type=F32)
         log_t = log_decay.T
         upper = iota((rows, rows), 1) >= iota((rows, rows), 0)
         drop = jnp.where(same & upper, 0.0, -jnp.inf)
@@ -956,8 +970,8 @@
         dcb = [jnp.zeros((half, rows), F32), jnp.zeros((half, half), F32)]
         ddt = jnp.zeros((rows, LANES), F32)
         cols = jnp.zeros((rows, LANES), F32)
-        rowsums = jnp.zeros((LANES, rows), F32)
-        lane_row = iota((LANES, rows), 0)
+        rowsums = jnp.zeros((up8(sz.nh), rows), F32)
+        lane_row = iota((up8(sz.nh), rows), 0)
         for j in range(tiles):
             at = j * LANES
             tile = slice(at, at + LANES)
@@ -968,16 +982,19 @@
             dt2 = jnp.where(low, dt[:, 2 * j : 2 * j + 1], dt[:, 2 * j + 1 : 2 * j + 2])
             xd = xa * dt2
             dyh, dyl = split(dy)
+            xh, xl = split(xd)
+            left = jnp.concatenate([xh, xl, xh], axis=1)
+            none = jnp.zeros((), BF16)
             tops = []
             for e in range(2):
                 h = 2 * j + e
                 mine = low if e == 0 else jnp.logical_not(low)
-                xh, xl = split(jnp.where(mine, xd, 0.0))
-                dym = jnp.where(mine, dy, 0.0).astype(BF16)
+                dym, dyr = jnp.where(mine, dyh, none), jnp.where(mine, dyl, none)
+                right = jnp.concatenate([dym, dym, dyr], axis=1)
                 parts, psums, tsum = [], [], []
                 for quad, (r, c) in enumerate(quads):
-                    decay = jnp.exp(log_t[h : h + 1, c] - log_decay[r, h : h + 1] + drop[r, c])
-                    df = (nt(xh[r], dyh[c]) + (nt(xh[r], dyl[c]) + nt(xl[r], dyh[c]))) * decay
+                    decay = jnp.exp2(log_t[h : h + 1, c] - log_decay[r, h : h + 1] + drop[r, c])
+                    df = nt(left[r], right[c]) * decay
                     dcb[quad] = dcb[quad] + df
                     p = df * inner_t[r, c]
                     psums.append(jnp.sum(p, axis=1, keepdims=True))
@@ -992,32 +1009,35 @@
             ddt = jnp.where(lane == 2 * j, jnp.sum(jnp.where(low, both, 0.0), axis=1, keepdims=True), ddt)
             ddt = jnp.where(lane == 2 * j + 1, jnp.sum(jnp.where(low, 0.0, both), axis=1, keepdims=True), ddt)
             skip2 = jnp.where(low[0:1], head[2:3, 2 * j : 2 * j + 1], head[2:3, 2 * j + 1 : 2 * j + 2])
-            dx[slot, :, tile] = conv_back(ux, dxd * dt2 + dy * skip2, xslope, at).astype(BF16)
-
-        ga = jnp.dot(upper.astype(F32), rowsums.T - cols, precision=EXACT, preferred_element_type=F32)
+            dp[slot, :, cs + at : cs + at + LANES] = conv_back(ux, dxd * dt2 + dy * skip2, xslope, at).astype(BF16)
+
+        rowsums = jnp.concatenate([rowsums, jnp.zeros((LANES - up8(sz.nh), rows), F32)], axis=0)
+        ga = running(upper, rowsums.T - cols)
         ddt = ddt + ga * rate
         small[sz.at_head : sz.at_head + 1, :] += rate * colsum(ga * dt)
         draw = jnp.where(lane < sz.nh, ddt * jax.nn.sigmoid(raw), 0.0)
         small[sz.at_head + 1 : sz.at_head + 2, :] += colsum(draw)
-        dtv[slot, :, 2 * st_dim : 2 * st_dim + LANES] = pltpu.roll(draw, sz.nh * me.t, 1).astype(BF16)
+        dp[slot, :, 2 * cs + 2 * st_dim : 2 * cs + 2 * st_dim + LANES] = pltpu.roll(draw, sz.nh * me.t, 1).astype(BF16)
         top, bottom = dcb[0].astype(BF16), dcb[1].astype(BF16)
         bb, cb = bm.astype(BF16), cm.astype(BF16)
         db = jnp.concatenate([nn(top, cb), nn(bottom, cb[half:])], axis=0)
         dc = tn(top, bb[:half]) + jnp.concatenate([jnp.zeros((half, st_dim), F32), tn(bottom, bb[half:])], axis=0)
-        dtv[slot, :, 0:st_dim] = conv_back(ub, db, bslope, cs).astype(BF16)
-        dtv[slot, :, st_dim : 2 * st_dim] = conv_back(uc, dc, cslope, cs + st_dim).astype(BF16)
+        dp[slot, :, 2 * cs : 2 * cs + st_dim] = conv_back(ub, db, bslope, cs).astype(BF16)
+        dp[slot, :, 2 * cs + st_dim : 2 * cs + 2 * st_dim] = conv_back(uc, dc, cslope, cs + st_dim).astype(BF16)
         between(k == 0, hid.sent0)
-        gn.block(k, nt(dz[slot], wz[...].reshape(d, cs)) + nt(dx[slot], wx[...].reshape(d, cs)) + nt(dtv[slot], wt[...].reshape(d, sz.tl)))
+        between(k == 4, hid.sent1)
+        between(k == 6, hid.sent2)
+        gn.block(k, nt(dp[slot], wall[...].reshape(d, 2 * cs + sz.tl)))
 
     @pl.loop(0, T)
     def _(k):
         between(k == 0, lambda: line_z.step(1))
-        between(k == 1, lambda: [line_z.step(step) for step in range(2, G - 1)], out_sends)
-        between(k == 3, hid.middle)
-        between(k == 6, hid.finish)
+        between(k == 2, lambda: [line_z.step(step) for step in range(2, G - 1)], out_sends)
+        between(k == 4, hid.middle)
+        between(k == 7, hid.finish)
         scan_back(k)
 
-    weight_grad(dx, dwx)
+    weight_grad(cs, cs, dwx, by_plane)
     line_x.step(0)
     line_z.total(acc)
     szz[...] = acc[...].astype(BF16)
@@ -1030,16 +1050,13 @@
 
     hand(szz, raz, 0)
     line_z.sent()
-    dwt = dwz.at[:, :, :, pl.ds(0, sz.tl)]
-    weight_grad(dtv, dwz)
-
-    def t_copy(step):
-        there = lax.rem(me.t + step, T)
-        return [remote(sz, dwt.at[g, there], rtt.at[me.t, g], ts.at[0], tr.at[0], me.g, there) for g in range(G)]
-
-    for step in range(1, T):
-        for copy in t_copy(step):
-            copy.start()
+    gn.middle()
+    weight_grad(2 * cs, sz.tl, dwz, by_rank)
+
+    tails = lambda t: dwz.at[pl.ds(t * G, G), :, pl.ds(0, sz.tl)]
+    for fi in range(sz.fi):
+        remote(sz, tails(2 * fi + me.other), rtp.at[fi], ts.at[0], tr.at[0], me.g, me.fi * 2 + me.other).start()
+    line_x.step(1)
 
     for j in range(tiles):
         spot = iota((LANES, LANES), 1) == 2 * j + (iota((LANES, LANES), 0) >= sz.hd).astype(jnp.int32)
@@ -1052,8 +1069,12 @@
     saves = [pltpu.make_async_copy(Folded().at(c), HS.at[:, pl.ds(c * cs, cs)], wsem.at[7 + c]) for c in range(pieces)]
     for copy in saves:
         copy.start()
-    gn.middle()
-    line_x.step(1)
+    landed(rtp, tr.at[0])
+    for fi in (me.fa, me.fb, me.fd, me.fi):
+        mine = tails(2 * fi + me.c)
+        mine[...] = (mine[...].astype(F32) + rtp[fi].astype(F32)).astype(BF16)
+    for fi in (me.fd, me.fa, me.fb):
+        remote(sz, tails(2 * fi + me.c), rtt.at[me.fi], ts.at[1], tr.at[1], me.g, 2 * fi + me.c).start()
 
     mine = lax.div(me.i, G) == me.t
 
@@ -1085,15 +1106,6 @@
 
     for step in range(2, G - 1):
         line_x.step(step)
-    landed(rtt.at[pl.ds(0, T - 1)], tr.at[0])
-    for g in range(G):
-        total = dwt[g, me.t].astype(F32)
-        for step in range(1, T):
-            total = total + rtt[lax.rem(me.t + step, T), g].astype(F32)
-        st[g] = total.astype(BF16)
-    t_line = lambda step: remote(sz, st.at[lax.rem(me.g + step, G)], rtz.at[me.g], us.at[0], ur.at[0], lax.rem(me.g + step, G), me.t)
-    for step in range(1, G):
-        t_line(step).start()
     gn.finish()
     saves.append(pltpu.make_async_copy(gs, GS, wsem.at[2]))
     saves[-1].start()
@@ -1109,8 +1121,14 @@
     saves[-1].start()
 
     line_x.total(acc)
-    szx[...] = acc[...].astype(BF16)
-    hand(szx, rax, 1)
+    landed(raz.at[pl.ds(0, T - 1)], as_.at[0])
+    szz[...] = acc[...].astype(BF16)
+    hand(szz, rax, 1)
+    landed(rtt.at[pl.ds(0, sz.fi - 1)], tr.at[1])
+    st[...] = (tails(me.t)[...].astype(F32) + rtt[me.fa].astype(F32) + rtt[me.fb].astype(F32) + rtt[me.fd].astype(F32)).astype(BF16)
+    t_line = lambda step: remote(sz, st.at[lax.rem(me.g + step, G)], rtz.at[me.g], us.at[0], ur.at[0], lax.rem(me.g + step, G), me.t)
+    for step in range(1, G):
+        t_line(step).start()
     landed(raz.at[pl.ds(0, T - 1)], ar_.at[0])
     saves.append(pltpu.make_async_copy(raz, RAZ, wsem.at[4]))
     saves[-1].start()
@@ -1125,17 +1143,17 @@
     saves.append(pltpu.make_async_copy(rax, RAX, wsem.at[6]))
     saves[-1].start()
 
-    hid.sent()
     gn.sent0()
-    gn.sent()
+    gn.sent1()
+    gn.sent2()
     line_x.sent()
     for k in range(G):
         @pl.when(t_differs(sz, me, k))
         def _(k=k):
             o_copy(k).wait_send()
-    for k in range(2):
-        landed(raz.at[pl.ds(0, T - 1)], as_.at[k])
-    landed(rtt.at[pl.ds(0, T - 1)], ts.at[0])
+    landed(raz.at[pl.ds(0, T - 1)], as_.at[1])
+    landed(rtp, ts.at[0])
+    landed(rtt.at[pl.ds(0, sz.fi - 1)], ts.at[1])
     landed(rtz.at[pl.ds(0, G - 1)], us.at[0])
     landed(rs1.at[pl.ds(0, G - 1)], ss.at[0])
     landed(rs2.at[pl.ds(0, T - 1)], ss.at[1])
@@ -1168,14 +1186,14 @@
             jax.ShapeDtypeStruct((total_rows, LANES), F32),
         ],
         scratch_shapes=[
-            b(d, t * rows), b(t, rows, d), f(2, max(3 * rows, -(-d // (2 * cs)) * rows), cs), f(2, rows, cs), f(2, rows, tl), b(n, dn, cs), b(n, dn, cs), b(n, dn, tl), b(g, on, d),
-            b(t, rows, cs), b(t, rows, cs), b(t, rows, tl), f(t, rows, cs),
-            b(4, rows, d), b(3, rows, d), b(2, rows, d), b(rows, d), b(4, rows, d), b(2, rows, d), b(rows, d), f(rows, d),
-            b(g, t, dn, max(cs, tl)), b(g, t, dn, cs), b(g, on, d), b(g + 1, t, dn, cs), b(g + 1, t, dn, cs), f(t, dn, cs),
-            b(t, dn, cs), b(t, dn, cs), b(t, dn, cs), b(t, dn, cs), b(g, on, d), f(on, d), b(t, g, dn, tl), b(g, dn, tl), b(g, dn, tl), f(dn, tl),
+            b(d, t * rows), b(t, rows, d), f(2, max(3 * rows, -(-d // (2 * cs)) * rows), cs), f(2, rows, cs), f(2, rows, pt.shape[2]), b(n, dn, 2 * cs + tl), b(g, on, d),
+            b(t, rows, 2 * cs + tl), f(t, rows, cs),
+            b(4, rows, d), b(2, rows, d), b(rows, d), b(4, rows, d), b(2, rows, d), b(rows, d), f(rows, d),
+            b(n, dn, max(cs, tl)), b(n, dn, cs), b(g, on, d), b(g + 1, t, dn, cs), b(g + 1, t, dn, cs), f(t, dn, cs),
+            b(t, dn, cs), b(t, dn, cs), b(t, dn, cs), b(g, on, d), f(on, d), b(sz.fi, g, dn, tl), b(sz.fi, g, dn, tl), b(g, dn, tl), b(g, dn, tl), f(dn, tl),
             f(sr, LANES), f(g, sr, LANES), f(sr, LANES), f(t, sr, LANES), f(total_rows, LANES),
             dma((6,)), dma((2,)), dma((2, 2)), *plane(), *plane(), dma((g,)), dma((g + 1,)), dma((g,)), dma((g + 1,)), dma((g,)), dma((g,)),
-            dma((2,)), dma((2,)), dma((1,)), dma((1,)), dma((1,)), dma((1,)), dma((2,)), dma((2,)), dma((7 + d // cs,)),
+            dma((2,)), dma((2,)), dma((2,)), dma((2,)), dma((1,)), dma((1,)), dma((2,)), dma((2,)), dma((7 + d // cs,)),
         ],
         compiler_params=pltpu.CompilerParams(collective_id=1, has_side_effects=True, vmem_limit_bytes=67043328),
         name="back",

time: 217 us -> 197 us (0.908)
  Pallas kernels: 213 us -> 194 us
    pallas_call x1, Pallas kernels: 116 us -> 101 us  [run_back(): pl.pallas_call(functools.partial(back_kernel, sz), in_specs=[any_] * 11 +...]
    pallas_call x1, Pallas kernels: 90.9 us -> 86.8 us  [run_front(): pl.pallas_call(functools.partial(front_kernel, sz), in_specs=[any_] * 5 +...]
where the time goes in v4:
time: 197 us
  Pallas kernels  194 us (98%)
    pallas_call x1, Pallas kernels, run_back(): pl.pallas_call(functools.partial(back_kernel, sz), in_specs=[any_] * 11 +...  101 us
    pallas_call x1, Pallas kernels, run_front(): pl.pallas_call(functools.partial(front_kernel, sz), in_specs=[any_] * 5 +...  86.8 us
    pallas_call x1, Pallas kernels, run_finish(): pl.pallas_call(functools.partial(finish_kernel, sz), in_specs=[any_] * 8...  6.27 us

profile of v4, /device:TPU:0, one launch (start us, length us, event | category | flops | bytes accessed | tf_op | source)
XLA Modules:
  0.0 196.6 jit_solution(1674610023252304359)
XLA Ops:
  0.6 0.8 slice.3
  1.4 0.6 pad.4.tail
  2.0 86.8 %front.1 = (bf16[1536,2048]{1,0:T(8,128)(2,1)}, bf16[8,256,1536]{2,1,0:T(8,128)(2,1)}, f32[8,256,384]{2,1,0:T(8,128)}, f32[8,256,640]{2,1,0:T(8,128)}, f32[8,256...) custom-call(bf16[256,1536]{1,0:T(8,128)(2,1)} %X.1, ...), custom_call_target="tpu_custom_call" | custom-call | tf_op jit(solution)/shard_map/front/pallas_call | solution.py:640
  88.8 101.3 %back.1 = (f32[256,1536]{1,0:T(8,128)}, f32[256,1536]{1,0:T(8,128)}, bf16[8,48,384]{2,1,0:T(8,128)(2,1)}, bf16[8,48,384]{2,1,0:T(8,128)(2,1)}, f32[48,384]{1,0:T...) custom-call(bf16[1536,2048]{1,0:T(8,128)(2,1)} %get-tuple-element.44.NT, bf16[8,256,1536]{2,1,0:T(8,128)(2,1)} %get-tuple-element.45.GO, ...), custom_call_target="tpu_custom_call" | custom-call | tf_op jit(solution)/shard_map/back/pallas_call | solution.py:1175
  190.1 6.3 %finish.1 = (bf16[256,1536]{1,0:T(8,128)(2,1)}, f32[256,1536]{1,0:T(8,128)}, f32[1,48]{1,0:T(1,128)}, f32[48,6448]{1,0:T(8,128)}, f32[4,104]{1,0:T(4,128)}, /*in...) custom-call(f32[256,1536]{1,0:T(8,128)} %get-tuple-element.59.HS, ...), custom_call_target="tpu_custom_call" | custom-call | tf_op jit(solution)/shard_map/finish/pallas_call | solution.py:1284

commit v5 on v4

--- a/solution.py
+++ b/solution.py
@@ -241,7 +241,7 @@
                  NT, GO, PX, PT, PZ, Y, GM, WX, WZ, WT, WO, Q, PAR, HEAD, TILE,
                  xv, nv, gov, px, pt, pz, yv, gmv, wxv, wzv, wtv, wov, pack, smv, par, head, qv, qr, tilev, flip,
                  xsend, xrecv, gsend, grecv, wsend, wrecv, axsend, axrecv, azsend, azrecv, zxsend, zxrecv, zzsend, zzrecv,
-                 tsend, trecv, osend, orecv, ssend, srecv, qsend, qrecv, lsem, esem, wsem):
+                 tsend, trecv, osend, orecv, ssend, srecv, qsend, qrecv, lsem, esem, wsem, fsem):
     me = Place(sz)
     cs, rows, G, T, st, taps = sz.cs, sz.rows, sz.g, sz.t, sz.state, sz.taps
     tiles = cs // LANES
@@ -371,6 +371,8 @@
     gt.start(0)
     for step in range(1, T):
         exchange(0, step).start()
+    for p in range(1, sz.parts):
+        gx.start(p)
 
     def arrive(half):
         wv, _, recv = ((wzv, azsend, azrecv), (wxv, axsend, axrecv))[half]
@@ -384,22 +386,25 @@
         plane = jnp.clip(plane, 0, G - 1)
         nxt = jnp.clip(me.g + 1 if up else me.g - 1, 0, G - 1)
 
-        def push():
-            for fi in range(sz.fi):
+        def push(part):
+            for fi in range(part * sz.fi // 2, (part + 1) * sz.fi // 2):
                 block = wv.at[pl.ds(index_of(sz, plane, jnp.int32(2 * fi)), 2)]
-                remote(sz, block, block, send.at[int(up), plane], recv.at[plane], nxt, me.t).start()
+                remote(sz, block, block, send.at[int(up), plane], recv.at[part, plane], nxt, me.t).start()
 
         return have, more, plane, push, wv.at[pl.ds(0, T)], send, recv
 
     def advance(half, step):
-        for up in (True, False):
-            have, more, plane, push, gauge, _, recv = line(half, step, up)
-            if step > 0:
-                @pl.when(have)
-                def _(gauge=gauge, recv=recv, plane=plane):
-                    landed(gauge, recv.at[plane])
-            if step < G - 1:
-                pl.when(have & more)(push)
+        for part in range(2):
+            for up in (True, False):
+                have, more, plane, push, _, _, recv = line(half, step, up)
+                if step > 0:
+                    @pl.when(have)
+                    def _(recv=recv, plane=plane, part=part):
+                        landed(wxv.at[pl.ds(0, T // 2)], recv.at[part, plane])
+                if step < G - 1:
+                    @pl.when(have & more)
+                    def _(push=push, part=part):
+                        push(part)
 
     arrive(1)
     advance(1, 0)
@@ -421,10 +426,14 @@
         mean = jnp.mean(xb * xb, axis=1, keepdims=True)
         nrm = (xb * lax.rsqrt(mean + EPS) * par[taps + 2 : taps + 3, 0 : sz.d]).astype(BF16)
         nv[slot] = nrm
-        flip[...] = nrm.T
-        turn = pltpu.make_async_copy(flip, NT.at[:, pl.ds(pl.multiple_of(slot * rows, LANES), rows)], esem.at[0])
-        turn.start()
-        turn.wait()
+        half = lax.rem(k, 2)
+
+        @pl.when(k > 1)
+        def _():
+            landed(flip.at[half], fsem.at[half])
+
+        flip[half] = nrm.T
+        pltpu.make_async_copy(flip.at[half], NT.at[:, pl.ds(pl.multiple_of(slot * rows, LANES), rows)], fsem.at[half]).start()
 
     def wait_pair(gather, k):
         slot = slot_of(me, k)
@@ -432,8 +441,6 @@
             gather.arrived(slot, p)
 
     gt.relay(0)
-    for p in range(1, sz.parts):
-        gx.start(p)
     normalize(jnp.int32(0))
     wait_pair(gx, jnp.int32(1))
     normalize(jnp.int32(1))
@@ -442,8 +449,14 @@
         advance(1, step)
     arrive(0)
     advance(0, 0)
+    advance(1, G - 1)
+    for p in range(1, sz.parts):
+        gx.relay(p)
+    for p in range(sz.parts):
+        gg.start(p)
     gt.relay_far(0)
-    advance(1, G - 1)
+    advance(0, 1)
+    out_steps(0)
     for fi in (me.fi, me.fa, me.fb, me.fd):
         gt.arrived(fi * 2 + me.other, 0)
 
@@ -520,15 +533,15 @@
 
     @pl.loop(0, T)
     def _(k):
-        between(k == 2, lambda: advance(0, 1), lambda: out_steps(0), lambda: [gx.relay(p) for p in range(1, sz.parts)],
-                lambda: [gg.start(p) for p in range(sz.parts)])
         between(k == 3, lambda: gx.relay_far(0))
         between(k == 4, lambda: [advance(0, step) for step in range(2, G - 1)])
-        between(k == 6, lambda: [gx.relay_far(p) for p in range(1, sz.parts)], lambda: out_steps(1))
-        between(k == 7, lambda: [gg.relay(p) for p in range(sz.parts)])
+        between(k == 5, lambda: [gx.relay_far(p) for p in range(1, sz.parts)])
+        between(k == 6, lambda: out_steps(1))
+        between(k == 7, lambda: advance(0, G - 1))
         scan(k)
 
-    advance(0, G - 1)
+    for p in range(sz.parts):
+        gg.relay(p)
     out_steps(*range(2, G - 1))
     save(4)
 
@@ -620,6 +633,8 @@
                     landed(gauge, send.at[int(up), plane])
     for k, (src, dst) in enumerate(whole):
         pltpu.make_async_copy(src, dst, wsem.at[k]).wait()
+    for half in range(2):
+        landed(flip.at[half], fsem.at[half])
     for a, (src, dst) in enumerate([(px, PX), (pt, PT), (yv, Y), (pz, PZ), (gmv, GM), (gov, GO)]):
         pltpu.make_async_copy(src, dst, esem.at[a + 1]).wait()
 
@@ -645,10 +660,10 @@
         scratch_shapes=scr("nrm", "nrm", "go", "px", "pt", "pz", "y", "gm", "wx", "wz", "wt", "wo")
         + [pltpu.VMEM((8, LANES), F32), pltpu.VMEM((n, 8, LANES), F32)]
         + scr("par", "head", "q")
-        + [pltpu.VMEM((t, 2 * t, rows), F32), pltpu.VMEM((t, 8, LANES), F32), pltpu.VMEM((d, rows), BF16)]
+        + [pltpu.VMEM((t, 2 * t, rows), F32), pltpu.VMEM((t, 8, LANES), F32), pltpu.VMEM((2, d, rows), BF16)]
         + [dma((1,)), dma((t, parts)), dma((1,)), dma((t, parts)), dma((1,)), dma((t, 1)), dma((1,)), dma((1,)), dma((1,)), dma((1,)),
-           dma((2, g)), dma((g,)), dma((2, g)), dma((g,)), dma((1,)), dma((1,)), dma((3, g)), dma((g,)), dma((2,)), dma((2,)),
-           dma((1,)), dma((1,)), dma((7,)), dma((7,)), dma((7,))],
+           dma((2, g)), dma((2, g)), dma((2, g)), dma((2, g)), dma((1,)), dma((1,)), dma((3, g)), dma((g,)), dma((2,)), dma((2,)),
+           dma((1,)), dma((1,)), dma((7,)), dma((7,)), dma((7,)), dma((2,))],
         compiler_params=pltpu.CompilerParams(collective_id=0, has_side_effects=True, vmem_limit_bytes=67043328),
         name="front",
     )(x, go, win, tail, wout, norm, cw, cb, gate, lens, decay, bias, skip)
@@ -658,8 +673,12 @@
     def __init__(self, sz, me, own, recv, send_sem, recv_sem):
         self.sz, self.me, self.own, self.recv, self.send_sem, self.recv_sem = sz, me, own, recv, send_sem, recv_sem
 
-    def piece(self, p):
-        return self.own.at[pl.ds(p * self.sz.t, self.sz.t)]
+    def piece(self, p, part=None):
+        t = self.sz.t
+        return self.own.at[pl.ds(p * t, t)] if part is None else self.own.at[pl.ds(p * t + part * (t // 2), t // 2)]
+
+    def got(self, p, part):
+        return self.recv.at[p, pl.ds(part * (self.sz.t // 2), self.sz.t // 2)]
 
     def leg(self, step, up):
         g, last = self.me.g, self.sz.g - 1
@@ -670,22 +689,23 @@
         inner = (g > 0) if up else (g < last)
         nxt = jnp.clip(g + 1 if up else g - 1, 0, last)
         there = p if up else jnp.where(p == nxt, last + 1, p)
-        copy = lambda: remote(self.sz, self.piece(p), self.recv.at[there], self.send_sem.at[p], self.recv_sem.at[there], nxt, self.me.t)
+        copy = lambda part: remote(self.sz, self.piece(p, part), self.got(there, part), self.send_sem.at[p], self.recv_sem.at[part, there], nxt, self.me.t)
         return p, moves, inner, copy
 
     def step(self, step):
-        for up in (True, False):
-            p, moves, inner, copy = self.leg(step, up)
-
-            @pl.when(moves & inner)
-            def _(p=p):
-                landed(self.recv.at[p], self.recv_sem.at[p])
-                piece = self.piece(p)
-                piece[...] = (piece[...].astype(F32) + self.recv[p].astype(F32)).astype(BF16)
-
-            @pl.when(moves)
-            def _(copy=copy):
-                copy().start()
+        for part in range(2):
+            for up in (True, False):
+                p, moves, inner, copy = self.leg(step, up)
+
+                @pl.when(moves & inner)
+                def _(p=p, part=part):
+                    landed(self.got(p, part), self.recv_sem.at[part, p])
+                    piece = self.piece(p, part)
+                    piece[...] = (piece[...].astype(F32) + self.got(p, part)[...].astype(F32)).astype(BF16)
+
+                @pl.when(moves)
+                def _(copy=copy, part=part):
+                    copy(part).start()
 
     def total(self, acc):
         g = self.me.g
@@ -693,17 +713,18 @@
         for k, there in ((g, g > 0), (self.sz.g, g < self.sz.g - 1)):
             @pl.when(there)
             def _(k=k):
-                landed(self.recv.at[k], self.recv_sem.at[k])
+                for part in range(2):
+                    landed(self.got(k, part), self.recv_sem.at[part, k])
                 acc[...] += self.recv[k].astype(F32)
 
     def sent(self):
         for step in range(self.sz.g - 1):
             for up in (True, False):
-                _, moves, _, copy = self.leg(step, up)
+                p, moves, _, _ = self.leg(step, up)
 
                 @pl.when(moves)
-                def _(copy=copy):
-                    copy().wait_send()
+                def _(p=p):
+                    landed(self.piece(p), self.send_sem.at[p])
 
 
 class PlaneReduce:
@@ -781,7 +802,7 @@
                 HS, GS, RAZ, RAX, GTL, GOUT, GSM,
                 nt_, gov, ra, rx, rt_, wall, wo, dp, dyv, r0h, r1h, r2h, r0g, r1g, r2g, gs,
                 dwz, dwx, dwo, rzz, rzx, acc, szz, raz, rax, ro, gout, rtp, rtt, st, rtz, gtl, small, rs1, s1, rs2, gsm,
-                lsem, asem, bsem, h0s, h0r, h1s, h1r, h2s, h2r, g0s, g0r, g1s, g1r, g2s, g2r, zzs, zzr, zxs, zxr, os_, or_, as_, ar_, ts, tr, us, ur, ss, sr, wsem):
+                lsem, asem, gsem, bsem, h0s, h0r, h1s, h1r, h2s, h2r, g0s, g0r, g1s, g1r, g2s, g2r, zzs, zzr, zxs, zxr, os_, or_, as_, ar_, ts, tr, us, ur, ss, sr, wsem):
     me = Place(sz)
     rows, cs, st_dim, taps, T, G, d = sz.rows, sz.cs, sz.state, sz.taps, sz.t, sz.g, sz.d
     tiles = cs // LANES
@@ -798,7 +819,7 @@
 
     class Folded:
         def at(self, c):
-            return ra.at[c // (pieces // 2), pl.ds(c % (pieces // 2) * rows, rows)]
+            return ra.at[c // 2, pl.ds(c % 2 * rows, rows)]
 
         def put(self, value, more):
             for c in range(pieces):
@@ -812,14 +833,15 @@
     gn = PlaneReduce(sz, me, stage, r0g, sums, r1g, r2g, put_gs, (g0s, g0r, g1s, g1r, g2s, g2r))
 
     def fetch_a(k):
-        slot, par_ = hid.slot(k), lax.rem(k, 2)
-        return [pltpu.make_async_copy(src.at[slot], ra.at[par_, pl.ds(a * rows, rows)], asem.at[par_]) for a, src in enumerate((PZ, Y, GM))]
+        slot, turn = hid.slot(k), lax.rem(k, 3)
+        ring = [pltpu.make_async_copy(src.at[slot], ra.at[turn, pl.ds(a * rows, rows)], asem.at[turn]) for a, src in enumerate((PZ, Y))]
+        return ring + [pltpu.make_async_copy(GM.at[slot], dyv.at[slot], gsem.at[slot])]
 
     def fetch_b(k):
         slot, par_ = gn.slot(k), lax.rem(k, 2)
         return [pltpu.make_async_copy(PX.at[slot], rx.at[par_], bsem.at[0, par_]), pltpu.make_async_copy(PT.at[slot], rt_.at[par_], bsem.at[1, par_])]
 
-    for k in range(2):
+    for k in range(3):
         for copy in fetch_a(jnp.int32(k)):
             copy.start()
     loads = [pltpu.make_async_copy(src, dst, lsem.at[k]) for k, (src, dst) in enumerate((
@@ -843,13 +865,14 @@
 
     @pl.loop(0, T)
     def _(k):
-        slot, par_ = hid.slot(k), lax.rem(k, 2)
+        slot, turn = hid.slot(k), lax.rem(k, 3)
 
         @pl.when(k == T // 2)
         def _():
             loads[0].start()
 
-        landed(ra.at[par_, pl.ds(0, 3 * rows)], asem.at[par_])
+        landed(ra.at[turn], asem.at[turn])
+        landed(dyv.at[slot], gsem.at[slot])
         pos = iota((rows, LANES), 0).astype(F32)
         valid = (segments(pos, ends_of(tile_ref[slot, taps + 3 : taps + 4, :], sz.seqs)) < sz.seqs).astype(F32)
         q1 = jnp.broadcast_to(q_ref[pl.ds(slot, 1), :], (LANES, rows)).T
@@ -859,8 +882,8 @@
         for j in range(tiles):
             at = j * LANES
             tile = slice(at, at + LANES)
-            zt, y, gm = (ra[par_, a * rows : (a + 1) * rows, tile] for a in range(3))
-            gm = gm * valid
+            zt, y = (ra[turn, a * rows : (a + 1) * rows, tile] for a in range(2))
+            gm = dyv[slot, :, tile] * valid
             gate = par[taps + 1 : taps + 2, tile]
             up, slope = silu_pair(zt)
             gated = y * up
@@ -871,9 +894,9 @@
             dp[slot, :, tile] = (dgated * y * slope).astype(BF16)
             dyv[slot, :, tile] = dgated * up
 
-        @pl.when(k + 2 < T)
+        @pl.when(k + 3 < T)
         def _():
-            for copy in fetch_a(k + 2):
+            for copy in fetch_a(k + 3):
                 copy.start()
 
     for copy in loads[1:3]:
@@ -1037,27 +1060,6 @@
         between(k == 7, hid.finish)
         scan_back(k)
 
-    weight_grad(cs, cs, dwx, by_plane)
-    line_x.step(0)
-    line_z.total(acc)
-    szz[...] = acc[...].astype(BF16)
-
-    def hand(sums, into, k):
-        for step in range(1, T):
-            there = lax.rem(me.t + step, T)
-            remote(sz, sums.at[there], into.at[me.t], as_.at[k], ar_.at[k], me.g, there).start()
-        into[me.t] = sums[me.t]
-
-    hand(szz, raz, 0)
-    line_z.sent()
-    gn.middle()
-    weight_grad(2 * cs, sz.tl, dwz, by_rank)
-
-    tails = lambda t: dwz.at[pl.ds(t * G, G), :, pl.ds(0, sz.tl)]
-    for fi in range(sz.fi):
-        remote(sz, tails(2 * fi + me.other), rtp.at[fi], ts.at[0], tr.at[0], me.g, me.fi * 2 + me.other).start()
-    line_x.step(1)
-
     for j in range(tiles):
         spot = iota((LANES, LANES), 1) == 2 * j + (iota((LANES, LANES), 0) >= sz.hd).astype(jnp.int32)
         part = jnp.dot(small[sz.at_head + 3 + j : sz.at_head + 4 + j, :], spot.astype(F32), precision=EXACT, preferred_element_type=F32)
@@ -1065,6 +1067,36 @@
     s_line = lambda step: remote(sz, small, rs1.at[me.g], ss.at[0], sr.at[0], lax.rem(me.g + step, G), me.t)
     for step in range(1, G):
         s_line(step).start()
+
+    weight_grad(cs, cs, dwx, by_plane)
+    line_x.step(0)
+    line_z.total(acc)
+    szz[...] = acc[...].astype(BF16)
+
+    def hand(sums, into, k):
+        for step in range(1, T):
+            there = lax.rem(me.t + step, T)
+            remote(sz, sums.at[there], into.at[me.t], as_.at[k], ar_.at[k], me.g, there).start()
+        into[me.t] = sums[me.t]
+
+    hand(szz, raz, 0)
+    line_z.sent()
+    weight_grad(2 * cs, sz.tl, dwz, by_rank)
+
+    tails = lambda t: dwz.at[pl.ds(t * G, G), :, pl.ds(0, sz.tl)]
+    for fi in range(sz.fi):
+        remote(sz, tails(2 * fi + me.other), rtp.at[fi], ts.at[0], tr.at[0], me.g, me.fi * 2 + me.other).start()
+    landed(rs1.at[pl.ds(0, G - 1)], sr.at[0])
+    total = small[...]
+    for step in range(1, G):
+        total = total + rs1[lax.rem(me.g + step, G)]
+    s1[...] = total
+    rs2[me.t] = total
+    s_plane = lambda step: remote(sz, s1, rs2.at[me.t], ss.at[1], sr.at[1], me.g, lax.rem(me.t + step, T))
+    for step in range(1, T):
+        s_plane(step).start()
+    gn.middle()
+    line_x.step(1)
 
     saves = [pltpu.make_async_copy(Folded().at(c), HS.at[:, pl.ds(c * cs, cs)], wsem.at[7 + c]) for c in range(pieces)]
     for copy in saves:
@@ -1094,21 +1126,16 @@
 
     saves.append(pltpu.make_async_copy(gout, GOUT, wsem.at[1]))
     saves[-1].start()
-    landed(rs1.at[pl.ds(0, G - 1)], sr.at[0])
-    total = small[...]
-    for step in range(1, G):
-        total = total + rs1[lax.rem(me.g + step, G)]
-    s1[...] = total
-    rs2[me.t] = total
-    s_plane = lambda step: remote(sz, s1, rs2.at[me.t], ss.at[1], sr.at[1], me.g, lax.rem(me.t + step, T))
-    for step in range(1, T):
-        s_plane(step).start()
-
     for step in range(2, G - 1):
         line_x.step(step)
     gn.finish()
     saves.append(pltpu.make_async_copy(gs, GS, wsem.at[2]))
     saves[-1].start()
+    landed(rtt.at[pl.ds(0, sz.fi - 1)], tr.at[1])
+    st[...] = (tails(me.t)[...].astype(F32) + rtt[me.fa].astype(F32) + rtt[me.fb].astype(F32) + rtt[me.fd].astype(F32)).astype(BF16)
+    t_line = lambda step: remote(sz, st.at[lax.rem(me.g + step, G)], rtz.at[me.g], us.at[0], ur.at[0], lax.rem(me.g + step, G), me.t)
+    for step in range(1, G):
+        t_line(step).start()
     landed(rs2.at[pl.ds(0, T - 1)], sr.at[1])
     total = rs2[0, 0 : sz.common]
     for t in range(1, T):
@@ -1124,11 +1151,6 @@
     landed(raz.at[pl.ds(0, T - 1)], as_.at[0])
     szz[...] = acc[...].astype(BF16)
     hand(szz, rax, 1)
-    landed(rtt.at[pl.ds(0, sz.fi - 1)], tr.at[1])
-    st[...] = (tails(me.t)[...].astype(F32) + rtt[me.fa].astype(F32) + rtt[me.fb].astype(F32) + rtt[me.fd].astype(F32)).astype(BF16)
-    t_line = lambda step: remote(sz, st.at[lax.rem(me.g + step, G)], rtz.at[me.g], us.at[0], ur.at[0], lax.rem(me.g + step, G), me.t)
-    for step in range(1, G):
-        t_line(step).start()
     landed(raz.at[pl.ds(0, T - 1)], ar_.at[0])
     saves.append(pltpu.make_async_copy(raz, RAZ, wsem.at[4]))
     saves[-1].start()
@@ -1186,13 +1208,13 @@
             jax.ShapeDtypeStruct((total_rows, LANES), F32),
         ],
         scratch_shapes=[
-            b(d, t * rows), b(t, rows, d), f(2, max(3 * rows, -(-d // (2 * cs)) * rows), cs), f(2, rows, cs), f(2, rows, pt.shape[2]), b(n, dn, 2 * cs + tl), b(g, on, d),
+            b(d, t * rows), b(t, rows, d), f(3, 2 * rows, cs), f(2, rows, cs), f(2, rows, pt.shape[2]), b(n, dn, 2 * cs + tl), b(g, on, d),
             b(t, rows, 2 * cs + tl), f(t, rows, cs),
             b(4, rows, d), b(2, rows, d), b(rows, d), b(4, rows, d), b(2, rows, d), b(rows, d), f(rows, d),
             b(n, dn, max(cs, tl)), b(n, dn, cs), b(g, on, d), b(g + 1, t, dn, cs), b(g + 1, t, dn, cs), f(t, dn, cs),
             b(t, dn, cs), b(t, dn, cs), b(t, dn, cs), b(g, on, d), f(on, d), b(sz.fi, g, dn, tl), b(sz.fi, g, dn, tl), b(g, dn, tl), b(g, dn, tl), f(dn, tl),
             f(sr, LANES), f(g, sr, LANES), f(sr, LANES), f(t, sr, LANES), f(total_rows, LANES),
-            dma((6,)), dma((2,)), dma((2, 2)), *plane(), *plane(), dma((g,)), dma((g + 1,)), dma((g,)), dma((g + 1,)), dma((g,)), dma((g,)),
+            dma((6,)), dma((3,)), dma((t,)), dma((2, 2)), *plane(), *plane(), dma((g,)), dma((2, g + 1)), dma((g,)), dma((2, g + 1)), dma((g,)), dma((g,)),
             dma((2,)), dma((2,)), dma((2,)), dma((2,)), dma((1,)), dma((1,)), dma((2,)), dma((2,)), dma((7 + d // cs,)),
         ],
         compiler_params=pltpu.CompilerParams(collective_id=1, has_side_effects=True, vmem_limit_bytes=67043328),

time: 197 us -> 190 us (0.964)
  Pallas kernels: 194 us -> 187 us
    pallas_call x1, Pallas kernels: 86.8 us -> 82.8 us  [run_front(): pl.pallas_call(functools.partial(front_kernel, sz), in_specs=[any_] * 5 +...]
    pallas_call x1, Pallas kernels: 101 us -> 98.2 us  [run_back(): pl.pallas_call(functools.partial(back_kernel, sz), in_specs=[any_] * 11 +...]
where the time goes in v5:
time: 190 us; the launch traced here: 189 us
  Pallas kernels  187 us (98%)
    pallas_call x1, Pallas kernels, run_back(): pl.pallas_call(functools.partial(back_kernel, sz), in_specs=[any_] * 11 +...  98.2 us
    pallas_call x1, Pallas kernels, run_front(): pl.pallas_call(functools.partial(front_kernel, sz), in_specs=[any_] * 5 +...  82.8 us
    pallas_call x1, Pallas kernels, run_finish(): pl.pallas_call(functools.partial(finish_kernel, sz), in_specs=[any_] * 8...  6.27 us

profile of v5, /device:TPU:0, one launch (start us, length us, event | category | flops | bytes accessed | tf_op | source)
XLA Modules:
  0.0 189.5 jit_solution(8705495488430081947)
XLA Ops:
  0.6 0.8 slice.3
  1.4 0.6 pad.4.tail
  2.0 82.8 %front.1 = (bf16[1536,2048]{1,0:T(8,128)(2,1)}, bf16[8,256,1536]{2,1,0:T(8,128)(2,1)}, f32[8,256,384]{2,1,0:T(8,128)}, f32[8,256,640]{2,1,0:T(8,128)}, f32[8,256...) custom-call(bf16[256,1536]{1,0:T(8,128)(2,1)} %X.1, ...), custom_call_target="tpu_custom_call" | custom-call | tf_op jit(solution)/shard_map/front/pallas_call | solution.py:655
  84.8 98.2 %back.1 = (f32[256,1536]{1,0:T(8,128)}, f32[256,1536]{1,0:T(8,128)}, bf16[8,48,384]{2,1,0:T(8,128)(2,1)}, bf16[8,48,384]{2,1,0:T(8,128)(2,1)}, f32[48,384]{1,0:T...) custom-call(bf16[1536,2048]{1,0:T(8,128)(2,1)} %get-tuple-element.44.NT, bf16[8,256,1536]{2,1,0:T(8,128)(2,1)} %get-tuple-element.45.GO, ...), custom_call_target="tpu_custom_call" | custom-call | tf_op jit(solution)/shard_map/back/pallas_call | solution.py:1197
  183.0 6.3 %finish.1 = (bf16[256,1536]{1,0:T(8,128)(2,1)}, f32[256,1536]{1,0:T(8,128)}, f32[1,48]{1,0:T(1,128)}, f32[48,6448]{1,0:T(8,128)}, f32[4,104]{1,0:T(4,128)}, /*in...) custom-call(f32[256,1536]{1,0:T(8,128)} %get-tuple-element.59.HS, ...), custom_call_target="tpu_custom_call" | custom-call | tf_op jit(solution)/shard_map/finish/pallas_call | solution.py:1306
